TPU v7x, 16 devices: a whole 2x2x2 slice. The times are simulated.
16 devices in a mesh: dp: 2 (over z), ep: 8 (over y, x, core).
Axes of the slice: x: 2, y: 2, z: 2, core: 2. Of those that a mesh axis runs over, the one named last changes fastest.
Arguments:
- x: bfloat16 [32768, 768], P(('dp', 'ep'))
- gy: bfloat16 [32768, 768], P(('dp', 'ep'))
- idx: int32 [32768], P(('dp', 'ep'))
- w_gate: bfloat16 [768, 32], replicated
- w_up: bfloat16 [32, 768, 3072], P('ep')
- w_down: bfloat16 [32, 3072, 768], P('ep')
Outputs:
- output 1: bfloat16 [32768, 768], P(('dp', 'ep'))
- output 2: bfloat16 [32768, 768], P(('dp', 'ep'))
- output 3: float32 [32, 768, 3072], P('ep')
- output 4: float32 [32, 3072, 768], P('ep')
- output 5: float32 [768, 32], replicated
All inputs are finite; a program needn't handle non-finite values.
Results may differ from a plain program's by a relative error of at most 0.00656847.
Values are sent between devices in bfloat16 or wider.
A program may use at most 1 GiB of HBM per device.

v0:
```python
import jax
import jax.numpy as jnp
from jax import lax
from jax.sharding import PartitionSpec as P

PAD_FACTOR = 4


def solution(mesh):
    ep_size = mesh.shape['ep']
    tok_spec = P(('dp', 'ep'), None)
    idx_spec = P(('dp', 'ep'))
    rep_spec = P(None, None)
    exp_spec = P('ep', None, None)

    def local_step(x_loc, gy_loc, idx_loc, w_gate, w_up, w_down):
        tok_count, d_model = x_loc.shape
        n_experts = w_gate.shape[1]
        local_experts = w_up.shape[0]
        cap_rows = PAD_FACTOR * tok_count // n_experts
        onehot = idx_loc[:, None] == jnp.arange(n_experts, dtype=jnp.int32)[None, :]
        expert_count = jnp.sum(onehot, axis=0, dtype=jnp.int32)
        sort_order = jnp.argsort(idx_loc, stable=True)
        sorted_pos = jnp.argsort(sort_order)
        expert_start = jnp.cumsum(expert_count) - expert_count
        slot_k = jnp.arange(cap_rows, dtype=jnp.int32)
        slot_valid = slot_k[None, :] < expert_count[:, None]
        src_tok = sort_order[jnp.minimum(expert_start[:, None] + slot_k[None, :], tok_count - 1)]
        slot_tok = idx_loc * cap_rows + sorted_pos - expert_start[idx_loc]

        def dispatch(tok_rows):
            picked = jnp.where(slot_valid[:, :, None], tok_rows[src_tok], jnp.zeros((), tok_rows.dtype))
            picked = picked.reshape(ep_size, local_experts, cap_rows, d_model)
            return lax.all_to_all(picked, 'ep', 0, 0, tiled=True)

        def combine(expert_rows):
            returned = lax.all_to_all(expert_rows, 'ep', 1, 0, tiled=True)
            return returned.reshape(n_experts * cap_rows, d_model)[slot_tok]

        router_logit = jnp.dot(x_loc, w_gate, preferred_element_type=jnp.float32)
        router_prob = jax.nn.softmax(router_logit, axis=-1)
        gate_val = n_experts * jnp.sum(jnp.where(onehot, router_prob, 0.0), axis=1)
        recv_rows = dispatch(x_loc)
        pre_act = jnp.einsum('sekd,edf->eskf', recv_rows, w_up, preferred_element_type=jnp.float32)
        hid_full, gelu_back = jax.vjp(jax.nn.gelu, pre_act)
        hidden = hid_full.astype(jnp.bfloat16)
        expert_out = jnp.einsum('eskf,efd->eskd', hidden, w_down, preferred_element_type=jnp.float32).astype(jnp.bfloat16)
        y_tok = combine(expert_out)
        gy_full = gy_loc.astype(jnp.float32)
        moe_out = (gate_val[:, None] * y_tok.astype(jnp.float32)).astype(jnp.bfloat16)

        dy_tok = (gate_val[:, None] * gy_full).astype(jnp.bfloat16)
        recv_grad = dispatch(dy_tok)
        d_hidden = jnp.einsum('sekd,efd->eskf', recv_grad, w_down, preferred_element_type=jnp.float32)
        d_pre = gelu_back(d_hidden)[0].astype(jnp.bfloat16)
        grad_down = jnp.einsum('eskf,sekd->efd', hidden, recv_grad, preferred_element_type=jnp.float32)
        grad_up = jnp.einsum('sekd,eskf->edf', recv_rows, d_pre, preferred_element_type=jnp.float32)
        d_rows = jnp.einsum('eskf,edf->eskd', d_pre, w_up, preferred_element_type=jnp.float32).astype(jnp.bfloat16)
        dx_expert = combine(d_rows)
        d_gate = jnp.sum(gy_full * y_tok.astype(jnp.float32), axis=1)
        d_logit = ((d_gate * gate_val)[:, None] * (onehot.astype(jnp.float32) - router_prob)).astype(jnp.bfloat16)
        dx_router = jnp.einsum('te,de->td', d_logit, w_gate, preferred_element_type=jnp.float32)
        grad_x = (dx_expert.astype(jnp.float32) + dx_router).astype(jnp.bfloat16)
        grad_gate = jnp.einsum('td,te->de', x_loc, d_logit, preferred_element_type=jnp.float32)
        grad_up = lax.psum(grad_up, 'dp')
        grad_down = lax.psum(grad_down, 'dp')
        grad_gate = lax.psum(grad_gate, ('dp', 'ep'))
        return moe_out, grad_x, grad_up, grad_down, grad_gate

    sharded_fn = jax.shard_map(local_step, mesh=mesh, in_specs=(tok_spec, tok_spec, idx_spec, rep_spec, exp_spec, exp_spec), out_specs=(tok_spec, tok_spec, exp_spec, exp_spec, rep_spec), check_vma=False)
    return sharded_fn
```

profile of v0, /device:TPU:0, one launch (start us, length us, event | category | flops | bytes accessed | tf_op | source)
XLA Modules:
  0.0 2645.7 jit_solution(17377207336787458307)
XLA Ops:
  8.5 5.7 sort.34
  14.4 45.5 %gather_fusion = s32[8192]{0:T(1024)S(1)} fusion(s32[2048]{0:T(1024)S(1)} %get-tuple-element.7, s32[8192]{0:T(1024)S(1)} %broadcast_clamp_fusion), kind=kCustom, calls=%fused_computation | custom fusion | bytes 98304 | tf_op jit(solution)/shard_map/gather | solution.py:28
  60.1 34.4 %gather_fusion.1 = bf16[8192,768]{1,0:T(8,128)(2,1)} fusion(bf16[2048,768]{1,0:T(8,128)(2,1)S(1)} %copy-done, s32[8192]{0:T(1024)S(1)} %broadcast_clamp_fusion.1), kind=kCustom, calls=%fused_computation.1 | custom fusion | bytes 25198592 | tf_op jit(solution)/shard_map/gather | solution.py:32
  94.6 6.6 broadcast_select_fusion.1
  101.3 144.4 %all_to_all.40 = bf16[8,4,256,768]{3,2,1,0:T(8,128)(2,1)} all-to-all(bf16[8,4,256,768]{3,2,1,0:T(8,128)(2,1)S(1)} %broadcast_select_fusion.1), channel_id=1, replica_groups=mesh['dp'=2,'ep'=8] {'ep'}, dimensions={0} | all-to-all | bytes 25165824 | tf_op jit(solution)/shard_map/all_to_all | solution.py:34
  245.6 53.7 %fusion.11 = f32[4,8,256,3072]{3,2,1,0:T(8,128)} fusion(bf16[4,768,3072]{2,1,0:T(8,128)(2,1)} %param.10, bf16[8,4,256,768]{3,2,1,0:T(8,128)(2,1)} %all_to_all.40), kind=kOutput, calls=%fused_computation.19 | convolution fusion | flops 38654705664 | bytes 132120576 | tf_op jit(solution)/shard_map/sekd,edf->eskf/dot_general | solution.py:44
  299.3 57.5 %fusion.22 = bf16[4,8,256,768]{3,2,1,0:T(8,128)(2,1)} fusion(bf16[4,3072,768]{2,1,0:T(8,128)(2,1)} %param.11, f32[4,8,256,3072]{3,2,1,0:T(8,128)} %fusion.11), kind=kOutput, calls=%fused_computation.34 | convolution fusion | flops 38887489536 | bytes 132120576 | tf_op jit(solution)/shard_map/eskf,efd->eskd/dot_general | solution.py:47
  356.8 10.7 copy.25
  380.9 19.5 fusion.35
  400.4 111.8 %all-to-all-done.1 = bf16[4,8,256,768]{3,2,0,1:T(8,128)(2,1)} async-done(((bf16[4,8,256,768]{3,2,0,1:T(8,128)(2,1)}), bf16[4,8,256,768]{3,2,0,1:T(8,128)(2,1)}, u32[]{:S(2)}, u32[]{:S(2)}) %all-to-all-start.1) | async-done | bytes 12582944 | tf_op jit(solution)/shard_map/all_to_all | solution.py:37
  512.2 16.3 gather_fusion.2
  533.9 39.3 %gather_fusion.3 = bf16[8192,768]{1,0:T(8,128)(2,1)} fusion(bf16[2048,768]{1,0:T(8,128)(2,1)} %get-tuple-element.12, s32[8192]{0:T(1024)S(1)} %copy-done.11), kind=kCustom, calls=%fused_computation.3 | custom fusion | bytes 25198592 | tf_op jit(solution)/shard_map/gather | solution.py:32
  573.2 10.8 broadcast_select_fusion
  591.1 138.1 %all-to-all-done.2 = bf16[8,4,256,768]{3,2,1,0:T(8,128)(2,1)} async-done(((bf16[8,4,256,768]{3,2,1,0:T(8,128)(2,1)}), bf16[8,4,256,768]{3,2,1,0:T(8,128)(2,1)}, u32[]{:S(2)}, u32[]{:S(2)}) %all-to-all-start.2) | async-done | bytes 12582944 | tf_op jit(solution)/shard_map/all_to_all | solution.py:34
  729.3 64.4 %convolution_bitcast_fusion = f32[4,3072,768]{2,1,0:T(8,128)} fusion(bf16[8,4,256,768]{3,2,1,0:T(8,128)(2,1)} %all-to-all-done.2, f32[4,8,256,3072]{3,2,1,0:T(8,128)} %fusion.11), kind=kOutput, calls=%fused_computation.25 | convolution fusion | flops 38881198080 | bytes 150994944 | tf_op jit(solution)/shard_map/eskf,sekd->efd/dot_general | solution.py:56
  793.7 104.6 %fusion.6 = bf16[4,8,256,3072]{3,2,1,0:T(8,128)(2,1)} fusion(f32[4,8,256,3072]{3,2,1,0:T(8,128)} %fusion.11, bf16[4,3072,768]{2,1,0:T(8,128)(2,1)} %param.11, bf16[8,4,256,768]{3,2,1,0:T(8,128)(2,1)} %all-to-all-done.2), kind=kOutput, calls=%fused_computation.13 | convolution fusion | flops 39158022144 | bytes 182452224 | tf_op jit(solution)/shard_map/sekd,efd->eskf/dot_general | solution.py:54
  898.3 49.5 %fusion.16 = f32[4,768,3072]{2,1,0:T(8,128)} fusion(bf16[8,4,256,768]{3,2,1,0:T(8,128)(2,1)} %all_to_all.40, bf16[4,8,256,3072]{3,2,1,0:T(8,128)(2,1)} %fusion.6), kind=kOutput, calls=%fused_computation.24 | convolution fusion | flops 38654705664 | bytes 100663296 | tf_op jit(solution)/shard_map/sekd,eskf->edf/dot_general | solution.py:57
  947.8 48.3 %fusion.25 = bf16[4,8,256,768]{3,2,1,0:T(8,128)(2,1)} fusion(bf16[4,8,256,3072]{3,2,1,0:T(8,128)(2,1)} %fusion.6, bf16[4,768,3072]{2,1,0:T(8,128)(2,1)} %param.10), kind=kOutput, calls=%fused_computation.35 | convolution fusion | flops 38660997120 | bytes 81788928 | tf_op jit(solution)/shard_map/eskf,edf->eskd/dot_general | solution.py:58
  996.1 6.5 copy.27
  1002.7 142.7 %all_to_all.41 = bf16[4,8,256,768]{3,2,0,1:T(8,128)(2,1)} all-to-all(bf16[4,8,256,768]{3,2,0,1:T(8,128)(2,1)S(1)} %copy.27), channel_id=1, replica_groups=mesh['dp'=2,'ep'=8] {'ep'}, dimensions={1} | all-to-all | bytes 25165824 | tf_op jit(solution)/shard_map/all_to_all | solution.py:37
  1145.4 14.7 gather_fusion.4
  1162.9 1418.7 %all-reduce.6.cloned.1.call-done = (f32[4,768,3072]{2,1,0:T(8,128)}, f32[4,3072,768]{2,1,0:T(8,128)}) async-done(((f32[4,768,3072]{2,1,0:T(8,128)}, f32[4,3072,768]{2,1,0:T(8,128)}), (f32[4,768,3072]{2,1,0:T(8,128)}, f32[4,3072,768]{2,1,0:T(8,128)})) %all-reduce.6.cloned.1.call-update) | async-done | bytes 75497488 | tf_op jit(solution)/shard_map/psum | solution.py:65
  2581.6 28.1 %copy.53 = f32[4,768,3072]{2,1,0:T(8,128)} copy(f32[4,768,3072]{2,1,0:T(8,128)} %get-tuple-element.50) | data formatting | bytes 75497472
  2609.7 28.2 %copy.54 = f32[4,3072,768]{2,1,0:T(8,128)} copy(f32[4,3072,768]{2,1,0:T(8,128)} %get-tuple-element.51) | data formatting | bytes 75497472
  (85 shorter events, 30.7 us)
Async XLA Ops:
  7.2 53.0 %copy-start = (bf16[2048,768]{1,0:T(8,128)(2,1)S(1)}, bf16[2048,768]{1,0:T(8,128)(2,1)}, u32[]{:S(2)}) copy-start(bf16[2048,768]{1,0:T(8,128)(2,1)} %param.6) | copy-start | bytes 9437188
  8.5 86.1 %copy-start.6 = (s32[32]{0:T(128)}, s32[32]{0:T(128)S(1)}, u32[]{:S(2)}) copy-start(s32[32]{0:T(128)S(1)} %sub.26) | copy-start | bytes 388
  14.3 80.3 %copy-start.2 = (s32[2048]{0:T(1024)}, s32[2048]{0:T(1024)S(1)}, u32[]{:S(2)}) copy-start(s32[2048]{0:T(1024)S(1)} %get-tuple-element.7) | copy-start | bytes 24580
  60.0 34.6 %copy-start.10 = (s32[8192]{0:T(1024)}, s32[8192]{0:T(1024)S(1)}, u32[]{:S(2)}) copy-start(s32[8192]{0:T(1024)S(1)} %broadcast_clamp_fusion.1) | copy-start | bytes 98308
  60.1 34.5 %copy-start.21 = (pred[8,4,256]{2,1,0:T(4,128)(4,1)}, pred[8,4,256]{2,1,0:T(4,128)(4,1)S(1)}, u32[]{:S(2)}) copy-start(pred[8,4,256]{2,1,0:T(4,128)(4,1)S(1)} %iota_compare_fusion.1) | copy-start | bytes 24580
  367.5 144.7 %all-to-all-start.1 = ((bf16[4,8,256,768]{3,2,0,1:T(8,128)(2,1)}), bf16[4,8,256,768]{3,2,0,1:T(8,128)(2,1)}, u32[]{:S(2)}, u32[]{:S(2)}) async-start(bf16[4,8,256,768]{3,2,0,1:T(8,128)(2,1)} %copy.25), calls=%async_computation.1 | async-start | bytes 25165824 | tf_op jit(solution)/shard_map/all_to_all | solution.py:37
  380.7 208.7 %copy-start.4 = (f32[2048,32]{0,1:T(8,128)}, f32[2048,32]{0,1:T(8,128)S(1)}, u32[]{:S(2)}) copy-start(f32[2048,32]{0,1:T(8,128)S(1)} %get-tuple-element.47) | copy-start | bytes 786436
  380.7 208.7 %copy-start.12 = (f32[2048]{0:T(1024)}, f32[2048]{0:T(1024)S(1)}, u32[]{:S(2)}) copy-start(f32[2048]{0:T(1024)S(1)} %get-tuple-element.46) | copy-start | bytes 24580
  380.8 208.7 %copy-start.16 = (f32[2048]{0:T(1024)}, f32[2048]{0:T(1024)S(1)}, u32[]{:S(2)}) copy-start(f32[2048]{0:T(1024)S(1)} %fusion.32) | copy-start | bytes 24580
  400.4 133.5 %copy-start.23 = (s32[2048]{0:T(1024)}, s32[2048]{0:T(1024)S(1)}, u32[]{:S(2)}) copy-start(s32[2048]{0:T(1024)S(1)} %fusion.35) | copy-start | bytes 24580
  512.2 21.7 copy-start.11
  533.9 39.4 %copy-start.22 = (pred[8,4,256]{2,1,0:T(4,128)(4,1)S(1)}, pred[8,4,256]{2,1,0:T(4,128)(4,1)}, u32[]{:S(2)}) copy-start(pred[8,4,256]{2,1,0:T(4,128)(4,1)} %copy-done.21) | copy-start | bytes 24580
  584.0 145.2 %all-to-all-start.2 = ((bf16[8,4,256,768]{3,2,1,0:T(8,128)(2,1)}), bf16[8,4,256,768]{3,2,1,0:T(8,128)(2,1)}, u32[]{:S(2)}, u32[]{:S(2)}) async-start(bf16[8,4,256,768]{3,2,1,0:T(8,128)(2,1)} %broadcast_select_fusion), calls=%async_computation.2 | async-start | bytes 25165824 | tf_op jit(solution)/shard_map/all_to_all | solution.py:34
  589.4 573.5 %all-reduce.4.cloned.1.call-start = ((), (), s32[]{:S(2)}) async-start(), calls=%async_computation.4 | async-start | bytes 196608 | tf_op jit(solution)/shard_map/psum | solution.py:67
  589.5 204.2 %copy-start.19 = (f32[2048]{0:T(1024)}, f32[2048]{0:T(1024)S(1)}, u32[]{:S(2)}) copy-start(f32[2048]{0:T(1024)S(1)} %fusion.38) | copy-start | bytes 24580
  590.8 1990.8 %all-reduce.6.cloned.1.call-start = ((), (), s32[]{:S(2)}) async-start(), calls=%async_computation.5 | async-start | bytes 150994944 | tf_op jit(solution)/shard_map/psum | solution.py:65
  1002.6 142.8 %copy-start.24 = (s32[2048]{0:T(1024)S(1)}, s32[2048]{0:T(1024)}, u32[]{:S(2)}) copy-start(s32[2048]{0:T(1024)} %copy-done.23) | copy-start | bytes 24580
  1145.4 14.8 copy-start.9
  1145.4 14.8 copy-start.13
  1145.4 14.8 copy-start.15
  1145.4 14.8 copy-start.17
  1145.4 14.8 copy-start.20
  2609.7 28.2 %copy-start.18 = (f32[768,32]{0,1:T(8,128)S(1)}, f32[768,32]{0,1:T(8,128)}, u32[]{:S(2)}) copy-start(f32[768,32]{0,1:T(8,128)} %all-reduce.4.cloned.1.call-done) | copy-start | bytes 294916
  2609.7 28.9 %copy-start.1 = (bf16[2048,768]{1,0:T(8,128)(2,1)S(1)}, bf16[2048,768]{1,0:T(8,128)(2,1)}, u32[]{:S(2)}) copy-start(bf16[2048,768]{1,0:T(8,128)(2,1)} %param.6) | copy-start | bytes 9437188
  (5 other events, 56.7 us)
Sparse Core Ops, SparseCore 0:
  595.0 159.5 all-reduce.3
  947.9 1633.6 all-reduce.5
where the time goes:
time: 2650 us
  waiting for transfers between devices  1670 us (63%)
  matrix products  383 us (14%)
  blocking collectives  287 us (11%)
  local copies, waits for them, and re-layouts  226 us (9%)
  other arithmetic  54.6 us (2%)
    psum x1, waiting for transfers between devices, local_step(): grad_up = lax.psum(grad_up, 'dp')  1420 us
    all_to_all x1, blocking collectives, dispatch(): return lax.all_to_all(picked, 'ep', 0, 0, tiled=True)  144 us
    all_to_all x1, blocking collectives, combine(): returned = lax.all_to_all(expert_rows, 'ep', 1, 0, tiled=True)  143 us
    all_to_all x1, waiting for transfers between devices, dispatch(): return lax.all_to_all(picked, 'ep', 0, 0, tiled=True)  138 us
    all_to_all x1, waiting for transfers between devices, combine(): returned = lax.all_to_all(expert_rows, 'ep', 1, 0, tiled=True)  112 us
    dot_general x1, matrix products, local_step(): jnp.einsum('sekd,efd->eskf', recv_grad, w_down, preferred_element_type=jn...  105 us
    gather x2, local copies, waits for them, and re-layouts, dispatch(): tok_rows[src_tok]  73.8 us
    dot_general x1, matrix products, local_step(): jnp.einsum('eskf,sekd->efd', hidden, recv_grad, preferred_element_type=jn...  64.4 us
  transfers between devices with their start and end apart: 4, of which 3 were waited for; matrix products, arithmetic and copies ran while one was open for 12% of the time, Pallas kernels for 0%

commit v1 on v0

v1 whole, which is shorter than its diff:
```python
import jax
import jax.numpy as jnp
from jax import lax
from jax.experimental import pallas as pl
from jax.experimental.pallas import tpu as pltpu
from jax.sharding import PartitionSpec as P


PAD_FACTOR = 4
GROUP = 8
BASE_GROUPS = 7
OVER_GROUPS = 50
MAX_OVER_TILES = 8
TILE_GROUPS = 26
TILE = TILE_GROUPS * GROUP
PERM_TILE = 256
CHUNK = 512
ROW_CHUNK = 256
SQRT_2_PI = 0.7978845608028654
CUBIC = 0.044715
VMEM_BYTES = 67_043_328

F32 = jnp.float32
BF16 = jnp.bfloat16
I32 = jnp.int32


def dot(a, b, dims=((1,), (0,))):
    return lax.dot_general(a, b, (dims, ((), ())), preferred_element_type=F32)


def exclusive_cumsum(v, axis):
    return jnp.cumsum(v, axis=axis) - v


def token_positions(idx, n_experts):
    tok_count = idx.shape[0]
    block = 128
    base_rows = BASE_GROUPS * GROUP
    onehot = (idx[:, None] == jnp.arange(n_experts, dtype=I32)[None, :]).astype(BF16)
    blocks = onehot.reshape(tok_count // block, block, n_experts)
    lower = jnp.tril(jnp.ones((block, block), BF16))
    inclusive = jnp.einsum('ij,bje->bie', lower, blocks, preferred_element_type=F32)
    totals = jnp.sum(blocks.astype(F32), axis=1)
    counts = jnp.sum(totals, axis=0).astype(I32)
    groups = (counts + GROUP - 1) // GROUP
    over = jnp.maximum(groups - BASE_GROUPS, 0)
    over_start = exclusive_cumsum(over, 0)
    rank = inclusive + (exclusive_cumsum(totals, 0) - 1.0)[:, None, :]
    base_at = jnp.arange(n_experts, dtype=F32) * base_rows
    over_at = (n_experts * base_rows - base_rows + over_start * GROUP).astype(F32)
    row = jnp.sum(blocks.astype(F32) * (rank + jnp.where(rank < base_rows, base_at, over_at)), axis=2)
    return groups, row.reshape(tok_count).astype(I32)


def permute_kernel(pos_ref, x_ref, gy_ref, out_ref):
    rows, d_model = out_ref.shape[0], x_ref.shape[1]
    row_id = pl.program_id(0) * rows + lax.broadcasted_iota(I32, (rows, x_ref.shape[0]), 0)
    select = jnp.where(row_id == pos_ref[...], 1.0, 0.0).astype(BF16)
    out_ref[:, :d_model] = dot(select, x_ref[...]).astype(BF16)
    out_ref[:, d_model:] = dot(select, gy_ref[...]).astype(BF16)


def permute_rows(pos, x, gy, first_row, n_rows):
    tok_count, d_model = x.shape
    tile = n_rows if n_rows % PERM_TILE else PERM_TILE
    return pl.pallas_call(
        permute_kernel,
        grid=(n_rows // tile,),
        in_specs=[
            pl.BlockSpec((1, tok_count), lambda i: (0, 0)),
            pl.BlockSpec((tok_count, d_model), lambda i: (0, 0)),
            pl.BlockSpec((tok_count, d_model), lambda i: (0, 0)),
        ],
        out_specs=pl.BlockSpec((tile, 2 * d_model), lambda i: (i, 0)),
        out_shape=jax.ShapeDtypeStruct((n_rows, 2 * d_model), BF16),
        cost_estimate=pl.CostEstimate(flops=4 * n_rows * tok_count * d_model, bytes_accessed=16_000_000, transcendentals=0),
        name='permute',
    )((pos - first_row).reshape(1, tok_count), x, gy)


def unpermute_kernel(pos_ref, base_ref, over_ref, out_ref, dx_ref):
    toks, d_model = out_ref.shape
    n_base = base_ref.shape[0]
    base_id = lax.broadcasted_iota(I32, (toks, n_base), 1)
    over_id = lax.broadcasted_iota(I32, (toks, over_ref.shape[0]), 1) + n_base
    base = jnp.where(base_id == pos_ref[...], 1.0, 0.0).astype(BF16)
    over = jnp.where(over_id == pos_ref[...], 1.0, 0.0).astype(BF16)
    out_ref[...] = (dot(base, base_ref[:, :d_model]) + dot(over, over_ref[:, :d_model])).astype(BF16)
    dx_ref[...] = (dot(base, base_ref[:, d_model:]) + dot(over, over_ref[:, d_model:])).astype(BF16)


def unpermute_rows(pos, base, over):
    n_base, width = base.shape
    tok_count = pos.shape[0]
    d_model = width // 2
    shape = jax.ShapeDtypeStruct((tok_count, d_model), BF16)
    return pl.pallas_call(
        unpermute_kernel,
        grid=(tok_count // PERM_TILE,),
        in_specs=[
            pl.BlockSpec((PERM_TILE, 1), lambda i: (i, 0)),
            pl.BlockSpec(base.shape, lambda i: (0, 0)),
            pl.BlockSpec(over.shape, lambda i: (0, 0)),
        ],
        out_specs=[pl.BlockSpec((PERM_TILE, d_model), lambda i: (i, 0))] * 2,
        out_shape=[shape, shape],
        cost_estimate=pl.CostEstimate(flops=4 * n_base * tok_count * d_model, bytes_accessed=16_000_000, transcendentals=0),
        name='unpermute',
    )(pos.reshape(tok_count, 1), base, over)


def gate(x, wg, expert):
    logit = dot(x, wg)
    unnorm = jnp.exp(logit - jnp.max(logit, axis=1, keepdims=True))
    prob = unnorm / jnp.sum(unnorm, axis=1, keepdims=True)
    onehot = lax.broadcasted_iota(I32, prob.shape, 1) == expert
    gate_val = prob.shape[1] * jnp.sum(jnp.where(onehot, prob, 0.0), axis=1, keepdims=True)
    return prob, onehot, gate_val


def activations(x, dy, w_up, w_down, cols):
    a = dot(x, w_up[:, cols])
    dh = dot(dy, w_down[cols, :], ((1,), (1,)))
    cubic = (SQRT_2_PI * CUBIC) * (a * a)
    half = 0.5 + 0.5 * jnp.tanh(a * (SQRT_2_PI + cubic))
    h = a * half
    slope = half + (h - h * half) * (2.0 * SQRT_2_PI + 6.0 * cubic)
    return h.astype(BF16), (slope * dh).astype(BF16)


def own_rows_step(x, gy, expert, wg_ref, w_up, w_down, store, dwg_ref):
    dy_ref, h_ref, da_ref = store
    prob, onehot, gate_val = gate(x, wg_ref[...], expert)
    gy_full = gy.astype(F32)
    dy = (gate_val * gy_full).astype(BF16)
    dy_ref[...] = dy
    for lo in range(0, h_ref.shape[1], ROW_CHUNK):
        cols = pl.ds(lo, ROW_CHUNK)
        h, da = activations(x, dy, w_up, w_down, cols)
        h_ref[:, cols] = h
        da_ref[:, cols] = da
    y = dot(h_ref[...], w_down[...]).astype(BF16).astype(F32)
    dxe = dot(da_ref[...], w_up[...], ((1,), (1,))).astype(BF16).astype(F32)
    d_gate = jnp.sum(gy_full * y, axis=1, keepdims=True)
    d_logit = ((d_gate * gate_val) * (onehot.astype(F32) - prob)).astype(BF16)
    dwg_ref[...] += dot(x, d_logit, ((0,), (0,)))
    out = (gate_val * y).astype(BF16)
    dx = (dxe + dot(d_logit, wg_ref[...], ((1,), (1,)))).astype(BF16)
    return out, dx


def own_base_kernel(first_ref, rows_ref, wg_ref, up_ref, down_ref, od_ref, dy_ref, h_ref, da_ref, dwg_ref, zero_ref):
    expert = pl.program_id(0)
    d_model = wg_ref.shape[0]

    @pl.when(expert == 0)
    def _():
        dwg_ref[...] = jnp.zeros_like(dwg_ref)

    zero_ref[...] = jnp.zeros_like(zero_ref)
    rows = rows_ref[...].reshape(dy_ref.shape[0], 2 * d_model)
    out, dx = own_rows_step(rows[:, :d_model], rows[:, d_model:], first_ref[0] + expert, wg_ref,
                            up_ref.at[0], down_ref.at[0], (dy_ref, h_ref, da_ref), dwg_ref)
    block = od_ref.shape[:3] + (d_model,)
    od_ref[:, :, :, :d_model] = out.reshape(block)
    od_ref[:, :, :, d_model:] = dx.reshape(block)


def own_base_pass(first_expert, rows, wg, w_up, w_down, over_shape):
    n_src, local, seg, width = rows.shape
    d_model, d_ff = w_up.shape[1], w_up.shape[2]
    tile = n_src * seg
    row_spec = pl.BlockSpec((n_src, 1, seg, width), lambda e, first: (0, e, 0, 0))
    store_spec = lambda cols: pl.BlockSpec((tile, cols), lambda e, first: (e, 0))
    const = lambda e, first: (0, 0)
    rows_of = lambda cols: jax.ShapeDtypeStruct((local * tile, cols), BF16)
    zero_block = (over_shape[0] // local,) + over_shape[1:]
    return pl.pallas_call(
        own_base_kernel,
        grid_spec=pltpu.PrefetchScalarGridSpec(
            num_scalar_prefetch=1,
            grid=(local,),
            in_specs=[
                row_spec,
                pl.BlockSpec(wg.shape, const),
                pl.BlockSpec((1, d_model, d_ff), lambda e, first: (e, 0, 0)),
                pl.BlockSpec((1, d_ff, d_model), lambda e, first: (e, 0, 0)),
            ],
            out_specs=[row_spec, store_spec(d_model), store_spec(d_ff), store_spec(d_ff), pl.BlockSpec(wg.shape, const),
                       pl.BlockSpec(zero_block, lambda e, first: (e, 0, 0))],
        ),
        out_shape=[jax.ShapeDtypeStruct(rows.shape, BF16), rows_of(d_model), rows_of(d_ff), rows_of(d_ff),
                   jax.ShapeDtypeStruct(wg.shape, F32), jax.ShapeDtypeStruct(over_shape, BF16)],
        compiler_params=pltpu.CompilerParams(vmem_limit_bytes=VMEM_BYTES, dimension_semantics=('arbitrary',)),
        cost_estimate=pl.CostEstimate(flops=34_000_000_000, bytes_accessed=80_000_000, transcendentals=6_000_000),
        name='own_base',
    )(first_expert, rows, wg, w_up, w_down)


def group_copies(ids_ref, slot_base, count, hbm, buf, sem, to_hbm):
    def body(g, carry):
        gid = ids_ref[slot_base + g]
        ends = (buf.at[g], hbm.at[gid]) if to_hbm else (hbm.at[gid], buf.at[g])
        pltpu.make_async_copy(*ends, sem).start()
        return carry

    lax.fori_loop(0, count, body, 0)


def group_waits(count, hbm, buf, sem, to_hbm):
    def body(g, carry):
        ends = (buf.at[0], hbm.at[0]) if to_hbm else (hbm.at[0], buf.at[0])
        pltpu.make_async_copy(*ends, sem).wait()
        return carry

    lax.fori_loop(0, count, body, 0)


def tile_rows(buf, count):
    rows = buf[...].reshape(TILE, buf.shape[-1])
    row_id = lax.broadcasted_iota(I32, rows.shape, 0)
    return jnp.where(row_id < count * GROUP, rows, jnp.zeros((), rows.dtype))


def own_over_kernel(tab_ref, ids_ref, first_ref, rows_hbm, wg_ref, up_ref, down_ref, dwg_in, zero_od,
                    od_hbm, x_ref, dy_ref, h_ref, da_ref, dwg_ref, in_buf, out_buf, in_sem, out_sem):
    del zero_od
    step = pl.program_id(0)
    d_model = wg_ref.shape[0]
    slot = step % 2
    count = tab_ref[1, step]

    @pl.when(step == 0)
    def _():
        dwg_ref[...] = dwg_in[...]
        group_copies(ids_ref, 0, count, rows_hbm, in_buf.at[0], in_sem.at[0], False)

    @pl.when(count > 0)
    def _():
        group_waits(count, rows_hbm, in_buf.at[slot], in_sem.at[slot], False)

        @pl.when(step + 1 < pl.num_programs(0))
        def _():
            group_copies(ids_ref, (step + 1) * TILE_GROUPS, tab_ref[1, step + 1], rows_hbm, in_buf.at[1 - slot],
                         in_sem.at[1 - slot], False)

        rows = tile_rows(in_buf.at[slot], count)
        x = rows[:, :d_model]
        x_ref[...] = x
        out, dx = own_rows_step(x, rows[:, d_model:], first_ref[0] + tab_ref[0, step], wg_ref,
                                up_ref.at[0], down_ref.at[0], (dy_ref, h_ref, da_ref), dwg_ref)

        @pl.when(step > 0)
        def _():
            group_waits(tab_ref[1, step - 1], od_hbm, out_buf, out_sem, True)

        out_buf[:, :, :d_model] = out.reshape(TILE_GROUPS, GROUP, d_model)
        out_buf[:, :, d_model:] = dx.reshape(TILE_GROUPS, GROUP, d_model)
        group_copies(ids_ref, step * TILE_GROUPS, count, od_hbm, out_buf, out_sem, True)

        @pl.when(tab_ref[3, step] == 1)
        def _():
            group_waits(count, od_hbm, out_buf, out_sem, True)


def own_over_pass(table, ids, first_expert, rows, wg, w_up, w_down, dwg, zero_od):
    d_model, d_ff = w_up.shape[1], w_up.shape[2]
    width = rows.shape[-1]
    n_tiles = table.shape[1]
    hbm = pl.BlockSpec(memory_space=pl.ANY)
    const = lambda i, tab, ids, first: (0, 0)
    store_spec = lambda cols: pl.BlockSpec((TILE, cols), lambda i, tab, ids, first: (tab[2, i], 0))
    rows_of = lambda cols: jax.ShapeDtypeStruct((n_tiles * TILE, cols), BF16)
    return pl.pallas_call(
        own_over_kernel,
        grid_spec=pltpu.PrefetchScalarGridSpec(
            num_scalar_prefetch=3,
            grid=(n_tiles,),
            in_specs=[
                hbm,
                pl.BlockSpec(wg.shape, const),
                pl.BlockSpec((1, d_model, d_ff), lambda i, tab, ids, first: (tab[0, i], 0, 0)),
                pl.BlockSpec((1, d_ff, d_model), lambda i, tab, ids, first: (tab[0, i], 0, 0)),
                pl.BlockSpec(wg.shape, const),
                hbm,
            ],
            out_specs=[hbm, store_spec(d_model), store_spec(d_model), store_spec(d_ff), store_spec(d_ff),
                       pl.BlockSpec(wg.shape, const)],
            scratch_shapes=[
                pltpu.VMEM((2, TILE_GROUPS, GROUP, width), BF16),
                pltpu.VMEM((TILE_GROUPS, GROUP, width), BF16),
                pltpu.SemaphoreType.DMA((2,)),
                pltpu.SemaphoreType.DMA,
            ],
        ),
        out_shape=[jax.ShapeDtypeStruct(zero_od.shape, BF16), rows_of(d_model), rows_of(d_model), rows_of(d_ff),
                   rows_of(d_ff), jax.ShapeDtypeStruct(dwg.shape, F32)],
        input_output_aliases={8: 0},
        compiler_params=pltpu.CompilerParams(vmem_limit_bytes=VMEM_BYTES, dimension_semantics=('arbitrary',)),
        cost_estimate=pl.CostEstimate(flops=10_000_000_000, bytes_accessed=40_000_000, transcendentals=2_000_000),
        name='own_over',
    )(table, ids, first_expert, rows, wg, w_up, w_down, dwg, zero_od)


OWN_BASE, OWN_OVER, OTHER_BASE, OTHER_OVER = range(4)


def grad_kernel(tab_ref, ids_ref, first_ref, xb_ref, dyb_ref, hb_ref, dab_ref, xo_ref, dyo_ref, ho_ref, dao_ref, base_ref,
                over_hbm, wg_ref, up_hbm, down_hbm, dup_hbm, ddown_hbm,
                dup, ddown, up_buf, down_buf, h_buf, da_buf, in_buf, w_sems, in_sem, out_sems):
    step = pl.program_id(0)
    d_model, d_ff = dup.shape
    expert, kind, last, count = tab_ref[0, step], tab_ref[1, step], tab_ref[2, step], tab_ref[4, step]
    n_local = dup_hbm.shape[0]
    base_rows = h_buf.shape[0]

    def weights(e):
        return (pltpu.make_async_copy(up_hbm.at[e], up_buf, w_sems.at[0]),
                pltpu.make_async_copy(down_hbm.at[e], down_buf, w_sems.at[1]))

    def flush_down(e):
        return pltpu.make_async_copy(ddown, ddown_hbm.at[e], out_sems.at[0])

    def flush_up(e):
        return pltpu.make_async_copy(dup, dup_hbm.at[e], out_sems.at[1])

    def add_down(dy, h_src, add):
        for lo in range(0, d_ff, CHUNK):
            cols = pl.ds(lo, CHUNK)
            term = dot(h_src[:, cols], dy, ((0,), (0,)))
            ddown[cols, :] = ddown[cols, :] + term if add else term

    def add_up(x, da_src, add):
        for lo in range(0, d_ff, CHUNK):
            cols = pl.ds(lo, CHUNK)
            term = dot(x, da_src[:, cols], ((0,), (0,)))
            dup[:, cols] = dup[:, cols] + term if add else term

    def accumulate(x, dy, h_src, da_src):
        add_down(dy, h_src, True)

        @pl.when(last == 1)
        def _():
            flush_down(expert).start()

        add_up(x, da_src, True)

        @pl.when(last == 1)
        def _():
            flush_up(expert).start()

            @pl.when(expert + 1 < n_local)
            def _():
                for copy in weights(expert + 1):
                    copy.start()

            @pl.when(expert + 1 == n_local)
            def _():
                flush_down(expert).wait()
                flush_up(expert).wait()

    @pl.when(kind == OWN_BASE)
    def _():
        @pl.when(expert == 0)
        def _():
            for copy in weights(0):
                copy.start()

        @pl.when(expert > 0)
        def _():
            flush_down(expert - 1).wait()

        add_down(dyb_ref[...], hb_ref, False)

        @pl.when(expert > 0)
        def _():
            flush_up(expert - 1).wait()

        add_up(xb_ref[...].reshape(base_rows, d_model), dab_ref, False)

    @pl.when(kind == OWN_OVER)
    def _():
        add_down(dyo_ref[...], ho_ref, True)
        add_up(xo_ref[...], dao_ref, True)

    def other_rows(rows, n_rows):
        x, gy = rows[:, :d_model], rows[:, d_model:]
        _, _, gate_val = gate(x, wg_ref[...], first_ref[0] + expert)
        dy = (gate_val * gy.astype(F32)).astype(BF16)
        h_dst, da_dst = h_buf.at[:n_rows], da_buf.at[:n_rows]
        for lo in range(0, d_ff, ROW_CHUNK):
            cols = pl.ds(lo, ROW_CHUNK)
            h, da = activations(x, dy, up_buf, down_buf, cols)
            h_dst[:, cols] = h
            da_dst[:, cols] = da
        accumulate(x, dy, h_dst, da_dst)

    @pl.when(kind == OTHER_BASE)
    def _():
        for copy in weights(expert):
            copy.wait()
        other_rows(base_ref[...].reshape(base_rows, 2 * d_model), base_rows)

    @pl.when(kind == OTHER_OVER)
    def _():
        group_copies(ids_ref, tab_ref[5, step] * TILE_GROUPS, count, over_hbm, in_buf, in_sem, False)
        group_waits(count, over_hbm, in_buf, in_sem, False)
        other_rows(tile_rows(in_buf, count), TILE)


def grad_pass(table, ids, first_expert, own_base, base_store, over_store, base, over, wg, w_up, w_down):
    n_src, _, seg, width = base.shape
    d_model, d_ff = w_up.shape[1], w_up.shape[2]
    base_rows = n_src * seg
    base_spec = lambda cols: pl.BlockSpec((base_rows, cols), lambda i, tab, ids, first: (tab[6, i], 0))
    over_spec = lambda cols: pl.BlockSpec((TILE, cols), lambda i, tab, ids, first: (tab[3, i], 0))
    slot_spec = lambda cols, row: pl.BlockSpec((n_src, 1, seg, cols), lambda i, tab, ids, first: (0, tab[row, i], 0, 0))
    hbm = pl.BlockSpec(memory_space=pl.ANY)
    return pl.pallas_call(
        grad_kernel,
        grid_spec=pltpu.PrefetchScalarGridSpec(
            num_scalar_prefetch=3,
            grid=(table.shape[1],),
            in_specs=[
                slot_spec(d_model, 6),
                base_spec(d_model),
                base_spec(d_ff),
                base_spec(d_ff),
                over_spec(d_model),
                over_spec(d_model),
                over_spec(d_ff),
                over_spec(d_ff),
                slot_spec(width, 0),
                hbm,
                pl.BlockSpec(wg.shape, lambda i, tab, ids, first: (0, 0)),
                hbm,
                hbm,
            ],
            out_specs=[hbm, hbm],
            scratch_shapes=[
                pltpu.VMEM((d_model, d_ff), F32),
                pltpu.VMEM((d_ff, d_model), F32),
                pltpu.VMEM((d_model, d_ff), BF16),
                pltpu.VMEM((d_ff, d_model), BF16),
                pltpu.VMEM((base_rows, d_ff), BF16),
                pltpu.VMEM((base_rows, d_ff), BF16),
                pltpu.VMEM((TILE_GROUPS, GROUP, width), BF16),
                pltpu.SemaphoreType.DMA((2,)),
                pltpu.SemaphoreType.DMA,
                pltpu.SemaphoreType.DMA((2,)),
            ],
        ),
        out_shape=[jax.ShapeDtypeStruct(w_up.shape, F32), jax.ShapeDtypeStruct(w_down.shape, F32)],
        compiler_params=pltpu.CompilerParams(vmem_limit_bytes=VMEM_BYTES, dimension_semantics=('arbitrary',)),
        cost_estimate=pl.CostEstimate(flops=70_000_000_000, bytes_accessed=150_000_000, transcendentals=8_000_000),
        name='grad_pass',
    )(table, ids, first_expert, own_base, *base_store, *over_store, base, over, wg, w_up, w_down)


def over_tiles(over, start, max_tiles):
    per_expert = jnp.sum(over, axis=0)
    tiles = (per_expert + TILE_GROUPS - 1) // TILE_GROUPS
    end = jnp.cumsum(tiles)
    step = jnp.arange(max_tiles, dtype=I32)
    expert = jnp.minimum(jnp.sum(step[:, None] >= end[None, :], axis=1, dtype=I32), over.shape[1] - 1)
    pick = (expert[:, None] == jnp.arange(over.shape[1], dtype=I32)[None, :]).astype(I32)
    of = lambda v: jnp.sum(pick * v[None, :], axis=1)
    done = (step - of(end - tiles)) * TILE_GROUPS
    count = jnp.clip(of(per_expert) - done, 0, TILE_GROUPS)
    rank = done[:, None] + jnp.arange(TILE_GROUPS, dtype=I32)[None, :]
    before = exclusive_cumsum(over, 0)
    shift = jnp.sum(pick[:, None, :] * (start - before)[None, :, :], axis=2)
    first = jnp.sum(pick[:, None, :] * before[None, :, :], axis=2)
    size = jnp.sum(pick[:, None, :] * over[None, :, :], axis=2)
    inside = (rank[:, :, None] >= first[:, None, :]) & (rank[:, :, None] < (first + size)[:, None, :])
    gid = jnp.sum(jnp.where(inside, rank[:, :, None] + shift[:, None, :], 0), axis=2)
    return expert, count, gid.reshape(-1), end - tiles, tiles


def grad_table(own_first, own_tiles, other_first, other_tiles, other_count, max_steps):
    n_exp = own_tiles.shape[0]
    one = jnp.ones((n_exp,), I32)
    length = jnp.stack([one, own_tiles, one, other_tiles], axis=1).reshape(-1)
    end = jnp.cumsum(length)
    step = jnp.arange(max_steps, dtype=I32)
    seg = jnp.minimum(jnp.sum(step[:, None] >= end[None, :], axis=1, dtype=I32), 4 * n_exp - 1)
    pick = (seg[:, None] == jnp.arange(4 * n_exp, dtype=I32)[None, :]).astype(I32)
    of = lambda v: jnp.sum(pick * v[None, :], axis=1)
    tile = step - of(end - length)
    expert, kind = seg // 4, seg % 4
    live = step < end[-1]
    last = live & (step + 1 == of(jnp.repeat(end[3::4], 4)))
    last_own = jnp.maximum(jnp.sum(own_tiles) - 1, 0)
    own_tile = jnp.where(kind == OWN_OVER, of(jnp.repeat(own_first, 4)) + tile, of(jnp.repeat(own_first + own_tiles, 4)))
    own_tile = jnp.where(kind == OWN_BASE, of(jnp.repeat(own_first, 4)), own_tile)
    other_tile = jnp.where(kind == OTHER_OVER, of(jnp.repeat(other_first, 4)) + tile, 0)
    tile_pick = (other_tile[:, None] == jnp.arange(other_count.shape[0], dtype=I32)[None, :]).astype(I32)
    count = jnp.sum(tile_pick * other_count[None, :], axis=1)
    next_base = jnp.minimum(expert + (kind > OWN_BASE), n_exp - 1)
    return jnp.stack([expert, jnp.where(live, kind, -1), last.astype(I32), jnp.minimum(own_tile, last_own), count,
                      jnp.minimum(other_tile, other_count.shape[0] - 1), next_base]).astype(I32)


def padded_step(x_loc, gy_loc, idx_loc, w_gate, w_up, w_down, ep_size, dp_size):
    tok_count, d_model = x_loc.shape
    n_experts = w_gate.shape[1]
    local_experts = w_up.shape[0]
    cap_rows = PAD_FACTOR * tok_count // n_experts
    onehot = idx_loc[:, None] == jnp.arange(n_experts, dtype=I32)[None, :]
    expert_count = jnp.sum(onehot, axis=0, dtype=I32)
    sort_order = jnp.argsort(idx_loc, stable=True)
    sorted_pos = jnp.argsort(sort_order)
    expert_start = jnp.cumsum(expert_count) - expert_count
    slot_k = jnp.arange(cap_rows, dtype=I32)
    slot_valid = slot_k[None, :] < expert_count[:, None]
    src_tok = sort_order[jnp.minimum(expert_start[:, None] + slot_k[None, :], tok_count - 1)]
    slot_tok = idx_loc * cap_rows + sorted_pos - expert_start[idx_loc]

    def dispatch(tok_rows):
        picked = jnp.where(slot_valid[:, :, None], tok_rows[src_tok], jnp.zeros((), tok_rows.dtype))
        picked = picked.reshape(ep_size, local_experts, cap_rows, d_model)
        return lax.all_to_all(picked, 'ep', 0, 0, tiled=True)

    def combine(expert_rows):
        returned = lax.all_to_all(expert_rows, 'ep', 1, 0, tiled=True)
        return returned.reshape(n_experts * cap_rows, d_model)[slot_tok]

    router_logit = jnp.dot(x_loc, w_gate, preferred_element_type=F32)
    router_prob = jax.nn.softmax(router_logit, axis=-1)
    gate_val = n_experts * jnp.sum(jnp.where(onehot, router_prob, 0.0), axis=1)
    recv_rows = dispatch(x_loc)
    gy_full = gy_loc.astype(F32)
    dy_tok = (gate_val[:, None] * gy_full).astype(BF16)
    recv_grad = dispatch(dy_tok)

    def one_expert(carry, per_expert):
        rows, grad, up, down = per_expert
        rows, grad = rows.reshape(-1, d_model), grad.reshape(-1, d_model)
        pre_act = dot(rows, up)
        hid_full, gelu_back = jax.vjp(jax.nn.gelu, pre_act)
        hidden = hid_full.astype(BF16)
        out_rows = dot(hidden, down).astype(BF16)
        d_pre = gelu_back(dot(grad, down, ((1,), (1,))))[0].astype(BF16)
        grad_down = dot(hidden, grad, ((0,), (0,)))
        grad_up = dot(rows, d_pre, ((0,), (0,)))
        d_rows = dot(d_pre, up, ((1,), (1,))).astype(BF16)
        shape = (ep_size, cap_rows, d_model)
        return carry, (out_rows.reshape(shape), d_rows.reshape(shape), grad_up, grad_down)

    swap = lambda rows: jnp.swapaxes(rows, 0, 1)
    _, (expert_out, d_rows, grad_up, grad_down) = lax.scan(
        one_expert, 0, (swap(recv_rows), swap(recv_grad), w_up, w_down))
    y_tok = combine(expert_out)
    moe_out = (gate_val[:, None] * y_tok.astype(F32)).astype(BF16)
    dx_expert = combine(d_rows)
    d_gate = jnp.sum(gy_full * y_tok.astype(F32), axis=1)
    d_logit = ((d_gate * gate_val)[:, None] * (onehot.astype(F32) - router_prob)).astype(BF16)
    dx_router = dot(d_logit, w_gate, ((1,), (1,)))
    grad_x = (dx_expert.astype(F32) + dx_router).astype(BF16)
    grad_gate = dot(x_loc, d_logit, ((0,), (0,)))

    def sum_dp(term):
        total = term
        for shift in range(1, dp_size):
            total = total + lax.ppermute(term, 'dp', [(i, (i + shift) % dp_size) for i in range(dp_size)])
        return total

    return (moe_out, grad_x, sum_dp(grad_up), sum_dp(grad_down), lax.psum(grad_gate, ('dp', 'ep')))


def solution(mesh):
    dp_size, ep_size = mesh.shape['dp'], mesh.shape['ep']
    tok_spec = P(('dp', 'ep'), None)
    idx_spec = P(('dp', 'ep'))
    rep_spec = P(None, None)
    exp_spec = P('ep', None, None)
    swap = [(i, (i + 1) % dp_size) for i in range(dp_size)]

    def local_step(x, gy, idx, w_gate, w_up, w_down):
        _, d_model = x.shape
        n_experts = w_gate.shape[1]
        local = w_up.shape[0]
        width = 2 * d_model
        base_rows = BASE_GROUPS * GROUP
        n_base = n_experts * base_rows
        n_over = OVER_GROUPS * GROUP
        max_tiles = MAX_OVER_TILES
        max_steps = 2 * (local + max_tiles)
        dp, ep = lax.axis_index('dp'), lax.axis_index('ep')
        first_expert = (ep * local).astype(I32).reshape(1)

        my_groups, pos = token_positions(idx, n_experts)
        base_sent = permute_rows(pos, x, gy, 0, n_base)
        base = lax.all_to_all(base_sent.reshape(ep_size, local * base_rows, width), 'ep', 0, 0, tiled=True)
        over_sent = permute_rows(pos, x, gy, n_base, n_over).reshape(OVER_GROUPS, GROUP, width)
        all_groups = lax.all_gather(my_groups, ('dp', 'ep')).reshape(dp_size, ep_size, n_experts)
        over = lax.all_gather(over_sent, 'ep').reshape(ep_size * OVER_GROUPS, GROUP, width)
        base_z = lax.ppermute(base, 'dp', swap)
        over_sent_z = lax.ppermute(over_sent, 'dp', swap)
        over_z = lax.all_gather(over_sent_z, 'ep').reshape(over.shape)

        all_over = jnp.maximum(all_groups - BASE_GROUPS, 0)
        owner_over = jnp.sum(all_over, axis=1).reshape(dp_size * ep_size, local)
        owner_tiles = jnp.sum((owner_over + TILE_GROUPS - 1) // TILE_GROUPS, axis=1)
        fits = jnp.all(jnp.sum(all_over, axis=2) <= OVER_GROUPS) & jnp.all(owner_tiles <= max_tiles)
        all_over = jnp.where(fits, all_over, 0)

        def plane_over(plane):
            over = lax.dynamic_index_in_dim(all_over, plane, 0, keepdims=False)
            start = exclusive_cumsum(over, 1) + (jnp.arange(ep_size, dtype=I32) * OVER_GROUPS)[:, None]
            here = lambda t: lax.dynamic_slice_in_dim(t, ep * local, local, 1)
            return over_tiles(here(over), here(start), max_tiles)

        expert, count, ids, own_first, own_tiles = plane_over(dp)
        _, count_z, ids_z, other_first, other_tiles = plane_over((dp + 1) % dp_size)
        gtable = grad_table(own_first, own_tiles, other_first, other_tiles, count_z, max_steps)
        tile_id = jnp.arange(max_tiles, dtype=I32)
        last = jnp.maximum(jnp.sum(own_tiles) - 1, 0)
        table = jnp.stack([expert, count, jnp.minimum(tile_id, last), tile_id == last]).astype(I32)

        slots = (ep_size, local, base_rows, width)
        base = base.reshape(slots)
        od, dy_b, h_b, da_b, dwg, zero_od = own_base_pass(first_expert, base, w_gate, w_up, w_down, over.shape)
        base_back = lax.all_to_all(od.reshape(ep_size, local * base_rows, width), 'ep', 0, 0, tiled=True)
        od_over, x_o, dy_o, h_o, da_o, dwg = own_over_pass(table, ids, first_expert, over, w_gate, w_up, w_down, dwg,
                                                          zero_od)
        over_back = lax.psum_scatter(od_over.reshape(ep_size, OVER_GROUPS, GROUP, width), 'ep', scatter_dimension=0)
        d_up, d_down = grad_pass(gtable, ids_z, first_expert, base, (dy_b, h_b, da_b), (x_o, dy_o, h_o, da_o),
                                 base_z.reshape(slots), over_z, w_gate, w_up, w_down)
        d_gate = lax.psum(dwg, ('dp', 'ep'))
        moe_out, grad_x = unpermute_rows(pos, base_back.reshape(n_base, width), over_back.reshape(n_over, width))
        sparse = (moe_out, grad_x, d_up, d_down, d_gate)

        def dense(carry):
            del carry
            return (jnp.array(True),) + padded_step(x, gy, idx, w_gate, w_up, w_down, ep_size, dp_size)

        return lax.while_loop(lambda carry: jnp.logical_not(carry[0]), dense, (fits,) + sparse)[1:]

    return jax.shard_map(
        local_step, mesh=mesh, in_specs=(tok_spec, tok_spec, idx_spec, rep_spec, exp_spec, exp_spec),
        out_specs=(tok_spec, tok_spec, exp_spec, exp_spec, rep_spec), check_vma=False)
```

time: 2650 us -> 581 us (0.22)
  the two profiles are of different devices: /device:TPU:0 before, /device:TPU:9 now
where the time goes in v1:
time: 581 us; the launch traced here: 576 us
  Pallas kernels  263 us (45%)
  waiting for transfers between devices  200 us (34%)
  blocking collectives  35.6 us (6%)
  starting transfers between devices  31.9 us (5%)
  between operations  16.2 us (3%)
  local copies, waits for them, and re-layouts  14.5 us (2%)
  other arithmetic  12.7 us (2%)
    pallas_call x1, Pallas kernels, grad_pass(): pl.pallas_call(grad_kernel, grid_spec=pltpu.PrefetchScalarGridSpec(num_sc...  140 us
    all_gather x1, waiting for transfers between devices, local_step(): over_z = lax.all_gather(over_sent_z, 'ep').reshape(over.shape)  70.2 us
    pallas_call x1, Pallas kernels, own_base_pass(): pl.pallas_call(own_base_kernel, grid_spec=pltpu.PrefetchScalarGridSpec(nu...  49.1 us
    all_to_all x1, waiting for transfers between devices, local_step(): lax.all_to_all(base_sent.reshape(ep_size, local * base_rows, width), 'ep'...  48.4 us
    psum x1, waiting for transfers between devices, local_step(): d_gate = lax.psum(dwg, ('dp', 'ep'))  47.2 us
    all_gather x1, blocking collectives, local_step(): lax.all_gather(my_groups, ('dp', 'ep')).reshape(dp_size, ep_size, n_experts)  35.6 us
    ppermute x1, waiting for transfers between devices, local_step(): base_z = lax.ppermute(base, 'dp', swap)  33.2 us
    pallas_call x1, Pallas kernels, own_over_pass(): pl.pallas_call(own_over_kernel, grid_spec=pltpu.PrefetchScalarGridSpec(nu...  30.2 us
  transfers between devices with their start and end apart: 8, of which 4 were waited for; matrix products, arithmetic and copies ran while one was open for 4% of the time, Pallas kernels for 41%

profile of v1, /device:TPU:9, one launch (start us, length us, event | category | flops | bytes accessed | tf_op | source)
XLA Modules:
  0.0 576.1 jit_solution(4511768671792003897)
XLA Ops:
  7.2 0.9 convert_reduce_fusion.1
  8.5 1.0 fusion.41
  10.2 6.6 %permute.3 = bf16[400,1536]{1,0:T(8,128)(2,1)} custom-call(s32[1,2048]{1,0:T(1,128)} %broadcast_add_fusion.pos_ref, bf16[2048,768]{1,0:T(8,128)(2,1)} %x_ref.3, bf16[2048,768]{1,0:T(8,128)(2,1)} %gy_ref.3), custom_call_target="tpu_custom_call" | custom-call | flops 2516582400 | bytes 16000000 | tf_op jit(solution)/shard_map/permute/pallas_call | solution.py:67
  16.9 35.6 %all-gather.1 = s32[16,1,32]{2,1,0:T(1,128)S(1)} all-gather(s32[1,1,32]{2,1,0:T(1,128)S(1)} %fusion.61), channel_id=1, replica_groups=mesh['dp'=2,'ep'=8] {'dp','ep'}, dimensions={0}, use_global_device_ids=true | all-gather | bytes 2176 | tf_op jit(solution)/shard_map/all_gather | solution.py:597
  52.7 16.5 %permute.2 = bf16[1792,1536]{1,0:T(8,128)(2,1)} custom-call(s32[1,2048]{1,0:T(1,128)} %bitcast.291, bf16[2048,768]{1,0:T(8,128)(2,1)} %x_ref.3, bf16[2048,768]{1,0:T(8,128)(2,1)} %gy_ref.3), custom_call_target="tpu_custom_call" | custom-call | flops 11274289152 | bytes 16000000 | tf_op jit(solution)/shard_map/permute/pallas_call | solution.py:67
  69.2 4.7 all-to-all-start.4
  83.7 0.8 copy.131.wg_ref
  85.2 48.4 %all-to-all-done.4 = bf16[8,224,1536]{2,1,0:T(8,128)(2,1)} async-done(((bf16[8,224,1536]{2,1,0:T(8,128)(2,1)}), bf16[8,224,1536]{2,1,0:T(8,128)(2,1)}, u32[]{:S(2)}, u32[]{:S(2)}) %all-to-all-start.4) | async-done | bytes 5505056 | tf_op jit(solution)/shard_map/all_to_all | solution.py:595
  133.6 49.1 %own_base.1 = (bf16[8,4,56,1536]{3,2,1,0:T(8,128)(2,1)}, bf16[1792,768]{1,0:T(8,128)(2,1)}, bf16[1792,3072]{1,0:T(8,128)(2,1)}, bf16[1792,3072]{1,0:T(8,128)(2,1...) custom-call(s32[1]{0:T(128)} %bitcast.63.first_ref, bf16[8,4,56,1536]{3,2,1,0:T(8,128)(2,1)} %bitcast.66.rows_ref.xb_ref, ...), custom_call_target="tpu_custom_call" | custom-call | flops 33999998976 | bytes 80000000 | tf_op jit(solution)/shard_map/own_base/pallas_call | solution.py:179
  182.7 30.2 %own_over.1 = (bf16[400,8,1536]{2,1,0:T(8,128)(2,1)}, bf16[1664,768]{1,0:T(8,128)(2,1)}, bf16[1664,768]{1,0:T(8,128)(2,1)}, bf16[1664,3072]{1,0:T(8,128)(2,1)}, ...) custom-call(s32[4,8]{1,0:T(4,128)} %pad_add_fusion.tab_ref, ...), custom_call_target="tpu_custom_call", output_to_operand_aliasing={{0}: (8, {})} | custom-call | flops 10000000000 | bytes 40000000 | tf_op jit(solution)/shard_map/own_over/pallas_call | solution.py:275
  214.3 20.6 %collective-permute-start.2 = (bf16[8,224,1536]{2,1,0:T(8,128)(2,1)}, bf16[8,224,1536]{2,1,0:T(8,128)(2,1)}, u32[]{:S(2)}, u32[]{:S(2)}) collective-permute-start(bf16[8,224,1536]{2,1,0:T(8,128)(2,1)} %all-to-all-done.4), channel_id=1, source_target_pairs={{0,8},{8,0},{1,9},{9,1},{2,10},{10,2},{3,11},{11,3},{4,12},{12,4},... | collective-permute-start | bytes 16515080 | tf_op jit(solution)/shard_map/ppermute | solution.py:599
  238.8 0.8 copy.148
  239.6 0.8 copy.150
  241.0 0.7 multiply_reduce_fusion.1
  243.5 2.1 copy.140.pos_ref
  247.8 47.2 %all-reduce.5.cloned.1.call-done = f32[768,32]{1,0:T(8,128)} async-done(((f32[768,32]{1,0:T(8,128)}), f32[768,32]{1,0:T(8,128)}) %all-reduce.5.cloned.1.call-update) | async-done | bytes 98320 | tf_op jit(solution)/shard_map/psum | solution.py:631
  295.0 1.8 copy.152
  296.8 6.1 %all-to-all-start.5 = ((bf16[8,224,1536]{2,1,0:T(8,128)(2,1)}), bf16[8,224,1536]{2,1,0:T(8,128)(2,1)}, u32[]{:S(2)}, u32[]{:S(2)}) async-start(bf16[8,224,1536]{2,1,0:T(8,128)(2,1)} %bitcast.279), calls=%async_computation.5 | async-start | bytes 11010048 | tf_op jit(solution)/shard_map/all_to_all | solution.py:625
  302.9 33.2 %collective-permute-done.2 = bf16[8,224,1536]{2,1,0:T(8,128)(2,1)} collective-permute-done((bf16[8,224,1536]{2,1,0:T(8,128)(2,1)}, bf16[8,224,1536]{2,1,0:T(8,128)(2,1)}, u32[]{:S(2)}, u32[]{:S(2)}) %collective-permute-start.2) | collective-permute-done | bytes 5505056 | tf_op jit(solution)/shard_map/ppermute | solution.py:599
  336.1 70.2 %all-gather.7.cloned.1.call-done.over_hbm = bf16[400,8,1536]{2,1,0:T(8,128)(2,1)} async-done(((bf16[50,8,1536]{2,1,0:T(8,128)(2,1)}), bf16[400,8,1536]{2,1,0:T(8,128)(2,1)}) %all-gather.7.cloned.1.call-update) | async-done | bytes 9830416 | tf_op jit(solution)/shard_map/all_gather | solution.py:601
  406.2 139.8 %grad_pass.1 = (f32[4,768,3072]{2,1,0:T(8,128)}, f32[4,3072,768]{2,1,0:T(8,128)}) custom-call(s32[7,24]{1,0:T(8,128)} %stack.11.tab_ref, s32[208]{0:T(256)} %reshape.1013.ids_ref, s32[1]{0:T(128)} %bitcast.63.first_ref, bf16[8,4,56,1536]{3,2,1,0:T(8,128)(2,1)} %bitcast.66.rows_ref.xb_ref, bf16[1792,768]{1,0:T(8,128)(2,1)} %get-tuple-element.205.dyb_ref, ...), custom_call_target="tpu_custom_call" | custom-call | flops 70000001024 | bytes 150000000 | tf_op jit(solution)/shard_map/grad_pass/pallas_call | solution.py:420
  546.1 20.5 %unpermute.1 = (bf16[2048,768]{1,0:T(8,128)(2,1)}, bf16[2048,768]{1,0:T(8,128)(2,1)}) custom-call(s32[2048,1]{1,0:T(8,128)} %copy.140.pos_ref, bf16[1792,1536]{1,0:T(8,128)(2,1)} %bitcast.68.base_ref, bf16[400,1536]{1,0:T(8,128)(2,1)} %bitcast.303), custom_call_target="tpu_custom_call" | custom-call | flops 11274289152 | bytes 16000000 | tf_op jit(solution)/shard_map/unpermute/pallas_call | solution.py:98
  566.6 1.3 while.34
  567.8 1.5 copy.207
  (128 shorter events, 19.5 us)
Async XLA Ops:
  7.2 175.5 %all-gather.5.cloned.1.call-start = ((), (), s32[]{:S(2)}) async-start(), calls=%async_computation.8 | async-start | bytes 11059200 | tf_op jit(solution)/shard_map/all_gather | solution.py:598
  9.6 43.1 %copy-start.22 = (s32[16,128]{1,0:T(8,128)}, s32[16,128]{1,0:T(8,128)S(1)}, u32[]{:S(2)}) copy-start(s32[16,128]{1,0:T(8,128)S(1)} %convert_element_type.168) | copy-start | bytes 24580
  16.8 196.2 %collective-permute-start.3 = (bf16[50,8,1536]{2,1,0:T(8,128)(2,1)}, bf16[50,8,1536]{2,1,0:T(8,128)(2,1)}, u32[]{:S(2)}, u32[]{:S(2)}) collective-permute-start(bf16[50,8,1536]{2,1,0:T(8,128)(2,1)} %bitcast.284), channel_id=1, source_target_pairs={{0,8},{8,0},{1,9},{9,1},{2,10},{10,2},{3,11},{11,3},{4,12},{12,4},... | collective-permute-start | bytes 3686408 | tf_op jit(solution)/shard_map/ppermute | solution.py:600
  52.7 31.0 %copy-start.11 = (bf16[768,32]{0,1:T(8,128)(2,1)S(1)}, bf16[768,32]{0,1:T(8,128)(2,1)}, u32[]{:S(2)}) copy-start(bf16[768,32]{0,1:T(8,128)(2,1)} %param.13) | copy-start | bytes 147460
  69.2 64.4 %all-to-all-start.4 = ((bf16[8,224,1536]{2,1,0:T(8,128)(2,1)}), bf16[8,224,1536]{2,1,0:T(8,128)(2,1)}, u32[]{:S(2)}, u32[]{:S(2)}) async-start(bf16[8,224,1536]{2,1,0:T(8,128)(2,1)} %bitcast.280), calls=%async_computation.4 | async-start | bytes 11010048 | tf_op jit(solution)/shard_map/all_to_all | solution.py:595
  74.0 221.0 %all-reduce.5.cloned.1.call-start = ((), (), s32[]{:S(2)}) async-start(), calls=%async_computation.10 | async-start | bytes 786432 | tf_op jit(solution)/shard_map/psum | solution.py:631
  77.2 0.6 copy-start.29
  77.8 1.6 copy-start.28
  78.0 6.6 %copy-start.26 = (s32[4,1]{0,1:T(1,128)}, s32[4,1]{0,1:T(1,128)S(1)}, u32[]{:S(2)}) copy-start(s32[4,1]{0,1:T(1,128)S(1)} %reduce-window.36) | copy-start | bytes 52
  78.6 6.0 %copy-start.24 = (s32[4]{0:T(128)}, s32[4]{0:T(128)S(1)}, u32[]{:S(2)}) copy-start(s32[4]{0:T(128)S(1)} %get-tuple-element.448) | copy-start | bytes 52
  79.3 0.6 copy-start.23
  82.2 2.4 copy-start.27
  82.2 0.8 copy-start.25
  213.0 193.3 %all-gather.7.cloned.1.call-start = ((), (), s32[]{:S(2)}) async-start(), calls=%async_computation.11 | async-start | bytes 11059200 | tf_op jit(solution)/shard_map/all_gather | solution.py:601
  213.7 332.3 %reduce-scatter.2.cloned.1.call-start = ((), (), s32[]{:S(2)}) async-start(), calls=%async_computation.9 | async-start | bytes 11059200 | tf_op jit(solution)/shard_map/reduce_scatter | solution.py:628
  214.3 121.8 %collective-permute-start.2 = (bf16[8,224,1536]{2,1,0:T(8,128)(2,1)}, bf16[8,224,1536]{2,1,0:T(8,128)(2,1)}, u32[]{:S(2)}, u32[]{:S(2)}) collective-permute-start(bf16[8,224,1536]{2,1,0:T(8,128)(2,1)} %all-to-all-done.4), channel_id=1, source_target_pairs={{0,8},{8,0},{1,9},{9,1},{2,10},{10,2},{3,11},{11,3},{4,12},{12,4},... | collective-permute-start | bytes 16515080 | tf_op jit(solution)/shard_map/ppermute | solution.py:599
  296.8 249.2 %all-to-all-start.5 = ((bf16[8,224,1536]{2,1,0:T(8,128)(2,1)}), bf16[8,224,1536]{2,1,0:T(8,128)(2,1)}, u32[]{:S(2)}, u32[]{:S(2)}) async-start(bf16[8,224,1536]{2,1,0:T(8,128)(2,1)} %bitcast.279), calls=%async_computation.5 | async-start | bytes 11010048 | tf_op jit(solution)/shard_map/all_to_all | solution.py:625
  546.1 20.5 %copy-start.2 = (bf16[2048,768]{1,0:T(8,128)(2,1)S(1)}, bf16[2048,768]{1,0:T(8,128)(2,1)}, u32[]{:S(2)}) copy-start(bf16[2048,768]{1,0:T(8,128)(2,1)} %x_ref.3) | copy-start | bytes 9437188
  546.1 20.5 %copy-start.8 = (s32[2048]{0:T(1024)S(1)}, s32[2048]{0:T(1024)}, u32[]{:S(2)}) copy-start(s32[2048]{0:T(1024)} %param.12) | copy-start | bytes 24580
  546.1 20.5 %copy-start.12 = (bf16[768,32]{0,1:T(8,128)(2,1)S(1)}, bf16[768,32]{0,1:T(8,128)(2,1)}, u32[]{:S(2)}) copy-start(bf16[768,32]{0,1:T(8,128)(2,1)} %param.13) | copy-start | bytes 147460
Sparse Core Ops, SparseCore 0:
  16.9 57.9 all-gather.4
  213.1 81.8 all-reduce.4
  296.8 109.3 all-gather.6
  409.6 72.6 reduce-scatter.1

commit v2 on v1

v2 whole, which is shorter than its diff:
```python
import functools

import jax
import jax.numpy as jnp
from jax import lax
from jax.experimental import pallas as pl
from jax.experimental.pallas import tpu as pltpu
from jax.sharding import PartitionSpec as P


PAD_FACTOR = 4
GROUP = 8
BASE_GROUPS = 7
OVER_GROUPS = 50
SENT_GROUPS = OVER_GROUPS + 1
MAX_OVER_TILES = 8
TILE_GROUPS = 26
TILE = TILE_GROUPS * GROUP
PERM_TILE = 256
CHUNK = 512
ROW_CHUNK = 256
CHUNKS = 2
SQRT_2_PI = 0.7978845608028654
CUBIC = 0.044715
VMEM_BYTES = 67_043_328

F32 = jnp.float32
BF16 = jnp.bfloat16
I32 = jnp.int32


def dot(a, b, dims=((1,), (0,))):
    return lax.dot_general(a, b, (dims, ((), ())), preferred_element_type=F32)


def exclusive_cumsum(v, axis):
    return jnp.cumsum(v, axis=axis) - v


def token_positions(idx, n_experts, local):
    tok_count = idx.shape[0]
    block = 128
    base_rows = BASE_GROUPS * GROUP
    onehot = (idx[:, None] == jnp.arange(n_experts, dtype=I32)[None, :]).astype(BF16)
    blocks = onehot.reshape(tok_count // block, block, n_experts)
    lower = jnp.tril(jnp.ones((block, block), BF16))
    inclusive = jnp.einsum('ij,bje->bie', lower, blocks, preferred_element_type=F32)
    totals = jnp.sum(blocks.astype(F32), axis=1)
    counts = jnp.sum(totals, axis=0).astype(I32)
    groups = (counts + GROUP - 1) // GROUP
    over = jnp.maximum(groups - BASE_GROUPS, 0)
    over_start = exclusive_cumsum(over, 0)
    rank = inclusive + (exclusive_cumsum(totals, 0) - 1.0)[:, None, :]
    expert = jnp.arange(n_experts, dtype=I32)
    per_chunk = local // CHUNKS
    slot = (expert % local // per_chunk) * (n_experts // CHUNKS) + expert // local * per_chunk + expert % per_chunk
    base_at = (slot * base_rows).astype(F32)
    over_at = (n_experts * base_rows - base_rows + over_start * GROUP).astype(F32)
    row = jnp.sum(blocks.astype(F32) * (rank + jnp.where(rank < base_rows, base_at, over_at)), axis=2)
    return groups, row.reshape(tok_count).astype(I32)


def permute_kernel(pos_ref, x_ref, gy_ref, *refs):
    *tail, out_ref = refs
    d_model = x_ref.shape[1]
    rows = out_ref.shape[0] - sum(t.shape[0] for t in tail)
    row_id = pl.program_id(0) * rows + lax.broadcasted_iota(I32, (rows, x_ref.shape[0]), 0)
    select = jnp.where(row_id == pos_ref[...], 1.0, 0.0).astype(BF16)
    out_ref[:rows, :d_model] = dot(select, x_ref[...]).astype(BF16)
    out_ref[:rows, d_model:] = dot(select, gy_ref[...]).astype(BF16)
    for t in tail:
        out_ref[rows:, :] = t[...]


def permute_rows(pos, x, gy, first_row, n_rows, *tail):
    tok_count, d_model = x.shape
    tile = n_rows if n_rows % PERM_TILE else PERM_TILE
    extra = sum(t.shape[0] for t in tail)
    return pl.pallas_call(
        permute_kernel,
        grid=(n_rows // tile,),
        in_specs=[
            pl.BlockSpec((1, tok_count), lambda i: (0, 0)),
            pl.BlockSpec((tok_count, d_model), lambda i: (0, 0)),
            pl.BlockSpec((tok_count, d_model), lambda i: (0, 0)),
        ] + [pl.BlockSpec(t.shape, lambda i: (0, 0)) for t in tail],
        out_specs=pl.BlockSpec((tile + extra, 2 * d_model), lambda i: (i, 0)),
        out_shape=jax.ShapeDtypeStruct((n_rows + extra, 2 * d_model), BF16),
        cost_estimate=pl.CostEstimate(flops=4 * n_rows * tok_count * d_model, bytes_accessed=16_000_000, transcendentals=0),
        name='permute',
    )((pos - first_row).reshape(1, tok_count), x, gy, *tail)


def unpermute_kernel(pos_ref, *refs):
    *parts, out_ref, dx_ref = refs
    toks, d_model = out_ref.shape
    first, out, dx = 0, 0.0, 0.0
    for part in parts:
        rows = part[...].reshape(-1, 2 * d_model)
        row_id = lax.broadcasted_iota(I32, (toks, rows.shape[0]), 1) + first
        select = jnp.where(row_id == pos_ref[...], 1.0, 0.0).astype(BF16)
        out += dot(select, rows[:, :d_model])
        dx += dot(select, rows[:, d_model:])
        first += rows.shape[0]
    out_ref[...] = out.astype(BF16)
    dx_ref[...] = dx.astype(BF16)


def unpermute_rows(pos, base, over):
    n_own, n_slot, width = base.shape
    tok_count = pos.shape[0]
    d_model = width // 2
    shape = jax.ShapeDtypeStruct((tok_count, d_model), BF16)
    chunk = (n_own, n_slot // CHUNKS, width)
    return pl.pallas_call(
        unpermute_kernel,
        grid=(tok_count // PERM_TILE,),
        in_specs=[pl.BlockSpec((PERM_TILE, 1), lambda i: (i, 0))]
        + [pl.BlockSpec(chunk, lambda i, c=c: (0, c, 0)) for c in range(CHUNKS)]
        + [pl.BlockSpec(over.shape, lambda i: (0, 0))],
        out_specs=[pl.BlockSpec((PERM_TILE, d_model), lambda i: (i, 0))] * 2,
        out_shape=[shape, shape],
        cost_estimate=pl.CostEstimate(flops=14_000_000_000, bytes_accessed=16_000_000, transcendentals=0),
        name='unpermute',
    )(pos.reshape(tok_count, 1), *[base] * CHUNKS, over)


def gate(x, wg, expert):
    logit = dot(x, wg)
    unnorm = jnp.exp(logit - jnp.max(logit, axis=1, keepdims=True))
    prob = unnorm / jnp.sum(unnorm, axis=1, keepdims=True)
    onehot = lax.broadcasted_iota(I32, prob.shape, 1) == expert
    gate_val = prob.shape[1] * jnp.sum(jnp.where(onehot, prob, 0.0), axis=1, keepdims=True)
    return prob, onehot, gate_val


def activations(x, dy, w_up, w_down, cols):
    a = dot(x, w_up[:, cols])
    dh = dot(dy, w_down[cols, :], ((1,), (1,)))
    cubic = (SQRT_2_PI * CUBIC) * (a * a)
    half = 0.5 + 0.5 * jnp.tanh(a * (SQRT_2_PI + cubic))
    h = a * half
    slope = half + (h - h * half) * (2.0 * SQRT_2_PI + 6.0 * cubic)
    return h.astype(BF16), (slope * dh).astype(BF16)


def own_rows_step(x, gy, expert, wg_ref, w_up, w_down, store, dwg_ref):
    dy_ref, h_ref, da_ref = store
    prob, onehot, gate_val = gate(x, wg_ref[...], expert)
    gy_full = gy.astype(F32)
    dy = (gate_val * gy_full).astype(BF16)
    dy_ref[...] = dy
    for lo in range(0, h_ref.shape[1], ROW_CHUNK):
        cols = pl.ds(lo, ROW_CHUNK)
        h, da = activations(x, dy, w_up, w_down, cols)
        h_ref[:, cols] = h
        da_ref[:, cols] = da
    y = dot(h_ref[...], w_down[...]).astype(BF16).astype(F32)
    dxe = dot(da_ref[...], w_up[...], ((1,), (1,))).astype(BF16).astype(F32)
    d_gate = jnp.sum(gy_full * y, axis=1, keepdims=True)
    d_logit = ((d_gate * gate_val) * (onehot.astype(F32) - prob)).astype(BF16)
    dwg_ref[...] += dot(d_logit, x, ((0,), (0,)))
    out = (gate_val * y).astype(BF16)
    dx = (dxe + dot(d_logit, wg_ref[...], ((1,), (1,)))).astype(BF16)
    return out, dx


def own_base_kernel(first_ref, rows_ref, wg_ref, up_ref, down_ref, dwg_in, *refs):
    od_ref, x_ref, dy_ref, h_ref, da_ref, dwg_ref, zero_ref = refs[-7:]
    step = pl.program_id(0)
    d_model = wg_ref.shape[0]

    @pl.when(step == 0)
    def _():
        dwg_ref[...] = dwg_in[...]

    zero_ref[...] = jnp.zeros_like(zero_ref)
    rows = rows_ref[...].reshape(dy_ref.shape[0], 2 * d_model)
    x = rows[:, :d_model]
    x_ref[...] = x
    out, dx = own_rows_step(x, rows[:, d_model:], first_ref[0] + step, wg_ref, up_ref.at[0], down_ref.at[0],
                            (dy_ref, h_ref, da_ref), dwg_ref)
    block = od_ref.shape[:3] + (d_model,)
    od_ref[:, :, :, :d_model] = out.reshape(block)
    od_ref[:, :, :, d_model:] = dx.reshape(block)


def own_base_pass(first_expert, chunk, rows, wg, w_up, w_down, dwg, stores, over_shape):
    n_src, count, seg, width = rows.shape
    local, d_model, d_ff = w_up.shape
    tile = n_src * seg
    lead = chunk * count
    row_spec = lambda at: pl.BlockSpec((n_src, 1, seg, width), lambda e, first: (0, at + e, 0, 0))
    store_spec = lambda cols: pl.BlockSpec((tile, cols), lambda e, first: (lead + e, 0))
    const = lambda e, first: (0, 0)
    rows_of = lambda cols: jax.ShapeDtypeStruct((local * tile, cols), BF16)
    zero_block = (over_shape[0] // local,) + over_shape[1:]
    kept = [] if stores is None else list(stores)
    return pl.pallas_call(
        own_base_kernel,
        grid_spec=pltpu.PrefetchScalarGridSpec(
            num_scalar_prefetch=1,
            grid=(count,),
            in_specs=[
                row_spec(0),
                pl.BlockSpec(wg.shape, const),
                pl.BlockSpec((1, d_model, d_ff), lambda e, first: (lead + e, 0, 0)),
                pl.BlockSpec((1, d_ff, d_model), lambda e, first: (lead + e, 0, 0)),
                pl.BlockSpec(dwg.shape, const),
            ] + [pl.BlockSpec(memory_space=pl.ANY)] * len(kept),
            out_specs=[row_spec(lead), store_spec(d_model), store_spec(d_model), store_spec(d_ff), store_spec(d_ff),
                       pl.BlockSpec(dwg.shape, const), pl.BlockSpec(zero_block, lambda e, first: (lead + e, 0, 0))],
        ),
        out_shape=[jax.ShapeDtypeStruct((n_src, local, seg, width), BF16), rows_of(d_model), rows_of(d_model), rows_of(d_ff), rows_of(d_ff),
                   jax.ShapeDtypeStruct(dwg.shape, F32), jax.ShapeDtypeStruct(over_shape, BF16)],
        input_output_aliases={6 + i: o for i, o in zip(range(len(kept)), (0, 1, 2, 3, 4, 6))},
        compiler_params=pltpu.CompilerParams(vmem_limit_bytes=VMEM_BYTES, dimension_semantics=('arbitrary',)),
        cost_estimate=pl.CostEstimate(flops=8_500_000_000 * count, bytes_accessed=20_000_000 * count,
                                      transcendentals=1_500_000 * count),
        name='own_base',
    )(first_expert + lead, rows, wg, w_up, w_down, dwg, *kept)


def group_copies(ids_ref, slot_base, count, hbm, buf, sem, to_hbm):
    def body(g, carry):
        gid = ids_ref[slot_base + g]
        ends = (buf.at[g], hbm.at[gid]) if to_hbm else (hbm.at[gid], buf.at[g])
        pltpu.make_async_copy(*ends, sem).start()
        return carry

    lax.fori_loop(0, count, body, 0)


def group_waits(count, hbm, buf, sem, to_hbm):
    def body(g, carry):
        ends = (buf.at[0], hbm.at[0]) if to_hbm else (hbm.at[0], buf.at[0])
        pltpu.make_async_copy(*ends, sem).wait()
        return carry

    lax.fori_loop(0, count, body, 0)


def tile_rows(buf, count):
    rows = buf[...].reshape(TILE, buf.shape[-1])
    row_id = lax.broadcasted_iota(I32, rows.shape, 0)
    return jnp.where(row_id < count * GROUP, rows, jnp.zeros((), rows.dtype))


def own_over_kernel(tab_ref, ids_ref, back_ids_ref, first_ref, rows_hbm, wg_ref, up_ref, down_ref, dwg_in, zero_od,
                    od_hbm, x_ref, dy_ref, h_ref, da_ref, dwg_ref, in_buf, out_buf, in_sem, out_sem):
    del zero_od
    step = pl.program_id(0)
    d_model = wg_ref.shape[0]
    slot = step % 2
    count = tab_ref[1, step]

    @pl.when(step == 0)
    def _():
        dwg_ref[...] = dwg_in[...]
        group_copies(ids_ref, 0, count, rows_hbm, in_buf.at[0], in_sem.at[0], False)

    @pl.when(count > 0)
    def _():
        group_waits(count, rows_hbm, in_buf.at[slot], in_sem.at[slot], False)

        @pl.when(step + 1 < pl.num_programs(0))
        def _():
            group_copies(ids_ref, (step + 1) * TILE_GROUPS, tab_ref[1, step + 1], rows_hbm, in_buf.at[1 - slot],
                         in_sem.at[1 - slot], False)

        rows = tile_rows(in_buf.at[slot], count)
        x = rows[:, :d_model]
        x_ref[...] = x
        out, dx = own_rows_step(x, rows[:, d_model:], first_ref[0] + tab_ref[0, step], wg_ref,
                                up_ref.at[0], down_ref.at[0], (dy_ref, h_ref, da_ref), dwg_ref)

        @pl.when(step > 0)
        def _():
            group_waits(tab_ref[1, step - 1], od_hbm, out_buf, out_sem, True)

        out_buf[:, :, :d_model] = out.reshape(TILE_GROUPS, GROUP, d_model)
        out_buf[:, :, d_model:] = dx.reshape(TILE_GROUPS, GROUP, d_model)
        group_copies(back_ids_ref, step * TILE_GROUPS, count, od_hbm, out_buf, out_sem, True)

        @pl.when(tab_ref[3, step] == 1)
        def _():
            group_waits(count, od_hbm, out_buf, out_sem, True)


def own_over_pass(table, ids, back_ids, first_expert, rows, wg, w_up, w_down, dwg, zero_od):
    d_model, d_ff = w_up.shape[1], w_up.shape[2]
    width = rows.shape[-1]
    n_tiles = table.shape[1]
    hbm = pl.BlockSpec(memory_space=pl.ANY)
    const = lambda i, tab, ids, back, first: (0, 0)
    store_spec = lambda cols: pl.BlockSpec((TILE, cols), lambda i, tab, ids, back, first: (tab[2, i], 0))
    rows_of = lambda cols: jax.ShapeDtypeStruct((n_tiles * TILE, cols), BF16)
    return pl.pallas_call(
        own_over_kernel,
        grid_spec=pltpu.PrefetchScalarGridSpec(
            num_scalar_prefetch=4,
            grid=(n_tiles,),
            in_specs=[
                hbm,
                pl.BlockSpec(wg.shape, const),
                pl.BlockSpec((1, d_model, d_ff), lambda i, tab, ids, back, first: (tab[0, i], 0, 0)),
                pl.BlockSpec((1, d_ff, d_model), lambda i, tab, ids, back, first: (tab[0, i], 0, 0)),
                pl.BlockSpec(dwg.shape, const),
                hbm,
            ],
            out_specs=[hbm, store_spec(d_model), store_spec(d_model), store_spec(d_ff), store_spec(d_ff),
                       pl.BlockSpec(dwg.shape, const)],
            scratch_shapes=[
                pltpu.VMEM((2, TILE_GROUPS, GROUP, width), BF16),
                pltpu.VMEM((TILE_GROUPS, GROUP, width), BF16),
                pltpu.SemaphoreType.DMA((2,)),
                pltpu.SemaphoreType.DMA,
            ],
        ),
        out_shape=[jax.ShapeDtypeStruct(zero_od.shape, BF16), rows_of(d_model), rows_of(d_model), rows_of(d_ff),
                   rows_of(d_ff), jax.ShapeDtypeStruct(dwg.shape, F32)],
        input_output_aliases={9: 0},
        compiler_params=pltpu.CompilerParams(vmem_limit_bytes=VMEM_BYTES, dimension_semantics=('arbitrary',)),
        cost_estimate=pl.CostEstimate(flops=10_000_000_000, bytes_accessed=40_000_000, transcendentals=2_000_000),
        name='own_over',
    )(table, ids, back_ids, first_expert, rows, wg, w_up, w_down, dwg, zero_od)


OWN_BASE, OWN_OVER, OTHER_BASE, OTHER_OVER = range(4)


def grad_kernel(tab_ref, ids_ref, first_ref, xb_ref, dyb_ref, hb_ref, dab_ref, xo_ref, dyo_ref, ho_ref, dao_ref, *refs):
    *base_hbm, over_hbm, wg_ref, up_hbm, down_hbm, dup_hbm, ddown_hbm = refs[:-12]
    dup, ddown, up_buf, down_buf, h_buf, da_buf, base_buf, in_buf, w_sems, base_sem, in_sem, out_sems = refs[-12:]
    step = pl.program_id(0)
    d_model, d_ff = dup.shape
    expert, kind, last, count = tab_ref[0, step], tab_ref[1, step], tab_ref[2, step], tab_ref[4, step]
    n_local = dup_hbm.shape[0]
    base_rows = h_buf.shape[0]

    def weights(e):
        return (pltpu.make_async_copy(up_hbm.at[e], up_buf, w_sems.at[0]),
                pltpu.make_async_copy(down_hbm.at[e], down_buf, w_sems.at[1]))

    def flush_down(e):
        return pltpu.make_async_copy(ddown, ddown_hbm.at[e], out_sems.at[0])

    def flush_up(e):
        return pltpu.make_async_copy(dup, dup_hbm.at[e], out_sems.at[1])

    def add_down(dy, h_src, add):
        for lo in range(0, d_ff, CHUNK):
            cols = pl.ds(lo, CHUNK)
            term = dot(h_src[:, cols], dy, ((0,), (0,)))
            ddown[cols, :] = ddown[cols, :] + term if add else term

    def add_up(x, da_src, add):
        for lo in range(0, d_ff, CHUNK):
            cols = pl.ds(lo, CHUNK)
            term = dot(x, da_src[:, cols], ((0,), (0,)))
            dup[:, cols] = dup[:, cols] + term if add else term

    def accumulate(x, dy, h_src, da_src):
        add_down(dy, h_src, True)

        @pl.when(last == 1)
        def _():
            flush_down(expert).start()

        add_up(x, da_src, True)

        @pl.when(last == 1)
        def _():
            flush_up(expert).start()

            @pl.when(expert + 1 < n_local)
            def _():
                for copy in weights(expert + 1):
                    copy.start()

            @pl.when(expert + 1 == n_local)
            def _():
                flush_down(expert).wait()
                flush_up(expert).wait()

    def base_copy(e):
        chunk = base_hbm[e // base_hbm[0].shape[1]]
        return pltpu.make_async_copy(chunk.at[:, e % chunk.shape[1]], base_buf, base_sem)

    @pl.when(kind == OWN_BASE)
    def _():
        for e in range(n_local):
            @pl.when(expert == e)
            def _():
                base_copy(e).start()

        @pl.when(expert == 0)
        def _():
            for copy in weights(0):
                copy.start()

        @pl.when(expert > 0)
        def _():
            flush_down(expert - 1).wait()

        add_down(dyb_ref[...], hb_ref, False)

        @pl.when(expert > 0)
        def _():
            flush_up(expert - 1).wait()

        add_up(xb_ref[...], dab_ref, False)

    @pl.when(kind == OWN_OVER)
    def _():
        add_down(dyo_ref[...], ho_ref, True)
        add_up(xo_ref[...], dao_ref, True)

    def other_rows(rows, n_rows):
        x, gy = rows[:, :d_model], rows[:, d_model:]
        _, _, gate_val = gate(x, wg_ref[...], first_ref[0] + expert)
        dy = (gate_val * gy.astype(F32)).astype(BF16)
        h_dst, da_dst = h_buf.at[:n_rows], da_buf.at[:n_rows]
        for lo in range(0, d_ff, ROW_CHUNK):
            cols = pl.ds(lo, ROW_CHUNK)
            h, da = activations(x, dy, up_buf, down_buf, cols)
            h_dst[:, cols] = h
            da_dst[:, cols] = da
        accumulate(x, dy, h_dst, da_dst)

    @pl.when(kind == OTHER_BASE)
    def _():
        for copy in weights(expert):
            copy.wait()
        base_copy(0).wait()
        other_rows(base_buf[...].reshape(base_rows, 2 * d_model), base_rows)

    @pl.when(kind == OTHER_OVER)
    def _():
        group_copies(ids_ref, tab_ref[5, step] * TILE_GROUPS, count, over_hbm, in_buf, in_sem, False)
        group_waits(count, over_hbm, in_buf, in_sem, False)
        other_rows(tile_rows(in_buf, count), TILE)


def grad_pass(table, ids, first_expert, base_store, over_store, base, over, wg, w_up, w_down):
    n_src, _, seg, width = base[0].shape
    d_model, d_ff = w_up.shape[1], w_up.shape[2]
    base_rows = n_src * seg
    base_spec = lambda cols: pl.BlockSpec((base_rows, cols), lambda i, tab, ids, first: (tab[6, i], 0))
    over_spec = lambda cols: pl.BlockSpec((TILE, cols), lambda i, tab, ids, first: (tab[3, i], 0))
    hbm = pl.BlockSpec(memory_space=pl.ANY)
    return pl.pallas_call(
        grad_kernel,
        grid_spec=pltpu.PrefetchScalarGridSpec(
            num_scalar_prefetch=3,
            grid=(table.shape[1],),
            in_specs=[
                base_spec(d_model),
                base_spec(d_model),
                base_spec(d_ff),
                base_spec(d_ff),
                over_spec(d_model),
                over_spec(d_model),
                over_spec(d_ff),
                over_spec(d_ff),
                *[hbm for _ in base],
                hbm,
                pl.BlockSpec(wg.shape, lambda i, tab, ids, first: (0, 0)),
                hbm,
                hbm,
            ],
            out_specs=[hbm, hbm],
            scratch_shapes=[
                pltpu.VMEM((d_model, d_ff), F32),
                pltpu.VMEM((d_ff, d_model), F32),
                pltpu.VMEM((d_model, d_ff), BF16),
                pltpu.VMEM((d_ff, d_model), BF16),
                pltpu.VMEM((base_rows, d_ff), BF16),
                pltpu.VMEM((base_rows, d_ff), BF16),
                pltpu.VMEM((n_src, seg, width), BF16),
                pltpu.VMEM((TILE_GROUPS, GROUP, width), BF16),
                pltpu.SemaphoreType.DMA((2,)),
                pltpu.SemaphoreType.DMA,
                pltpu.SemaphoreType.DMA,
                pltpu.SemaphoreType.DMA((2,)),
            ],
        ),
        out_shape=[jax.ShapeDtypeStruct(w_up.shape, F32), jax.ShapeDtypeStruct(w_down.shape, F32)],
        compiler_params=pltpu.CompilerParams(vmem_limit_bytes=VMEM_BYTES, dimension_semantics=('arbitrary',)),
        cost_estimate=pl.CostEstimate(flops=70_000_000_000, bytes_accessed=150_000_000, transcendentals=8_000_000),
        name='grad_pass',
    )(table, ids, first_expert, *base_store, *over_store, *base, over, wg, w_up, w_down)


def overflow_spans(count_ref, local):
    groups = jnp.sum(count_ref[...].astype(F32), axis=(1, 2))
    over = jnp.maximum(groups - BASE_GROUPS, 0.0)
    lanes = over.shape[1]
    row, col = (lax.broadcasted_iota(I32, (lanes, lanes), d) for d in (0, 1))
    start = dot(over.astype(BF16), jnp.where(row < col, 1.0, 0.0).astype(BF16))
    tiles = jnp.ceil(jnp.sum(over, axis=0, keepdims=True) * (1.0 / TILE_GROUPS) - 1e-3)
    owner = dot(jnp.broadcast_to(tiles, over.shape).astype(BF16), jnp.where(row // local == col, 1.0, 0.0).astype(BF16))
    excess = jnp.max(jnp.maximum(start + over - OVER_GROUPS, owner - MAX_OVER_TILES))
    first = jnp.minimum(start, OVER_GROUPS)
    size = jnp.minimum(start + over, OVER_GROUPS) - first
    return size.astype(I32), first.astype(I32), excess


def fill_tiles(n_src, local, lead, size, first, write):
    firsts, tile = [], jnp.int32(0)
    for e in range(local):
        base = tile * TILE_GROUPS

        def per_source(s, at, e=e, base=base):
            begin = first[s, lead + e]

            def per_group(g, at):
                @pl.when(base + at < MAX_OVER_TILES * TILE_GROUPS)
                def _():
                    write(base + at, s, begin + g)

                return at + 1

            return lax.fori_loop(0, size[s, lead + e], per_group, at)

        total = lax.fori_loop(0, n_src, per_source, jnp.int32(0))
        tiles = jnp.minimum(lax.div(total + (TILE_GROUPS - 1), jnp.int32(TILE_GROUPS)), MAX_OVER_TILES - tile)
        firsts.append((tile, tiles, total))
        tile = tile + tiles
    return firsts, tile


def to_scalars(pairs, sems):
    copies = [pltpu.make_async_copy(v, m, sems.at[i]) for i, (v, m) in enumerate(pairs)]
    for copy in copies:
        copy.start()
    for copy in copies:
        copy.wait()


def own_plan_kernel(local, lead_ref, count_ref, tab_ref, ids_ref, back_ref, size_v, first_v, size_s, first_s, sems):
    size_v[...], first_v[...], _ = overflow_spans(count_ref, local)
    to_scalars([(size_v, size_s), (first_v, first_s)], sems)

    def write(at, s, g):
        ids_ref[at] = s * SENT_GROUPS + g
        back_ref[at] = s * OVER_GROUPS + g

    spans, n_tiles = fill_tiles(count_ref.shape[0], local, lead_ref[0], size_s, first_s, write)
    last = jnp.maximum(n_tiles - 1, 0)
    for t in range(MAX_OVER_TILES):
        tab_ref[0, t] = local - 1
        tab_ref[1, t] = 0
        tab_ref[2, t] = jnp.minimum(t, last)
        tab_ref[3, t] = (last == t).astype(I32)
    for e, (tile, tiles, total) in enumerate(spans):
        def body(k, left, e=e, tile=tile):
            tab_ref[0, tile + k] = e
            tab_ref[1, tile + k] = jnp.minimum(left, TILE_GROUPS)
            return left - TILE_GROUPS

        lax.fori_loop(0, tiles, body, total)


def grad_plan_kernel(local, lead_ref, own_ref, other_ref, tab_ref, ids_ref, fits_ref, size_v, first_v, size_s, first_s, sems):
    n_src = own_ref.shape[0]
    size_v[0], first_v[0], own_excess = overflow_spans(own_ref, local)
    size_v[1], first_v[1], other_excess = overflow_spans(other_ref, local)
    to_scalars([(size_v, size_s), (first_v, first_s)], sems)
    fits_ref[0] = (jnp.maximum(own_excess, other_excess) <= 0.0).astype(I32)

    def write(at, s, g):
        ids_ref[at] = s * SENT_GROUPS + g

    own, _ = fill_tiles(n_src, local, lead_ref[0], size_s.at[0], first_s.at[0], lambda at, s, g: None)
    other, _ = fill_tiles(n_src, local, lead_ref[0], size_s.at[1], first_s.at[1], write)
    max_steps = tab_ref.shape[1]
    for t in range(max_steps):
        tab_ref[1, t] = -1
        tab_ref[2, t] = 0
    step = jnp.int32(0)
    own_at = jnp.int32(0)

    def emit(step, expert, kind, own_tile, groups, other_tile, next_base):
        tab_ref[0, step] = expert
        tab_ref[1, step] = kind
        tab_ref[3, step] = jnp.clip(own_tile, 0, MAX_OVER_TILES - 1)
        tab_ref[4, step] = groups
        tab_ref[5, step] = other_tile
        tab_ref[6, step] = next_base

    for e in range(local):
        own_tile, own_tiles, _ = own[e]
        other_tile, other_tiles, total = other[e]
        after = min(e + 1, local - 1)
        emit(step, e, OWN_BASE, own_tile, 0, 0, e)

        def own_body(k, c, e=e, step=step, own_tile=own_tile, after=after):
            emit(step + 1 + k, e, OWN_OVER, own_tile + k, 0, 0, after)
            return c

        lax.fori_loop(0, own_tiles, own_body, 0)
        step = step + 1 + own_tiles
        own_at = own_tile + own_tiles
        emit(step, e, OTHER_BASE, own_at, 0, 0, after)

        def other_body(k, left, e=e, step=step, own_at=own_at, other_tile=other_tile, after=after):
            emit(step + 1 + k, e, OTHER_OVER, own_at, jnp.minimum(left, TILE_GROUPS), other_tile + k, after)
            return left - TILE_GROUPS

        lax.fori_loop(0, other_tiles, other_body, total)
        step = step + 1 + other_tiles
        tab_ref[2, step - 1] = 1

    def rest(t, c):
        emit(t, local - 1, -1, own_at, 0, 0, local - 1)
        return c

    lax.fori_loop(step, max_steps, rest, 0)


def plan_call(kernel, local, lead, counts, out_shapes, planes):
    n_src = counts[0].shape[0]
    smem = pl.BlockSpec(memory_space=pltpu.SMEM)
    spec = pl.BlockSpec((n_src, 1, GROUP, 128), lambda i: (0, OVER_GROUPS, 0, 0))
    shape = (n_src, 128) if planes == 1 else (planes, n_src, 128)
    return pl.pallas_call(
        functools.partial(kernel, local),
        grid=(1,),
        in_specs=[smem] + [spec] * len(counts),
        out_specs=[smem] * len(out_shapes),
        out_shape=[jax.ShapeDtypeStruct(o, I32) for o in out_shapes],
        scratch_shapes=[pltpu.VMEM(shape, I32), pltpu.VMEM(shape, I32), pltpu.SMEM(shape, I32), pltpu.SMEM(shape, I32),
                        pltpu.SemaphoreType.DMA((2,))],
    )(lead, *counts)


def padded_step(x_loc, gy_loc, idx_loc, w_gate, w_up, w_down, ep_size, dp_size):
    tok_count, d_model = x_loc.shape
    n_experts = w_gate.shape[1]
    local_experts = w_up.shape[0]
    cap_rows = PAD_FACTOR * tok_count // n_experts
    onehot = idx_loc[:, None] == jnp.arange(n_experts, dtype=I32)[None, :]
    expert_count = jnp.sum(onehot, axis=0, dtype=I32)
    sort_order = jnp.argsort(idx_loc, stable=True)
    sorted_pos = jnp.argsort(sort_order)
    expert_start = jnp.cumsum(expert_count) - expert_count
    slot_k = jnp.arange(cap_rows, dtype=I32)
    slot_valid = slot_k[None, :] < expert_count[:, None]
    src_tok = sort_order[jnp.minimum(expert_start[:, None] + slot_k[None, :], tok_count - 1)]
    slot_tok = idx_loc * cap_rows + sorted_pos - expert_start[idx_loc]

    def dispatch(tok_rows):
        picked = jnp.where(slot_valid[:, :, None], tok_rows[src_tok], jnp.zeros((), tok_rows.dtype))
        picked = picked.reshape(ep_size, local_experts, cap_rows, d_model)
        return lax.all_to_all(picked, 'ep', 0, 0, tiled=True)

    def combine(expert_rows):
        returned = lax.all_to_all(expert_rows, 'ep', 1, 0, tiled=True)
        return returned.reshape(n_experts * cap_rows, d_model)[slot_tok]

    router_logit = jnp.dot(x_loc, w_gate, preferred_element_type=F32)
    router_prob = jax.nn.softmax(router_logit, axis=-1)
    gate_val = n_experts * jnp.sum(jnp.where(onehot, router_prob, 0.0), axis=1)
    recv_rows = dispatch(x_loc)
    gy_full = gy_loc.astype(F32)
    dy_tok = (gate_val[:, None] * gy_full).astype(BF16)
    recv_grad = dispatch(dy_tok)

    def one_expert(carry, per_expert):
        rows, grad, up, down = per_expert
        rows, grad = rows.reshape(-1, d_model), grad.reshape(-1, d_model)
        pre_act = dot(rows, up)
        hid_full, gelu_back = jax.vjp(jax.nn.gelu, pre_act)
        hidden = hid_full.astype(BF16)
        out_rows = dot(hidden, down).astype(BF16)
        d_pre = gelu_back(dot(grad, down, ((1,), (1,))))[0].astype(BF16)
        grad_down = dot(hidden, grad, ((0,), (0,)))
        grad_up = dot(rows, d_pre, ((0,), (0,)))
        d_rows = dot(d_pre, up, ((1,), (1,))).astype(BF16)
        shape = (ep_size, cap_rows, d_model)
        return carry, (out_rows.reshape(shape), d_rows.reshape(shape), grad_up, grad_down)

    swap = lambda rows: jnp.swapaxes(rows, 0, 1)
    _, (expert_out, d_rows, grad_up, grad_down) = lax.scan(
        one_expert, 0, (swap(recv_rows), swap(recv_grad), w_up, w_down))
    y_tok = combine(expert_out)
    moe_out = (gate_val[:, None] * y_tok.astype(F32)).astype(BF16)
    dx_expert = combine(d_rows)
    d_gate = jnp.sum(gy_full * y_tok.astype(F32), axis=1)
    d_logit = ((d_gate * gate_val)[:, None] * (onehot.astype(F32) - router_prob)).astype(BF16)
    dx_router = dot(d_logit, w_gate, ((1,), (1,)))
    grad_x = (dx_expert.astype(F32) + dx_router).astype(BF16)
    grad_gate = dot(x_loc, d_logit, ((0,), (0,)))

    def sum_dp(term):
        total = term
        for shift in range(1, dp_size):
            total = total + lax.ppermute(term, 'dp', [(i, (i + shift) % dp_size) for i in range(dp_size)])
        return total

    return (moe_out, grad_x, sum_dp(grad_up), sum_dp(grad_down), lax.psum(grad_gate, ('dp', 'ep')))


def solution(mesh):
    dp_size, ep_size = mesh.shape['dp'], mesh.shape['ep']
    tok_spec = P(('dp', 'ep'), None)
    idx_spec = P(('dp', 'ep'))
    rep_spec = P(None, None)
    exp_spec = P('ep', None, None)
    swap = [(i, (i + 1) % dp_size) for i in range(dp_size)]

    def local_step(x, gy, idx, w_gate, w_up, w_down):
        _, d_model = x.shape
        n_experts = w_gate.shape[1]
        local = w_up.shape[0]
        width = 2 * d_model
        base_rows = BASE_GROUPS * GROUP
        n_base = n_experts * base_rows
        n_over = OVER_GROUPS * GROUP
        ep = lax.axis_index('ep')
        first_expert = (ep * local).astype(I32).reshape(1)

        my_groups, pos = token_positions(idx, n_experts, local)
        chunk_rows = n_base // CHUNKS
        slots = (ep_size, local // CHUNKS, base_rows, width)
        base, base_z = [], []
        for c in range(CHUNKS):
            sent = permute_rows(pos, x, gy, c * chunk_rows, chunk_rows)
            base.append(lax.all_to_all(sent.reshape(ep_size, -1, width), 'ep', 0, 0, tiled=True))
            base_z.append(lax.ppermute(base[c], 'dp', swap).reshape(slots))
        marks = jnp.pad(my_groups.astype(BF16)[None, :], ((0, GROUP - 1), (0, width - n_experts)))
        over_sent = permute_rows(pos, x, gy, n_base, n_over, marks).reshape(SENT_GROUPS, GROUP, width)
        over = lax.all_gather(over_sent, 'ep')
        over_sent_z = lax.ppermute(over_sent, 'dp', swap)
        over_z = lax.all_gather(over_sent_z, 'ep')

        n_ids = MAX_OVER_TILES * TILE_GROUPS
        table, ids, back_ids = plan_call(own_plan_kernel, local, first_expert, [over],
                                         [(4, MAX_OVER_TILES), (n_ids,), (n_ids,)], 1)
        gtable, ids_z, fits = plan_call(grad_plan_kernel, local, first_expert, [over, over_z],
                                        [(7, 2 * (local + MAX_OVER_TILES)), (n_ids,), (1,)], 2)
        over_shape = (ep_size * OVER_GROUPS, GROUP, width)
        over = over.reshape(-1, GROUP, width)
        over_z = over_z.reshape(-1, GROUP, width)
        dwg = jnp.zeros((n_experts, d_model), F32)
        stores = None
        for c in range(CHUNKS):
            kept = own_base_pass(first_expert, c, base[c].reshape(slots), w_gate, w_up, w_down, dwg, stores, over_shape)
            dwg = kept[5]
            stores = kept[:5] + kept[6:]
        od, *base_store, zero_od = stores
        base_back = lax.all_to_all(od.reshape(ep_size, -1, width), 'ep', 0, 0, tiled=True)
        od_over, x_o, dy_o, h_o, da_o, dwg = own_over_pass(table, ids, back_ids, first_expert, over, w_gate, w_up, w_down,
                                                          dwg, zero_od)
        over_back = lax.psum_scatter(od_over.reshape(ep_size, OVER_GROUPS, GROUP, width), 'ep', scatter_dimension=0)
        d_up, d_down = grad_pass(gtable, ids_z, first_expert, base_store, (x_o, dy_o, h_o, da_o), base_z, over_z,
                                 w_gate, w_up, w_down)
        d_gate = jnp.sum(lax.all_gather(dwg, ('dp', 'ep')), axis=0).T
        moe_out, grad_x = unpermute_rows(pos, base_back, over_back.reshape(n_over, width))
        sparse = (moe_out, grad_x, d_up, d_down, d_gate)

        def dense(carry):
            del carry
            return (jnp.array(True),) + padded_step(x, gy, idx, w_gate, w_up, w_down, ep_size, dp_size)

        return lax.while_loop(lambda carry: jnp.logical_not(carry[0]), dense, (fits[0] == 1,) + sparse)[1:]

    return jax.shard_map(
        local_step, mesh=mesh, in_specs=(tok_spec, tok_spec, idx_spec, rep_spec, exp_spec, exp_spec),
        out_specs=(tok_spec, tok_spec, exp_spec, exp_spec, rep_spec), check_vma=False)
```

time: 581 us -> 522 us (0.90)
  blocking collectives: 35.6 us -> 0 us
  waiting for transfers between devices: 200 us -> 167 us
  Pallas kernels: 263 us -> 283 us
  local copies, waits for them, and re-layouts: 14.5 us -> 5.76 us
  other arithmetic: 12.7 us -> 4.12 us
    all_gather x2 -> x3, waiting for transfers between devices: 70.2 us -> 0.04 us  [the longest x1 0.02 us: local_step(): d_gate = jnp.sum(lax.all_gather(dwg, ('dp', 'ep')), axis=0).T]
    ppermute x1 -> x2, waiting for transfers between devices: 33.2 us -> 92.8 us  [local_step(): base_z.append(lax.ppermute(base[c], 'dp', swap).reshape(slots))]
    psum x1 -> x0, waiting for transfers between devices: 47.2 us -> none  [local_step(): d_gate = lax.psum(dwg, ('dp', 'ep'))]
    all_gather x1 -> x0, blocking collectives: 35.6 us -> none  [local_step(): lax.all_gather(my_groups, ('dp', 'ep')).reshape(dp_size, ep_size, n_experts)]
    ppermute x1, waiting for transfers between devices: 0.01 us -> 28.7 us  [local_step(): over_sent_z = lax.ppermute(over_sent, 'dp', swap)]
    pallas_call x0 -> x2, Pallas kernels: none -> 8.67 us  [plan_call(): pl.pallas_call(functools.partial(kernel, local), grid=(1,), in_specs=[sme...]
    pallas_call x1 -> x2, Pallas kernels: 49.1 us -> 57.1 us  [own_base_pass(): pl.pallas_call(own_base_kernel, grid_spec=pltpu.PrefetchScalarGridSpec(nu...]
    all_to_all x2 -> x3, starting transfers between devices: 10.8 us -> 17.7 us  [the longest x2 13.1 us: local_step(): lax.all_to_all(sent.reshape(ep_size, -1, width), 'ep', 0, 0, tiled=True)]
  transfers between devices with their start and end apart: 8 -> 10, of which waited for: 4 -> 5; matrix products, arithmetic and copies ran while one was open for 4% -> 1% of each run, Pallas kernels for 41% -> 49%
where the time goes in v2:
time: 522 us; the launch traced here: 514 us
  Pallas kernels  283 us (54%)
  waiting for transfers between devices  167 us (32%)
  starting transfers between devices  37.3 us (7%)
  between operations  14.8 us (3%)
  local copies, waits for them, and re-layouts  5.76 us (1%)
    pallas_call x1, Pallas kernels, grad_pass(): pl.pallas_call(grad_kernel, grid_spec=pltpu.PrefetchScalarGridSpec(num_sc...  140 us
    ppermute x2, waiting for transfers between devices, local_step(): base_z.append(lax.ppermute(base[c], 'dp', swap).reshape(slots))  92.8 us
    pallas_call x2, Pallas kernels, own_base_pass(): pl.pallas_call(own_base_kernel, grid_spec=pltpu.PrefetchScalarGridSpec(nu...  57.1 us
    all_to_all x2, waiting for transfers between devices, local_step(): lax.all_to_all(sent.reshape(ep_size, -1, width), 'ep', 0, 0, tiled=True)  44.5 us
    pallas_call x1, Pallas kernels, own_over_pass(): pl.pallas_call(own_over_kernel, grid_spec=pltpu.PrefetchScalarGridSpec(nu...  29.4 us
    ppermute x1, waiting for transfers between devices, local_step(): over_sent_z = lax.ppermute(over_sent, 'dp', swap)  28.7 us
    pallas_call x3, Pallas kernels, permute_rows(): pl.pallas_call(permute_kernel, grid=(n_rows // tile,), in_specs=[pl.Block...  25.4 us
    pallas_call x1, Pallas kernels, unpermute_rows(): pl.pallas_call(unpermute_kernel, grid=(tok_count // PERM_TILE,), in_specs...  22.1 us
  transfers between devices with their start and end apart: 10, of which 5 were waited for; matrix products, arithmetic and copies ran while one was open for 1% of the time, Pallas kernels for 49%

profile of v2, /device:TPU:9, one launch (start us, length us, event | category | flops | bytes accessed | tf_op | source)
XLA Modules:
  0.0 513.6 jit_solution(12767156740249917478)
XLA Ops:
  7.2 1.1 convert_reduce_fusion.2
  11.0 6.6 %permute.3 = bf16[408,1536]{1,0:T(8,128)(2,1)} custom-call(s32[1,2048]{1,0:T(1,128)} %get-tuple-element.369.pos_ref, bf16[2048,768]{1,0:T(8,128)(2,1)} %x_ref.5, bf16[2048,768]{1,0:T(8,128)(2,1)} %gy_ref.5, bf16[8,1536]{1,0:T(8,128)(2,1)} %pad.4.refs_0_), custom_call_target="tpu_custom_call" | custom-call | flops 2516582400 | bytes 16000000 | tf_op jit(solution)/shard_map/permute/pallas_call | solution.py:79
  17.7 28.7 %collective-permute-done.2 = bf16[51,8,1536]{2,1,0:T(8,128)(2,1)} collective-permute-done((bf16[51,8,1536]{2,1,0:T(8,128)(2,1)}, bf16[51,8,1536]{2,1,0:T(8,128)(2,1)}, u32[]{:S(2)}, u32[]{:S(2)}) %collective-permute-start.2) | collective-permute-done | bytes 1253408 | tf_op jit(solution)/shard_map/ppermute | solution.py:735
  46.5 9.5 %permute.5 = bf16[896,1536]{1,0:T(8,128)(2,1)} custom-call(s32[1,2048]{1,0:T(1,128)} %bitcast.208, bf16[2048,768]{1,0:T(8,128)(2,1)S(1)} %copy-done.2, bf16[2048,768]{1,0:T(8,128)(2,1)} %gy_ref.5), custom_call_target="tpu_custom_call" | custom-call | flops 5637144576 | bytes 16000000 | tf_op jit(solution)/shard_map/permute/pallas_call | solution.py:79
  56.0 5.6 %all-to-all-start.5 = ((bf16[8,112,1536]{2,1,0:T(8,128)(2,1)}), bf16[8,112,1536]{2,1,0:T(8,128)(2,1)}, u32[]{:S(2)}, u32[]{:S(2)}) async-start(bf16[8,112,1536]{2,1,0:T(8,128)(2,1)} %bitcast.200), calls=%async_computation.5 | async-start | bytes 5505024 | tf_op jit(solution)/shard_map/all_to_all | solution.py:730
  61.6 9.3 %permute.4 = bf16[896,1536]{1,0:T(8,128)(2,1)} custom-call(s32[1,2048]{1,0:T(1,128)} %get-tuple-element.368.pos_ref, bf16[2048,768]{1,0:T(8,128)(2,1)S(1)} %copy-done.2, bf16[2048,768]{1,0:T(8,128)(2,1)} %gy_ref.5), custom_call_target="tpu_custom_call" | custom-call | flops 5637144576 | bytes 16000000 | tf_op jit(solution)/shard_map/permute/pallas_call | solution.py:79
  70.9 31.2 %all-to-all-done.5 = bf16[8,112,1536]{2,1,0:T(8,128)(2,1)} async-done(((bf16[8,112,1536]{2,1,0:T(8,128)(2,1)}), bf16[8,112,1536]{2,1,0:T(8,128)(2,1)}, u32[]{:S(2)}, u32[]{:S(2)}) %all-to-all-start.5) | async-done | bytes 2752544 | tf_op jit(solution)/shard_map/all_to_all | solution.py:730
  102.1 7.5 %all-to-all-start.4 = ((bf16[8,112,1536]{2,1,0:T(8,128)(2,1)}), bf16[8,112,1536]{2,1,0:T(8,128)(2,1)}, u32[]{:S(2)}, u32[]{:S(2)}) async-start(bf16[8,112,1536]{2,1,0:T(8,128)(2,1)} %bitcast.199), calls=%async_computation.4 | async-start | bytes 5505024 | tf_op jit(solution)/shard_map/all_to_all | solution.py:730
  111.3 28.4 %own_base.2 = (bf16[8,4,56,1536]{3,2,1,0:T(8,128)(2,1)}, bf16[1792,768]{1,0:T(8,128)(2,1)}, bf16[1792,768]{1,0:T(8,128)(2,1)}, bf16[1792,3072]{1,0:T(8,128)(2,1)...) custom-call(s32[1]{0:T(128)} %bitcast.54.lead_ref.first_ref, ...), custom_call_target="tpu_custom_call" | custom-call | flops 16999999488 | bytes 40000000 | tf_op jit(solution)/shard_map/own_base/pallas_call | solution.py:199
  139.7 13.4 %all-to-all-done.4 = bf16[8,112,1536]{2,1,0:T(8,128)(2,1)} async-done(((bf16[8,112,1536]{2,1,0:T(8,128)(2,1)}), bf16[8,112,1536]{2,1,0:T(8,128)(2,1)}, u32[]{:S(2)}, u32[]{:S(2)}) %all-to-all-start.4) | async-done | bytes 2752544 | tf_op jit(solution)/shard_map/all_to_all | solution.py:730
  153.1 28.8 %own_base.3 = (bf16[8,4,56,1536]{3,2,1,0:T(8,128)(2,1)}, bf16[1792,768]{1,0:T(8,128)(2,1)}, bf16[1792,768]{1,0:T(8,128)(2,1)}, bf16[1792,3072]{1,0:T(8,128)(2,1)...) custom-call(s32[1]{0:T(128)S(6)} %add.211.first_ref, ...), custom_call_target="tpu_custom_call", output_to_operand_aliasing={{0}: (6, {}), {1}: (7, {}), {2}: (8, {}), {3}: (9, {}), {4}... | custom-call | flops 16999999488 | bytes 40000000 | tf_op jit(solution)/shard_map/own_base/pallas_call | solution.py:199
  181.8 3.4 shard_map.102
  185.3 29.4 %own_over.1 = (bf16[400,8,1536]{2,1,0:T(8,128)(2,1)}, bf16[1664,768]{1,0:T(8,128)(2,1)}, bf16[1664,768]{1,0:T(8,128)(2,1)}, bf16[1664,3072]{1,0:T(8,128)(2,1)}, ...) custom-call(s32[4,8]{1,0:T(4,128)} %get-tuple-element.222.tab_ref, ...), custom_call_target="tpu_custom_call", output_to_operand_aliasing={{0}: (9, {})} | custom-call | flops 10000000000 | bytes 40000000 | tf_op jit(solution)/shard_map/own_over/pallas_call | solution.py:298
  215.3 19.1 %collective-permute-start.3 = (bf16[8,112,1536]{2,1,0:T(8,128)(2,1)}, bf16[8,112,1536]{2,1,0:T(8,128)(2,1)}, u32[]{:S(2)}, u32[]{:S(2)}) collective-permute-start(bf16[8,112,1536]{2,1,0:T(8,128)(2,1)} %all-to-all-done.5), channel_id=1, source_target_pairs={{0,8},{8,0},{1,9},{9,1},{2,10},{10,2},{3,11},{11,3},{4,12},{12,4},... | collective-permute-start | bytes 8257544 | tf_op jit(solution)/shard_map/ppermute | solution.py:731
  234.4 2.0 copy.50.pos_ref
  236.4 5.3 %shard_map.101 = (s32[7,24]{1,0:T(8,128)}, s32[208]{0:T(256)}, s32[1]{0:T(128)}) custom-call(s32[1]{0:T(128)} %bitcast.54.lead_ref.first_ref, bf16[8,51,8,1536]{3,2,1,0:T(8,128)(2,1)} %all-gather.6.cloned.1.call-done.own_ref.count_ref, bf16[8,51,8,1536]{3,2,1,0:T(8,128)(2,1)} %bitcast.196), custom_call_target="tpu_custom_call" | custom-call | tf_op jit(solution)/shard_map/pallas_call | solution.py:627
  242.3 4.6 all-to-all-start.6
  247.0 52.8 %collective-permute-done.3 = bf16[8,112,1536]{2,1,0:T(8,128)(2,1)} collective-permute-done((bf16[8,112,1536]{2,1,0:T(8,128)(2,1)}, bf16[8,112,1536]{2,1,0:T(8,128)(2,1)}, u32[]{:S(2)}, u32[]{:S(2)}) %collective-permute-start.3) | collective-permute-done | bytes 2752544 | tf_op jit(solution)/shard_map/ppermute | solution.py:731
  299.8 40.0 %collective-permute-done.4 = bf16[8,112,1536]{2,1,0:T(8,128)(2,1)} collective-permute-done((bf16[8,112,1536]{2,1,0:T(8,128)(2,1)}, bf16[8,112,1536]{2,1,0:T(8,128)(2,1)}, u32[]{:S(2)}, u32[]{:S(2)}) %collective-permute-start.4) | collective-permute-done | bytes 2752544 | tf_op jit(solution)/shard_map/ppermute | solution.py:731
  339.8 140.0 %grad_pass.1 = (f32[4,768,3072]{2,1,0:T(8,128)}, f32[4,3072,768]{2,1,0:T(8,128)}) custom-call(s32[7,24]{1,0:T(8,128)} %get-tuple-element.230.tab_ref, s32[208]{0:T(256)} %get-tuple-element.231.ids_ref, s32[1]{0:T(128)} %bitcast.54.lead_ref.first_ref, bf16[1792,768]{1,0:T(8,128)(2,1)} %get-tuple-element.232.xb_ref, ...), custom_call_target="tpu_custom_call" | custom-call | flops 70000001024 | bytes 150000000 | tf_op jit(solution)/shard_map/grad_pass/pallas_call | solution.py:452
  479.8 2.1 reduce_sum.75
  482.0 22.1 %unpermute.1 = (bf16[2048,768]{1,0:T(8,128)(2,1)}, bf16[2048,768]{1,0:T(8,128)(2,1)}) custom-call(s32[2048,1]{1,0:T(8,128)} %copy.50.pos_ref, bf16[8,224,1536]{2,1,0:T(8,128)(2,1)} %all-to-all-done.6.refs_0_.refs_1_, bf16[8,224,1536]{2,1,0:T(8,128)(2,1)} %all-to-all-done.6.refs_0_.refs_1_, bf16[400,1536]{1,0:T(8,128)(2,1)} %bitcast.210), custom_call_target="tpu_custom_call" | custom-call | flops 14000000000 | bytes 16000000 | tf_op jit(solution)/shard_map/unpermute/pallas_call | solution.py:115
  504.1 1.3 while.34
  505.3 1.5 copy.109
  (41 shorter events, 5.2 us)
Async XLA Ops:
  7.2 39.3 %copy-start.2 = (bf16[2048,768]{1,0:T(8,128)(2,1)S(1)}, bf16[2048,768]{1,0:T(8,128)(2,1)}, u32[]{:S(2)}) copy-start(bf16[2048,768]{1,0:T(8,128)(2,1)} %x_ref.5) | copy-start | bytes 9437188
  7.2 174.7 %all-gather.6.cloned.1.call-start = ((), (), s32[]{:S(2)}) async-start(), calls=%async_computation.9 | async-start | bytes 11280384 | tf_op jit(solution)/shard_map/all_gather | solution.py:734
  9.7 36.7 %copy-start.23 = (s32[16,128]{1,0:T(8,128)}, s32[16,128]{1,0:T(8,128)S(1)}, u32[]{:S(2)}) copy-start(s32[16,128]{1,0:T(8,128)S(1)} %convert_element_type.133) | copy-start | bytes 24580
  17.6 218.8 %all-gather.8.cloned.1.call-start = ((), (), s32[]{:S(2)}) async-start(), calls=%async_computation.11 | async-start | bytes 11280384 | tf_op jit(solution)/shard_map/all_gather | solution.py:736
  17.6 28.8 %collective-permute-start.2 = (bf16[51,8,1536]{2,1,0:T(8,128)(2,1)}, bf16[51,8,1536]{2,1,0:T(8,128)(2,1)}, u32[]{:S(2)}, u32[]{:S(2)}) collective-permute-start(bf16[51,8,1536]{2,1,0:T(8,128)(2,1)} %bitcast.203), channel_id=1, source_target_pairs={{0,8},{8,0},{1,9},{9,1},{2,10},{10,2},{3,11},{11,3},{4,12},{12,4},... | collective-permute-start | bytes 3760136 | tf_op jit(solution)/shard_map/ppermute | solution.py:735
  56.0 46.0 %all-to-all-start.5 = ((bf16[8,112,1536]{2,1,0:T(8,128)(2,1)}), bf16[8,112,1536]{2,1,0:T(8,128)(2,1)}, u32[]{:S(2)}, u32[]{:S(2)}) async-start(bf16[8,112,1536]{2,1,0:T(8,128)(2,1)} %bitcast.200), calls=%async_computation.5 | async-start | bytes 5505024 | tf_op jit(solution)/shard_map/all_to_all | solution.py:730
  61.6 48.3 %copy-start.12 = (bf16[768,32]{0,1:T(8,128)(2,1)S(1)}, bf16[768,32]{0,1:T(8,128)(2,1)}, u32[]{:S(2)}) copy-start(bf16[768,32]{0,1:T(8,128)(2,1)} %param.13) | copy-start | bytes 147460
  102.1 51.0 %all-to-all-start.4 = ((bf16[8,112,1536]{2,1,0:T(8,128)(2,1)}), bf16[8,112,1536]{2,1,0:T(8,128)(2,1)}, u32[]{:S(2)}, u32[]{:S(2)}) async-start(bf16[8,112,1536]{2,1,0:T(8,128)(2,1)} %bitcast.199), calls=%async_computation.4 | async-start | bytes 5505024 | tf_op jit(solution)/shard_map/all_to_all | solution.py:730
  109.6 370.3 %all-gather.10.cloned.1.call-start = ((), (), s32[]{:S(2)}) async-start(), calls=%async_computation.12 | async-start | bytes 1671168 | tf_op jit(solution)/shard_map/all_gather | solution.py:759
  214.7 267.3 %reduce-scatter.2.cloned.1.call-start = ((), (), s32[]{:S(2)}) async-start(), calls=%async_computation.10 | async-start | bytes 11059200 | tf_op jit(solution)/shard_map/reduce_scatter | solution.py:756
  215.3 84.5 %collective-permute-start.3 = (bf16[8,112,1536]{2,1,0:T(8,128)(2,1)}, bf16[8,112,1536]{2,1,0:T(8,128)(2,1)}, u32[]{:S(2)}, u32[]{:S(2)}) collective-permute-start(bf16[8,112,1536]{2,1,0:T(8,128)(2,1)} %all-to-all-done.5), channel_id=1, source_target_pairs={{0,8},{8,0},{1,9},{9,1},{2,10},{10,2},{3,11},{11,3},{4,12},{12,4},... | collective-permute-start | bytes 8257544 | tf_op jit(solution)/shard_map/ppermute | solution.py:731
  234.3 105.5 %collective-permute-start.4 = (bf16[8,112,1536]{2,1,0:T(8,128)(2,1)}, bf16[8,112,1536]{2,1,0:T(8,128)(2,1)}, u32[]{:S(2)}, u32[]{:S(2)}) collective-permute-start(bf16[8,112,1536]{2,1,0:T(8,128)(2,1)} %all-to-all-done.4), channel_id=1, source_target_pairs={{0,8},{8,0},{1,9},{9,1},{2,10},{10,2},{3,11},{11,3},{4,12},{12,4},... | collective-permute-start | bytes 8257544 | tf_op jit(solution)/shard_map/ppermute | solution.py:731
  242.3 239.6 %all-to-all-start.6 = ((bf16[8,224,1536]{2,1,0:T(8,128)(2,1)}), bf16[8,224,1536]{2,1,0:T(8,128)(2,1)}, u32[]{:S(2)}, u32[]{:S(2)}) async-start(bf16[8,224,1536]{2,1,0:T(8,128)(2,1)} %bitcast.192), calls=%async_computation.6 | async-start | bytes 11010048 | tf_op jit(solution)/shard_map/all_to_all | solution.py:753
  482.0 22.1 %copy-start.3 = (bf16[2048,768]{1,0:T(8,128)(2,1)S(1)}, bf16[2048,768]{1,0:T(8,128)(2,1)}, u32[]{:S(2)}) copy-start(bf16[2048,768]{1,0:T(8,128)(2,1)} %x_ref.5) | copy-start | bytes 9437188
  482.0 22.1 %copy-start.9 = (s32[2048]{0:T(1024)S(1)}, s32[2048]{0:T(1024)}, u32[]{:S(2)}) copy-start(s32[2048]{0:T(1024)} %param.12) | copy-start | bytes 24580
  482.0 22.1 %copy-start.13 = (bf16[768,32]{0,1:T(8,128)(2,1)S(1)}, bf16[768,32]{0,1:T(8,128)(2,1)}, u32[]{:S(2)}) copy-start(bf16[768,32]{0,1:T(8,128)(2,1)} %param.13) | copy-start | bytes 147460
Sparse Core Ops, SparseCore 0:
  17.7 76.1 all-gather.5
  95.8 93.0 all-gather.7
  214.8 71.1 all-gather.9
  289.4 71.5 reduce-scatter.1

commit v3 on v2

--- a/solution.py
+++ b/solution.py
@@ -14,6 +14,8 @@
 OVER_GROUPS = 50
 SENT_GROUPS = OVER_GROUPS + 1
 MAX_OVER_TILES = 8
+RUNS = 8
+RUN_SIZES = (16, 8, 4, 2, 1)
 TILE_GROUPS = 26
 TILE = TILE_GROUPS * GROUP
 PERM_TILE = 256
@@ -94,11 +96,12 @@
 def unpermute_kernel(pos_ref, *refs):
     *parts, out_ref, dx_ref = refs
     toks, d_model = out_ref.shape
+    pos = jnp.transpose(jnp.broadcast_to(pos_ref[...], (8, toks)))[:, :1]
     first, out, dx = 0, 0.0, 0.0
     for part in parts:
         rows = part[...].reshape(-1, 2 * d_model)
         row_id = lax.broadcasted_iota(I32, (toks, rows.shape[0]), 1) + first
-        select = jnp.where(row_id == pos_ref[...], 1.0, 0.0).astype(BF16)
+        select = jnp.where(row_id == pos, 1.0, 0.0).astype(BF16)
         out += dot(select, rows[:, :d_model])
         dx += dot(select, rows[:, d_model:])
         first += rows.shape[0]
@@ -115,14 +118,14 @@
     return pl.pallas_call(
         unpermute_kernel,
         grid=(tok_count // PERM_TILE,),
-        in_specs=[pl.BlockSpec((PERM_TILE, 1), lambda i: (i, 0))]
+        in_specs=[pl.BlockSpec((1, PERM_TILE), lambda i: (0, i))]
         + [pl.BlockSpec(chunk, lambda i, c=c: (0, c, 0)) for c in range(CHUNKS)]
         + [pl.BlockSpec(over.shape, lambda i: (0, 0))],
         out_specs=[pl.BlockSpec((PERM_TILE, d_model), lambda i: (i, 0))] * 2,
         out_shape=[shape, shape],
         cost_estimate=pl.CostEstimate(flops=14_000_000_000, bytes_accessed=16_000_000, transcendentals=0),
         name='unpermute',
-    )(pos.reshape(tok_count, 1), *[base] * CHUNKS, over)
+    )(pos.reshape(1, tok_count), *[base] * CHUNKS, over)
 
 
 def gate(x, wg, expert):
@@ -221,23 +224,31 @@
     )(first_expert + lead, rows, wg, w_up, w_down, dwg, *kept)
 
 
-def group_copies(ids_ref, slot_base, count, hbm, buf, sem, to_hbm):
-    def body(g, carry):
-        gid = ids_ref[slot_base + g]
-        ends = (buf.at[g], hbm.at[gid]) if to_hbm else (hbm.at[gid], buf.at[g])
-        pltpu.make_async_copy(*ends, sem).start()
+def run_copies(runs_ref, tile, n_runs, hbm, buf, sem, to_hbm):
+    def body(r, carry):
+        at = (tile * RUNS + r) * 3
+        first, left, slot = runs_ref[at], runs_ref[at + 1], runs_ref[at + 2]
+        for size in RUN_SIZES:
+            take = left >= size
+
+            @pl.when(take)
+            def _(first=first, slot=slot, size=size):
+                ends = (hbm.at[pl.ds(first, size)], buf.at[pl.ds(slot, size)])
+                pltpu.make_async_copy(*(ends[::-1] if to_hbm else ends), sem).start()
+
+            step = jnp.where(take, size, 0)
+            first, slot, left = first + step, slot + step, left - step
         return carry
 
-    lax.fori_loop(0, count, body, 0)
-
-
-def group_waits(count, hbm, buf, sem, to_hbm):
-    def body(g, carry):
-        ends = (buf.at[0], hbm.at[0]) if to_hbm else (hbm.at[0], buf.at[0])
-        pltpu.make_async_copy(*ends, sem).wait()
-        return carry
-
-    lax.fori_loop(0, count, body, 0)
+    lax.fori_loop(0, n_runs, body, 0)
+
+
+def run_waits(count, hbm, buf, sem, to_hbm):
+    for size in RUN_SIZES:
+        @pl.when((count & size) != 0)
+        def _(size=size):
+            ends = (hbm.at[pl.ds(0, size)], buf.at[pl.ds(0, size)])
+            pltpu.make_async_copy(*(ends[::-1] if to_hbm else ends), sem).wait()
 
 
 def tile_rows(buf, count):
@@ -246,7 +257,7 @@
     return jnp.where(row_id < count * GROUP, rows, jnp.zeros((), rows.dtype))
 
 
-def own_over_kernel(tab_ref, ids_ref, back_ids_ref, first_ref, rows_hbm, wg_ref, up_ref, down_ref, dwg_in, zero_od,
+def own_over_kernel(tab_ref, runs_ref, first_ref, rows_hbm, wg_ref, up_ref, down_ref, dwg_in, zero_od,
                     od_hbm, x_ref, dy_ref, h_ref, da_ref, dwg_ref, in_buf, out_buf, in_sem, out_sem):
     del zero_od
     step = pl.program_id(0)
@@ -257,16 +268,15 @@
     @pl.when(step == 0)
     def _():
         dwg_ref[...] = dwg_in[...]
-        group_copies(ids_ref, 0, count, rows_hbm, in_buf.at[0], in_sem.at[0], False)
+        run_copies(runs_ref, 0, tab_ref[4, 0], rows_hbm, in_buf.at[0], in_sem.at[0], False)
 
     @pl.when(count > 0)
     def _():
-        group_waits(count, rows_hbm, in_buf.at[slot], in_sem.at[slot], False)
+        run_waits(count, rows_hbm, in_buf.at[slot], in_sem.at[slot], False)
 
         @pl.when(step + 1 < pl.num_programs(0))
         def _():
-            group_copies(ids_ref, (step + 1) * TILE_GROUPS, tab_ref[1, step + 1], rows_hbm, in_buf.at[1 - slot],
-                         in_sem.at[1 - slot], False)
+            run_copies(runs_ref, step + 1, tab_ref[4, step + 1], rows_hbm, in_buf.at[1 - slot], in_sem.at[1 - slot], False)
 
         rows = tile_rows(in_buf.at[slot], count)
         x = rows[:, :d_model]
@@ -276,35 +286,35 @@
 
         @pl.when(step > 0)
         def _():
-            group_waits(tab_ref[1, step - 1], od_hbm, out_buf, out_sem, True)
+            run_waits(tab_ref[1, step - 1], od_hbm, out_buf, out_sem, True)
 
         out_buf[:, :, :d_model] = out.reshape(TILE_GROUPS, GROUP, d_model)
         out_buf[:, :, d_model:] = dx.reshape(TILE_GROUPS, GROUP, d_model)
-        group_copies(back_ids_ref, step * TILE_GROUPS, count, od_hbm, out_buf, out_sem, True)
+        run_copies(runs_ref, step, tab_ref[4, step], od_hbm, out_buf, out_sem, True)
 
         @pl.when(tab_ref[3, step] == 1)
         def _():
-            group_waits(count, od_hbm, out_buf, out_sem, True)
-
-
-def own_over_pass(table, ids, back_ids, first_expert, rows, wg, w_up, w_down, dwg, zero_od):
+            run_waits(count, od_hbm, out_buf, out_sem, True)
+
+
+def own_over_pass(table, runs, first_expert, rows, wg, w_up, w_down, dwg, zero_od):
     d_model, d_ff = w_up.shape[1], w_up.shape[2]
     width = rows.shape[-1]
     n_tiles = table.shape[1]
     hbm = pl.BlockSpec(memory_space=pl.ANY)
-    const = lambda i, tab, ids, back, first: (0, 0)
-    store_spec = lambda cols: pl.BlockSpec((TILE, cols), lambda i, tab, ids, back, first: (tab[2, i], 0))
+    const = lambda i, tab, runs, first: (0, 0)
+    store_spec = lambda cols: pl.BlockSpec((TILE, cols), lambda i, tab, runs, first: (tab[2, i], 0))
     rows_of = lambda cols: jax.ShapeDtypeStruct((n_tiles * TILE, cols), BF16)
     return pl.pallas_call(
         own_over_kernel,
         grid_spec=pltpu.PrefetchScalarGridSpec(
-            num_scalar_prefetch=4,
+            num_scalar_prefetch=3,
             grid=(n_tiles,),
             in_specs=[
                 hbm,
                 pl.BlockSpec(wg.shape, const),
-                pl.BlockSpec((1, d_model, d_ff), lambda i, tab, ids, back, first: (tab[0, i], 0, 0)),
-                pl.BlockSpec((1, d_ff, d_model), lambda i, tab, ids, back, first: (tab[0, i], 0, 0)),
+                pl.BlockSpec((1, d_model, d_ff), lambda i, tab, runs, first: (tab[0, i], 0, 0)),
+                pl.BlockSpec((1, d_ff, d_model), lambda i, tab, runs, first: (tab[0, i], 0, 0)),
                 pl.BlockSpec(dwg.shape, const),
                 hbm,
             ],
@@ -319,17 +329,17 @@
         ),
         out_shape=[jax.ShapeDtypeStruct(zero_od.shape, BF16), rows_of(d_model), rows_of(d_model), rows_of(d_ff),
                    rows_of(d_ff), jax.ShapeDtypeStruct(dwg.shape, F32)],
-        input_output_aliases={9: 0},
+        input_output_aliases={8: 0},
         compiler_params=pltpu.CompilerParams(vmem_limit_bytes=VMEM_BYTES, dimension_semantics=('arbitrary',)),
         cost_estimate=pl.CostEstimate(flops=10_000_000_000, bytes_accessed=40_000_000, transcendentals=2_000_000),
         name='own_over',
-    )(table, ids, back_ids, first_expert, rows, wg, w_up, w_down, dwg, zero_od)
+    )(table, runs, first_expert, rows, wg, w_up, w_down, dwg, zero_od)
 
 
 OWN_BASE, OWN_OVER, OTHER_BASE, OTHER_OVER = range(4)
 
 
-def grad_kernel(tab_ref, ids_ref, first_ref, xb_ref, dyb_ref, hb_ref, dab_ref, xo_ref, dyo_ref, ho_ref, dao_ref, *refs):
+def grad_kernel(tab_ref, runs_ref, first_ref, xb_ref, dyb_ref, hb_ref, dab_ref, xo_ref, dyo_ref, ho_ref, dao_ref, *refs):
     *base_hbm, over_hbm, wg_ref, up_hbm, down_hbm, dup_hbm, ddown_hbm = refs[:-12]
     dup, ddown, up_buf, down_buf, h_buf, da_buf, base_buf, in_buf, w_sems, base_sem, in_sem, out_sems = refs[-12:]
     step = pl.program_id(0)
@@ -386,6 +396,14 @@
     def base_copy(e):
         chunk = base_hbm[e // base_hbm[0].shape[1]]
         return pltpu.make_async_copy(chunk.at[:, e % chunk.shape[1]], base_buf, base_sem)
+
+    ahead = step + 1
+    ahead_at = jnp.minimum(ahead, pl.num_programs(0) - 1)
+
+    @pl.when((ahead < pl.num_programs(0)) & (tab_ref[1, ahead_at] == OTHER_OVER))
+    def _():
+        run_copies(runs_ref, tab_ref[5, ahead_at], tab_ref[7, ahead_at], over_hbm, in_buf.at[ahead % 2], in_sem.at[ahead % 2],
+                   False)
 
     @pl.when(kind == OWN_BASE)
     def _():
@@ -437,9 +455,8 @@
 
     @pl.when(kind == OTHER_OVER)
     def _():
-        group_copies(ids_ref, tab_ref[5, step] * TILE_GROUPS, count, over_hbm, in_buf, in_sem, False)
-        group_waits(count, over_hbm, in_buf, in_sem, False)
-        other_rows(tile_rows(in_buf, count), TILE)
+        run_waits(count, over_hbm, in_buf.at[step % 2], in_sem.at[step % 2], False)
+        other_rows(tile_rows(in_buf.at[step % 2], count), TILE)
 
 
 def grad_pass(table, ids, first_expert, base_store, over_store, base, over, wg, w_up, w_down):
@@ -478,10 +495,10 @@
                 pltpu.VMEM((base_rows, d_ff), BF16),
                 pltpu.VMEM((base_rows, d_ff), BF16),
                 pltpu.VMEM((n_src, seg, width), BF16),
-                pltpu.VMEM((TILE_GROUPS, GROUP, width), BF16),
+                pltpu.VMEM((2, TILE_GROUPS, GROUP, width), BF16),
                 pltpu.SemaphoreType.DMA((2,)),
                 pltpu.SemaphoreType.DMA,
-                pltpu.SemaphoreType.DMA,
+                pltpu.SemaphoreType.DMA((2,)),
                 pltpu.SemaphoreType.DMA((2,)),
             ],
         ),
@@ -506,28 +523,39 @@
     return size.astype(I32), first.astype(I32), excess
 
 
-def fill_tiles(n_src, local, lead, size, first, write):
-    firsts, tile = [], jnp.int32(0)
+def fill_tiles(n_src, local, lead, size, first, runs, n_runs, count):
+    for t in range(MAX_OVER_TILES):
+        n_runs[t] = 0
+        count[t] = 0
+
+    def put(tile, slot, begin, groups):
+        @pl.when((groups > 0) & (tile < MAX_OVER_TILES))
+        def _():
+            at = (tile * RUNS + n_runs[tile]) * 3
+            runs[at] = begin
+            runs[at + 1] = groups
+            runs[at + 2] = slot
+            n_runs[tile] = n_runs[tile] + 1
+            count[tile] = count[tile] + groups
+
+    spans, tile = [], jnp.int32(0)
     for e in range(local):
-        base = tile * TILE_GROUPS
-
-        def per_source(s, at, e=e, base=base):
-            begin = first[s, lead + e]
-
-            def per_group(g, at):
-                @pl.when(base + at < MAX_OVER_TILES * TILE_GROUPS)
-                def _():
-                    write(base + at, s, begin + g)
-
-                return at + 1
-
-            return lax.fori_loop(0, size[s, lead + e], per_group, at)
-
-        total = lax.fori_loop(0, n_src, per_source, jnp.int32(0))
-        tiles = jnp.minimum(lax.div(total + (TILE_GROUPS - 1), jnp.int32(TILE_GROUPS)), MAX_OVER_TILES - tile)
-        firsts.append((tile, tiles, total))
-        tile = tile + tiles
-    return firsts, tile
+        def per_source(s, where, e=e):
+            tile, slot = where
+            groups = size[s, lead + e]
+            begin = s * SENT_GROUPS + first[s, lead + e]
+            head = jnp.minimum(groups, TILE_GROUPS - slot)
+            rest = groups - head
+            put(tile, slot, begin, head)
+            put(tile + 1, 0, begin + head, rest)
+            full = (slot + head == TILE_GROUPS).astype(I32)
+            return tile + full, jnp.where(full == 1, rest, slot + head)
+
+        end, slot = lax.fori_loop(0, n_src, per_source, (tile, jnp.int32(0)))
+        end = jnp.minimum(end + (slot > 0).astype(I32), MAX_OVER_TILES)
+        spans.append((tile, end - tile))
+        tile = end
+    return spans, tile
 
 
 def to_scalars(pairs, sems):
@@ -538,85 +566,77 @@
         copy.wait()
 
 
-def own_plan_kernel(local, lead_ref, count_ref, tab_ref, ids_ref, back_ref, size_v, first_v, size_s, first_s, sems):
+def own_plan_kernel(local, lead_ref, count_ref, tab_ref, runs_ref, size_v, first_v, size_s, first_s, n_runs, count, sems):
     size_v[...], first_v[...], _ = overflow_spans(count_ref, local)
     to_scalars([(size_v, size_s), (first_v, first_s)], sems)
-
-    def write(at, s, g):
-        ids_ref[at] = s * SENT_GROUPS + g
-        back_ref[at] = s * OVER_GROUPS + g
-
-    spans, n_tiles = fill_tiles(count_ref.shape[0], local, lead_ref[0], size_s, first_s, write)
+    spans, n_tiles = fill_tiles(count_ref.shape[0], local, lead_ref[0], size_s, first_s, runs_ref, n_runs.at[0], count.at[0])
     last = jnp.maximum(n_tiles - 1, 0)
     for t in range(MAX_OVER_TILES):
         tab_ref[0, t] = local - 1
-        tab_ref[1, t] = 0
+        tab_ref[1, t] = count[0, t]
         tab_ref[2, t] = jnp.minimum(t, last)
         tab_ref[3, t] = (last == t).astype(I32)
-    for e, (tile, tiles, total) in enumerate(spans):
-        def body(k, left, e=e, tile=tile):
+        tab_ref[4, t] = n_runs[0, t]
+    for e, (tile, tiles) in enumerate(spans):
+        def body(k, c, e=e, tile=tile):
             tab_ref[0, tile + k] = e
-            tab_ref[1, tile + k] = jnp.minimum(left, TILE_GROUPS)
-            return left - TILE_GROUPS
-
-        lax.fori_loop(0, tiles, body, total)
-
-
-def grad_plan_kernel(local, lead_ref, own_ref, other_ref, tab_ref, ids_ref, fits_ref, size_v, first_v, size_s, first_s, sems):
+            return c
+
+        lax.fori_loop(0, tiles, body, 0)
+
+
+def grad_plan_kernel(local, lead_ref, own_ref, other_ref, tab_ref, runs_ref, fits_ref, size_v, first_v, size_s, first_s,
+                     n_runs, count, sems):
     n_src = own_ref.shape[0]
     size_v[0], first_v[0], own_excess = overflow_spans(own_ref, local)
     size_v[1], first_v[1], other_excess = overflow_spans(other_ref, local)
     to_scalars([(size_v, size_s), (first_v, first_s)], sems)
     fits_ref[0] = (jnp.maximum(own_excess, other_excess) <= 0.0).astype(I32)
-
-    def write(at, s, g):
-        ids_ref[at] = s * SENT_GROUPS + g
-
-    own, _ = fill_tiles(n_src, local, lead_ref[0], size_s.at[0], first_s.at[0], lambda at, s, g: None)
-    other, _ = fill_tiles(n_src, local, lead_ref[0], size_s.at[1], first_s.at[1], write)
+    lead = lead_ref[0]
+    own, n_tiles = fill_tiles(n_src, local, lead, size_s.at[0], first_s.at[0], runs_ref, n_runs.at[0], count.at[0])
+    other, _ = fill_tiles(n_src, local, lead, size_s.at[1], first_s.at[1], runs_ref, n_runs.at[1], count.at[1])
     max_steps = tab_ref.shape[1]
-    for t in range(max_steps):
-        tab_ref[1, t] = -1
-        tab_ref[2, t] = 0
-    step = jnp.int32(0)
-    own_at = jnp.int32(0)
-
-    def emit(step, expert, kind, own_tile, groups, other_tile, next_base):
+
+    def emit(step, expert, kind, own_tile, other_tile, next_base):
+        over = (kind == OTHER_OVER).astype(I32) if not isinstance(kind, int) else int(kind == OTHER_OVER)
         tab_ref[0, step] = expert
         tab_ref[1, step] = kind
+        tab_ref[2, step] = 0
         tab_ref[3, step] = jnp.clip(own_tile, 0, MAX_OVER_TILES - 1)
-        tab_ref[4, step] = groups
+        tab_ref[4, step] = count[1, other_tile] * over
         tab_ref[5, step] = other_tile
         tab_ref[6, step] = next_base
-
+        tab_ref[7, step] = n_runs[1, other_tile] * over
+
+    step = jnp.int32(0)
     for e in range(local):
-        own_tile, own_tiles, _ = own[e]
-        other_tile, other_tiles, total = other[e]
+        own_tile, own_tiles = own[e]
+        other_tile, other_tiles = other[e]
         after = min(e + 1, local - 1)
-        emit(step, e, OWN_BASE, own_tile, 0, 0, e)
+        emit(step, e, OWN_BASE, own_tile, 0, e)
 
         def own_body(k, c, e=e, step=step, own_tile=own_tile, after=after):
-            emit(step + 1 + k, e, OWN_OVER, own_tile + k, 0, 0, after)
+            emit(step + 1 + k, e, OWN_OVER, own_tile + k, 0, after)
             return c
 
         lax.fori_loop(0, own_tiles, own_body, 0)
         step = step + 1 + own_tiles
         own_at = own_tile + own_tiles
-        emit(step, e, OTHER_BASE, own_at, 0, 0, after)
-
-        def other_body(k, left, e=e, step=step, own_at=own_at, other_tile=other_tile, after=after):
-            emit(step + 1 + k, e, OTHER_OVER, own_at, jnp.minimum(left, TILE_GROUPS), other_tile + k, after)
-            return left - TILE_GROUPS
-
-        lax.fori_loop(0, other_tiles, other_body, total)
+        emit(step, e, OTHER_BASE, own_at, 0, after)
+
+        def other_body(k, c, e=e, step=step, own_at=own_at, other_tile=other_tile, after=after):
+            emit(step + 1 + k, e, OTHER_OVER, own_at, other_tile + k, after)
+            return c
+
+        lax.fori_loop(0, other_tiles, other_body, 0)
         step = step + 1 + other_tiles
         tab_ref[2, step - 1] = 1
 
-    def rest(t, c):
-        emit(t, local - 1, -1, own_at, 0, 0, local - 1)
+    def dead(t, c):
+        emit(t, local - 1, -1, n_tiles - 1, 0, local - 1)
         return c
 
-    lax.fori_loop(step, max_steps, rest, 0)
+    lax.fori_loop(step, max_steps, dead, 0)
 
 
 def plan_call(kernel, local, lead, counts, out_shapes, planes):
@@ -631,6 +651,7 @@
         out_specs=[smem] * len(out_shapes),
         out_shape=[jax.ShapeDtypeStruct(o, I32) for o in out_shapes],
         scratch_shapes=[pltpu.VMEM(shape, I32), pltpu.VMEM(shape, I32), pltpu.SMEM(shape, I32), pltpu.SMEM(shape, I32),
+                        pltpu.SMEM((planes, MAX_OVER_TILES), I32), pltpu.SMEM((planes, MAX_OVER_TILES), I32),
                         pltpu.SemaphoreType.DMA((2,))],
     )(lead, *counts)
 
@@ -699,7 +720,8 @@
             total = total + lax.ppermute(term, 'dp', [(i, (i + shift) % dp_size) for i in range(dp_size)])
         return total
 
-    return (moe_out, grad_x, sum_dp(grad_up), sum_dp(grad_down), lax.psum(grad_gate, ('dp', 'ep')))
+    grad_gate = jnp.sum(lax.all_gather(grad_gate, ('dp', 'ep')), axis=0)
+    return moe_out, grad_x, sum_dp(grad_up), sum_dp(grad_down), grad_gate
 
 
 def solution(mesh):
@@ -735,14 +757,13 @@
         over_sent_z = lax.ppermute(over_sent, 'dp', swap)
         over_z = lax.all_gather(over_sent_z, 'ep')
 
-        n_ids = MAX_OVER_TILES * TILE_GROUPS
-        table, ids, back_ids = plan_call(own_plan_kernel, local, first_expert, [over],
-                                         [(4, MAX_OVER_TILES), (n_ids,), (n_ids,)], 1)
-        gtable, ids_z, fits = plan_call(grad_plan_kernel, local, first_expert, [over, over_z],
-                                        [(7, 2 * (local + MAX_OVER_TILES)), (n_ids,), (1,)], 2)
-        over_shape = (ep_size * OVER_GROUPS, GROUP, width)
-        over = over.reshape(-1, GROUP, width)
-        over_z = over_z.reshape(-1, GROUP, width)
+        n_runs = MAX_OVER_TILES * RUNS * 3
+        table, runs = plan_call(own_plan_kernel, local, first_expert, [over], [(5, MAX_OVER_TILES), (n_runs,)], 1)
+        gtable, runs_z, fits = plan_call(grad_plan_kernel, local, first_expert, [over, over_z],
+                                         [(8, 2 * (local + MAX_OVER_TILES)), (n_runs,), (1,)], 2)
+        over_shape = (ep_size * SENT_GROUPS, GROUP, width)
+        over = over.reshape(over_shape)
+        over_z = over_z.reshape(over_shape)
         dwg = jnp.zeros((n_experts, d_model), F32)
         stores = None
         for c in range(CHUNKS):
@@ -751,13 +772,13 @@
             stores = kept[:5] + kept[6:]
         od, *base_store, zero_od = stores
         base_back = lax.all_to_all(od.reshape(ep_size, -1, width), 'ep', 0, 0, tiled=True)
-        od_over, x_o, dy_o, h_o, da_o, dwg = own_over_pass(table, ids, back_ids, first_expert, over, w_gate, w_up, w_down,
+        od_over, x_o, dy_o, h_o, da_o, dwg = own_over_pass(table, runs, first_expert, over, w_gate, w_up, w_down,
                                                           dwg, zero_od)
-        over_back = lax.psum_scatter(od_over.reshape(ep_size, OVER_GROUPS, GROUP, width), 'ep', scatter_dimension=0)
-        d_up, d_down = grad_pass(gtable, ids_z, first_expert, base_store, (x_o, dy_o, h_o, da_o), base_z, over_z,
+        over_back = lax.psum_scatter(od_over.reshape(ep_size, SENT_GROUPS, GROUP, width), 'ep', scatter_dimension=0)
+        d_up, d_down = grad_pass(gtable, runs_z, first_expert, base_store, (x_o, dy_o, h_o, da_o), base_z, over_z,
                                  w_gate, w_up, w_down)
         d_gate = jnp.sum(lax.all_gather(dwg, ('dp', 'ep')), axis=0).T
-        moe_out, grad_x = unpermute_rows(pos, base_back, over_back.reshape(n_over, width))
+        moe_out, grad_x = unpermute_rows(pos, base_back, over_back.reshape(-1, width))
         sparse = (moe_out, grad_x, d_up, d_down, d_gate)
 
         def dense(carry):

time: 522 us -> 514 us (0.985)
  Pallas kernels: 283 us -> 275 us
    pallas_call x1, Pallas kernels: 140 us -> 133 us  [grad_pass(): pl.pallas_call(grad_kernel, grid_spec=pltpu.PrefetchScalarGridSpec(num_sc...]
    ppermute x2, waiting for transfers between devices: 92.8 us -> 98.3 us  [local_step(): base_z.append(lax.ppermute(base[c], 'dp', swap).reshape(slots))]
  transfers between devices with their start and end apart: 10 -> 10, of which waited for: 5 -> 5; matrix products, arithmetic and copies ran while one was open for 1% -> 1% of each run, Pallas kernels for 49% -> 48%
where the time goes in v3:
time: 514 us; the launch traced here: 506 us
  Pallas kernels  275 us (54%)
  waiting for transfers between devices  172 us (33%)
  starting transfers between devices  35.5 us (7%)
  between operations  14.8 us (3%)
    pallas_call x1, Pallas kernels, grad_pass(): pl.pallas_call(grad_kernel, grid_spec=pltpu.PrefetchScalarGridSpec(num_sc...  133 us
    ppermute x2, waiting for transfers between devices, local_step(): base_z.append(lax.ppermute(base[c], 'dp', swap).reshape(slots))  98.3 us
    pallas_call x2, Pallas kernels, own_base_pass(): pl.pallas_call(own_base_kernel, grid_spec=pltpu.PrefetchScalarGridSpec(nu...  57.1 us
    all_to_all x2, waiting for transfers between devices, local_step(): lax.all_to_all(sent.reshape(ep_size, -1, width), 'ep', 0, 0, tiled=True)  44.6 us
    ppermute x1, waiting for transfers between devices, local_step(): over_sent_z = lax.ppermute(over_sent, 'dp', swap)  28.7 us
    pallas_call x1, Pallas kernels, own_over_pass(): pl.pallas_call(own_over_kernel, grid_spec=pltpu.PrefetchScalarGridSpec(nu...  27.8 us
    pallas_call x3, Pallas kernels, permute_rows(): pl.pallas_call(permute_kernel, grid=(n_rows // tile,), in_specs=[pl.Block...  25.4 us
    pallas_call x1, Pallas kernels, unpermute_rows(): pl.pallas_call(unpermute_kernel, grid=(tok_count // PERM_TILE,), in_specs...  23.2 us
  transfers between devices with their start and end apart: 10, of which 5 were waited for; matrix products, arithmetic and copies ran while one was open for 1% of the time, Pallas kernels for 48%

profile of v3, /device:TPU:9, one launch (start us, length us, event | category | flops | bytes accessed | tf_op | source)
XLA Modules:
  0.0 505.7 jit_solution(3339044165852931421)
XLA Ops:
  7.2 1.1 convert_reduce_fusion.2
  8.7 1.0 fusion.41
  11.0 6.6 %permute.3 = bf16[408,1536]{1,0:T(8,128)(2,1)} custom-call(s32[1,2048]{1,0:T(1,128)} %get-tuple-element.377.pos_ref, bf16[2048,768]{1,0:T(8,128)(2,1)} %x_ref.5, bf16[2048,768]{1,0:T(8,128)(2,1)} %gy_ref.5, bf16[8,1536]{1,0:T(8,128)(2,1)} %pad.4.refs_0_), custom_call_target="tpu_custom_call" | custom-call | flops 2516582400 | bytes 16000000 | tf_op jit(solution)/shard_map/permute/pallas_call | solution.py:81
  17.7 28.7 %collective-permute-done.2 = bf16[51,8,1536]{2,1,0:T(8,128)(2,1)} collective-permute-done((bf16[51,8,1536]{2,1,0:T(8,128)(2,1)}, bf16[51,8,1536]{2,1,0:T(8,128)(2,1)}, u32[]{:S(2)}, u32[]{:S(2)}) %collective-permute-start.2) | collective-permute-done | bytes 1253408 | tf_op jit(solution)/shard_map/ppermute | solution.py:757
  46.5 9.5 %permute.5 = bf16[896,1536]{1,0:T(8,128)(2,1)} custom-call(s32[1,2048]{1,0:T(1,128)} %bitcast.213, bf16[2048,768]{1,0:T(8,128)(2,1)S(1)} %copy-done.2, bf16[2048,768]{1,0:T(8,128)(2,1)} %gy_ref.5), custom_call_target="tpu_custom_call" | custom-call | flops 5637144576 | bytes 16000000 | tf_op jit(solution)/shard_map/permute/pallas_call | solution.py:81
  56.0 5.5 %all-to-all-start.5 = ((bf16[8,112,1536]{2,1,0:T(8,128)(2,1)}), bf16[8,112,1536]{2,1,0:T(8,128)(2,1)}, u32[]{:S(2)}, u32[]{:S(2)}) async-start(bf16[8,112,1536]{2,1,0:T(8,128)(2,1)} %bitcast.205), calls=%async_computation.5 | async-start | bytes 5505024 | tf_op jit(solution)/shard_map/all_to_all | solution.py:752
  61.6 9.3 %permute.4 = bf16[896,1536]{1,0:T(8,128)(2,1)} custom-call(s32[1,2048]{1,0:T(1,128)} %get-tuple-element.376.pos_ref, bf16[2048,768]{1,0:T(8,128)(2,1)S(1)} %copy-done.2, bf16[2048,768]{1,0:T(8,128)(2,1)} %gy_ref.5), custom_call_target="tpu_custom_call" | custom-call | flops 5637144576 | bytes 16000000 | tf_op jit(solution)/shard_map/permute/pallas_call | solution.py:81
  70.9 31.2 %all-to-all-done.5 = bf16[8,112,1536]{2,1,0:T(8,128)(2,1)} async-done(((bf16[8,112,1536]{2,1,0:T(8,128)(2,1)}), bf16[8,112,1536]{2,1,0:T(8,128)(2,1)}, u32[]{:S(2)}, u32[]{:S(2)}) %all-to-all-start.5) | async-done | bytes 2752544 | tf_op jit(solution)/shard_map/all_to_all | solution.py:752
  102.1 7.5 %all-to-all-start.4 = ((bf16[8,112,1536]{2,1,0:T(8,128)(2,1)}), bf16[8,112,1536]{2,1,0:T(8,128)(2,1)}, u32[]{:S(2)}, u32[]{:S(2)}) async-start(bf16[8,112,1536]{2,1,0:T(8,128)(2,1)} %bitcast.204), calls=%async_computation.4 | async-start | bytes 5505024 | tf_op jit(solution)/shard_map/all_to_all | solution.py:752
  109.9 0.8 copy.49.wg_ref.refs_3_
  111.3 28.4 %own_base.2 = (bf16[8,4,56,1536]{3,2,1,0:T(8,128)(2,1)}, bf16[1792,768]{1,0:T(8,128)(2,1)}, bf16[1792,768]{1,0:T(8,128)(2,1)}, bf16[1792,3072]{1,0:T(8,128)(2,1)...) custom-call(s32[1]{0:T(128)} %bitcast.54.lead_ref.first_ref, ...), custom_call_target="tpu_custom_call" | custom-call | flops 16999999488 | bytes 40000000 | tf_op jit(solution)/shard_map/own_base/pallas_call | solution.py:202
  139.7 13.4 %all-to-all-done.4 = bf16[8,112,1536]{2,1,0:T(8,128)(2,1)} async-done(((bf16[8,112,1536]{2,1,0:T(8,128)(2,1)}), bf16[8,112,1536]{2,1,0:T(8,128)(2,1)}, u32[]{:S(2)}, u32[]{:S(2)}) %all-to-all-start.4) | async-done | bytes 2752544 | tf_op jit(solution)/shard_map/all_to_all | solution.py:752
  153.1 28.8 %own_base.3 = (bf16[8,4,56,1536]{3,2,1,0:T(8,128)(2,1)}, bf16[1792,768]{1,0:T(8,128)(2,1)}, bf16[1792,768]{1,0:T(8,128)(2,1)}, bf16[1792,3072]{1,0:T(8,128)(2,1)...) custom-call(s32[1]{0:T(128)S(6)} %add.209.first_ref, ...), custom_call_target="tpu_custom_call", output_to_operand_aliasing={{0}: (6, {}), {1}: (7, {}), {2}: (8, {}), {3}: (9, {}), {4}... | custom-call | flops 16999999488 | bytes 40000000 | tf_op jit(solution)/shard_map/own_base/pallas_call | solution.py:202
  181.9 3.1 shard_map.102
  185.0 27.8 %own_over.1 = (bf16[408,8,1536]{2,1,0:T(8,128)(2,1)}, bf16[1664,768]{1,0:T(8,128)(2,1)}, bf16[1664,768]{1,0:T(8,128)(2,1)}, bf16[1664,3072]{1,0:T(8,128)(2,1)}, ...) custom-call(s32[5,8]{1,0:T(8,128)} %get-tuple-element.221.tab_ref, ...), custom_call_target="tpu_custom_call", output_to_operand_aliasing={{0}: (8, {})} | custom-call | flops 10000000000 | bytes 40000000 | tf_op jit(solution)/shard_map/own_over/pallas_call | solution.py:308
  213.5 17.3 %collective-permute-start.3 = (bf16[8,112,1536]{2,1,0:T(8,128)(2,1)}, bf16[8,112,1536]{2,1,0:T(8,128)(2,1)}, u32[]{:S(2)}, u32[]{:S(2)}) collective-permute-start(bf16[8,112,1536]{2,1,0:T(8,128)(2,1)} %all-to-all-done.5), channel_id=1, source_target_pairs={{0,8},{8,0},{1,9},{9,1},{2,10},{10,2},{3,11},{11,3},{4,12},{12,4},... | collective-permute-start | bytes 8257544 | tf_op jit(solution)/shard_map/ppermute | solution.py:753
  230.8 4.5 shard_map.101
  236.0 4.6 all-to-all-start.6
  240.7 55.6 %collective-permute-done.3 = bf16[8,112,1536]{2,1,0:T(8,128)(2,1)} collective-permute-done((bf16[8,112,1536]{2,1,0:T(8,128)(2,1)}, bf16[8,112,1536]{2,1,0:T(8,128)(2,1)}, u32[]{:S(2)}, u32[]{:S(2)}) %collective-permute-start.3) | collective-permute-done | bytes 2752544 | tf_op jit(solution)/shard_map/ppermute | solution.py:753
  296.2 42.7 %collective-permute-done.4 = bf16[8,112,1536]{2,1,0:T(8,128)(2,1)} collective-permute-done((bf16[8,112,1536]{2,1,0:T(8,128)(2,1)}, bf16[8,112,1536]{2,1,0:T(8,128)(2,1)}, u32[]{:S(2)}, u32[]{:S(2)}) %collective-permute-start.4) | collective-permute-done | bytes 2752544 | tf_op jit(solution)/shard_map/ppermute | solution.py:753
  338.9 133.4 %grad_pass.1 = (f32[4,768,3072]{2,1,0:T(8,128)}, f32[4,3072,768]{2,1,0:T(8,128)}) custom-call(s32[8,24]{1,0:T(8,128)} %get-tuple-element.228.tab_ref, s32[192]{0:T(256)} %get-tuple-element.229.runs_ref, s32[1]{0:T(128)} %bitcast.54.lead_ref.first_ref, bf16[1792,768]{1,0:T(8,128)(2,1)} %get-tuple-element.230.xb_ref, ...), custom_call_target="tpu_custom_call" | custom-call | flops 70000001024 | bytes 150000000 | tf_op jit(solution)/shard_map/grad_pass/pallas_call | solution.py:469
  472.4 2.1 reduce_sum.84
  474.6 23.2 %unpermute.1 = (bf16[2048,768]{1,0:T(8,128)(2,1)}, bf16[2048,768]{1,0:T(8,128)(2,1)}) custom-call(s32[1,2048]{1,0:T(1,128)} %bitcast.214, bf16[8,224,1536]{2,1,0:T(8,128)(2,1)} %all-to-all-done.6.refs_0_.refs_1_, bf16[8,224,1536]{2,1,0:T(8,128)(2,1)} %all-to-all-done.6.refs_0_.refs_1_, bf16[408,1536]{1,0:T(8,128)(2,1)} %bitcast.215), custom_call_target="tpu_custom_call" | custom-call | flops 14000000000 | bytes 16000000 | tf_op jit(solution)/shard_map/unpermute/pallas_call | solution.py:118
  497.8 1.2 while.34
  (39 shorter events, 3.4 us)
Async XLA Ops:
  7.2 39.3 %copy-start.2 = (bf16[2048,768]{1,0:T(8,128)(2,1)S(1)}, bf16[2048,768]{1,0:T(8,128)(2,1)}, u32[]{:S(2)}) copy-start(bf16[2048,768]{1,0:T(8,128)(2,1)} %x_ref.5) | copy-start | bytes 9437188
  7.2 174.7 %all-gather.10.cloned.1.call-start = ((), (), s32[]{:S(2)}) async-start(), calls=%async_computation.9 | async-start | bytes 11280384 | tf_op jit(solution)/shard_map/all_gather | solution.py:756
  9.7 36.7 %copy-start.23 = (s32[16,128]{1,0:T(8,128)}, s32[16,128]{1,0:T(8,128)S(1)}, u32[]{:S(2)}) copy-start(s32[16,128]{1,0:T(8,128)S(1)} %convert_element_type.123) | copy-start | bytes 24580
  17.6 213.2 %all-gather.12.cloned.1.call-start = ((), (), s32[]{:S(2)}) async-start(), calls=%async_computation.11 | async-start | bytes 11280384 | tf_op jit(solution)/shard_map/all_gather | solution.py:758
  17.6 28.8 %collective-permute-start.2 = (bf16[51,8,1536]{2,1,0:T(8,128)(2,1)}, bf16[51,8,1536]{2,1,0:T(8,128)(2,1)}, u32[]{:S(2)}, u32[]{:S(2)}) collective-permute-start(bf16[51,8,1536]{2,1,0:T(8,128)(2,1)} %bitcast.208), channel_id=1, source_target_pairs={{0,8},{8,0},{1,9},{9,1},{2,10},{10,2},{3,11},{11,3},{4,12},{12,4},... | collective-permute-start | bytes 3760136 | tf_op jit(solution)/shard_map/ppermute | solution.py:757
  56.0 46.0 %all-to-all-start.5 = ((bf16[8,112,1536]{2,1,0:T(8,128)(2,1)}), bf16[8,112,1536]{2,1,0:T(8,128)(2,1)}, u32[]{:S(2)}, u32[]{:S(2)}) async-start(bf16[8,112,1536]{2,1,0:T(8,128)(2,1)} %bitcast.205), calls=%async_computation.5 | async-start | bytes 5505024 | tf_op jit(solution)/shard_map/all_to_all | solution.py:752
  61.6 48.3 %copy-start.12 = (bf16[768,32]{0,1:T(8,128)(2,1)S(1)}, bf16[768,32]{0,1:T(8,128)(2,1)}, u32[]{:S(2)}) copy-start(bf16[768,32]{0,1:T(8,128)(2,1)} %param.13) | copy-start | bytes 147460
  102.1 51.0 %all-to-all-start.4 = ((bf16[8,112,1536]{2,1,0:T(8,128)(2,1)}), bf16[8,112,1536]{2,1,0:T(8,128)(2,1)}, u32[]{:S(2)}, u32[]{:S(2)}) async-start(bf16[8,112,1536]{2,1,0:T(8,128)(2,1)} %bitcast.204), calls=%async_computation.4 | async-start | bytes 5505024 | tf_op jit(solution)/shard_map/all_to_all | solution.py:752
  109.6 362.8 %all-gather.14.cloned.1.call-start = ((), (), s32[]{:S(2)}) async-start(), calls=%async_computation.12 | async-start | bytes 1671168 | tf_op jit(solution)/shard_map/all_gather | solution.py:780
  212.9 261.7 %reduce-scatter.2.cloned.1.call-start = ((), (), s32[]{:S(2)}) async-start(), calls=%async_computation.10 | async-start | bytes 11280384 | tf_op jit(solution)/shard_map/reduce_scatter | solution.py:777
  213.5 82.8 %collective-permute-start.3 = (bf16[8,112,1536]{2,1,0:T(8,128)(2,1)}, bf16[8,112,1536]{2,1,0:T(8,128)(2,1)}, u32[]{:S(2)}, u32[]{:S(2)}) collective-permute-start(bf16[8,112,1536]{2,1,0:T(8,128)(2,1)} %all-to-all-done.5), channel_id=1, source_target_pairs={{0,8},{8,0},{1,9},{9,1},{2,10},{10,2},{3,11},{11,3},{4,12},{12,4},... | collective-permute-start | bytes 8257544 | tf_op jit(solution)/shard_map/ppermute | solution.py:753
  230.8 108.2 %collective-permute-start.4 = (bf16[8,112,1536]{2,1,0:T(8,128)(2,1)}, bf16[8,112,1536]{2,1,0:T(8,128)(2,1)}, u32[]{:S(2)}, u32[]{:S(2)}) collective-permute-start(bf16[8,112,1536]{2,1,0:T(8,128)(2,1)} %all-to-all-done.4), channel_id=1, source_target_pairs={{0,8},{8,0},{1,9},{9,1},{2,10},{10,2},{3,11},{11,3},{4,12},{12,4},... | collective-permute-start | bytes 8257544 | tf_op jit(solution)/shard_map/ppermute | solution.py:753
  236.0 238.5 %all-to-all-start.6 = ((bf16[8,224,1536]{2,1,0:T(8,128)(2,1)}), bf16[8,224,1536]{2,1,0:T(8,128)(2,1)}, u32[]{:S(2)}, u32[]{:S(2)}) async-start(bf16[8,224,1536]{2,1,0:T(8,128)(2,1)} %bitcast.197), calls=%async_computation.6 | async-start | bytes 11010048 | tf_op jit(solution)/shard_map/all_to_all | solution.py:774
  474.5 23.2 %copy-start.3 = (bf16[2048,768]{1,0:T(8,128)(2,1)S(1)}, bf16[2048,768]{1,0:T(8,128)(2,1)}, u32[]{:S(2)}) copy-start(bf16[2048,768]{1,0:T(8,128)(2,1)} %x_ref.5) | copy-start | bytes 9437188
  474.5 23.2 %copy-start.9 = (s32[2048]{0:T(1024)S(1)}, s32[2048]{0:T(1024)}, u32[]{:S(2)}) copy-start(s32[2048]{0:T(1024)} %param.12) | copy-start | bytes 24580
  474.6 23.2 %copy-start.13 = (bf16[768,32]{0,1:T(8,128)(2,1)S(1)}, bf16[768,32]{0,1:T(8,128)(2,1)}, u32[]{:S(2)}) copy-start(bf16[768,32]{0,1:T(8,128)(2,1)} %param.13) | copy-start | bytes 147460
Sparse Core Ops, SparseCore 0:
  17.7 76.2 all-gather.9
  95.8 93.0 all-gather.11
  213.0 66.6 all-gather.13
  283.1 72.7 reduce-scatter.1

commit v4 on v3

--- a/solution.py
+++ b/solution.py
@@ -16,9 +16,11 @@
 MAX_OVER_TILES = 8
 RUNS = 8
 RUN_SIZES = (16, 8, 4, 2, 1)
+EXPERT, COUNT, STORE, LAST, N_RUNS = range(5)
 TILE_GROUPS = 26
 TILE = TILE_GROUPS * GROUP
 PERM_TILE = 256
+TOKEN_TILE = 512
 CHUNK = 512
 ROW_CHUNK = 256
 CHUNKS = 2
@@ -31,8 +33,24 @@
 I32 = jnp.int32
 
 
+BY_ROWS = ((0,), (0,))
+BY_COLS = ((1,), (1,))
+
+
 def dot(a, b, dims=((1,), (0,))):
     return lax.dot_general(a, b, (dims, ((), ())), preferred_element_type=F32)
+
+
+def origin(*ids):
+    return 0, 0
+
+
+def step_id():
+    return pl.program_id(0)
+
+
+def step_count():
+    return pl.num_programs(0)
 
 
 def exclusive_cumsum(v, axis):
@@ -59,14 +77,15 @@
     base_at = (slot * base_rows).astype(F32)
     over_at = (n_experts * base_rows - base_rows + over_start * GROUP).astype(F32)
     row = jnp.sum(blocks.astype(F32) * (rank + jnp.where(rank < base_rows, base_at, over_at)), axis=2)
-    return groups, row.reshape(tok_count).astype(I32)
+    last_row = n_experts * base_rows + OVER_GROUPS * GROUP - 1
+    return groups, jnp.minimum(row, last_row).reshape(tok_count).astype(I32)
 
 
 def permute_kernel(pos_ref, x_ref, gy_ref, *refs):
     *tail, out_ref = refs
     d_model = x_ref.shape[1]
     rows = out_ref.shape[0] - sum(t.shape[0] for t in tail)
-    row_id = pl.program_id(0) * rows + lax.broadcasted_iota(I32, (rows, x_ref.shape[0]), 0)
+    row_id = step_id() * rows + lax.broadcasted_iota(I32, (rows, x_ref.shape[0]), 0)
     select = jnp.where(row_id == pos_ref[...], 1.0, 0.0).astype(BF16)
     out_ref[:rows, :d_model] = dot(select, x_ref[...]).astype(BF16)
     out_ref[:rows, d_model:] = dot(select, gy_ref[...]).astype(BF16)
@@ -82,10 +101,10 @@
         permute_kernel,
         grid=(n_rows // tile,),
         in_specs=[
-            pl.BlockSpec((1, tok_count), lambda i: (0, 0)),
-            pl.BlockSpec((tok_count, d_model), lambda i: (0, 0)),
-            pl.BlockSpec((tok_count, d_model), lambda i: (0, 0)),
-        ] + [pl.BlockSpec(t.shape, lambda i: (0, 0)) for t in tail],
+            pl.BlockSpec((1, tok_count), origin),
+            pl.BlockSpec((tok_count, d_model), origin),
+            pl.BlockSpec((tok_count, d_model), origin),
+        ] + [pl.BlockSpec(t.shape, origin) for t in tail],
         out_specs=pl.BlockSpec((tile + extra, 2 * d_model), lambda i: (i, 0)),
         out_shape=jax.ShapeDtypeStruct((n_rows + extra, 2 * d_model), BF16),
         cost_estimate=pl.CostEstimate(flops=4 * n_rows * tok_count * d_model, bytes_accessed=16_000_000, transcendentals=0),
@@ -93,20 +112,54 @@
     )((pos - first_row).reshape(1, tok_count), x, gy, *tail)
 
 
-def unpermute_kernel(pos_ref, *refs):
-    *parts, out_ref, dx_ref = refs
+def unpermute_kernel(pos_ref, base_ref, over_ref, out_ref, dx_ref, out_rows, dx_rows, out_tile, dx_tile):
+    step = step_id()
     toks, d_model = out_ref.shape
-    pos = jnp.transpose(jnp.broadcast_to(pos_ref[...], (8, toks)))[:, :1]
-    first, out, dx = 0, 0.0, 0.0
-    for part in parts:
-        rows = part[...].reshape(-1, 2 * d_model)
-        row_id = lax.broadcasted_iota(I32, (toks, rows.shape[0]), 1) + first
-        select = jnp.where(row_id == pos, 1.0, 0.0).astype(BF16)
-        out += dot(select, rows[:, :d_model])
-        dx += dot(select, rows[:, d_model:])
-        first += rows.shape[0]
-    out_ref[...] = out.astype(BF16)
-    dx_ref[...] = dx.astype(BF16)
+    base_steps = 2 * CHUNKS
+    block = base_ref.shape[0] * base_ref.shape[1]
+    lanes = 128
+    parts = d_model // lanes
+
+    def spread(ref, first):
+        n = ref.shape[0]
+        size = max(k for k in range(GROUP, 65, GROUP) if n % k == 0)
+
+        @pl.loop(0, n // size)
+        def _(i):
+            at = pl.multiple_of(i * size, 8)
+            rows = ref[pl.ds(at, size), :].astype(F32)
+            for c in range(parts):
+                to = pl.ds((first + at) * 8 + c, size, stride=8)
+                out_rows[to, :] = rows[:, c * lanes:(c + 1) * lanes]
+                dx_rows[to, :] = rows[:, d_model + c * lanes:d_model + (c + 1) * lanes]
+
+    @pl.when(step < base_steps)
+    def _():
+        for d in range(base_ref.shape[0]):
+            spread(base_ref.at[d], step * block + d * base_ref.shape[1])
+
+    @pl.when(step == base_steps)
+    def _():
+        spread(over_ref, base_steps * block)
+
+    @pl.when(step > base_steps)
+    def _():
+        first = (step - base_steps - 1) * toks
+
+        @pl.loop(0, toks // 16)
+        def _(i):
+            rows = [pl.multiple_of(pos_ref[first + i * 16 + u] * 8, 8) for u in range(16)]
+            outs = [out_rows[pl.ds(r, 8), :] for r in rows]
+            dxs = [dx_rows[pl.ds(r, 8), :] for r in rows]
+            for u in range(16):
+                to = pl.ds(pl.multiple_of((i * 16 + u) * 8, 8), 8)
+                out_tile[to, :] = outs[u]
+                dx_tile[to, :] = dxs[u]
+
+        for c in range(parts):
+            cols = slice(c * lanes, (c + 1) * lanes)
+            out_ref[:, cols] = out_tile[pl.ds(c, toks, stride=8), :].astype(BF16)
+            dx_ref[:, cols] = dx_tile[pl.ds(c, toks, stride=8), :].astype(BF16)
 
 
 def unpermute_rows(pos, base, over):
@@ -114,18 +167,27 @@
     tok_count = pos.shape[0]
     d_model = width // 2
     shape = jax.ShapeDtypeStruct((tok_count, d_model), BF16)
-    chunk = (n_own, n_slot // CHUNKS, width)
+    base_steps = 2 * CHUNKS
+    n_rows = n_own * n_slot + over.shape[0]
+    token_tile = lambda i, pos: (jnp.maximum(i - base_steps - 1, 0), 0)
+    part = lambda i: jnp.minimum(i, base_steps - 1)
     return pl.pallas_call(
         unpermute_kernel,
-        grid=(tok_count // PERM_TILE,),
-        in_specs=[pl.BlockSpec((1, PERM_TILE), lambda i: (0, i))]
-        + [pl.BlockSpec(chunk, lambda i, c=c: (0, c, 0)) for c in range(CHUNKS)]
-        + [pl.BlockSpec(over.shape, lambda i: (0, 0))],
-        out_specs=[pl.BlockSpec((PERM_TILE, d_model), lambda i: (i, 0))] * 2,
+        grid_spec=pltpu.PrefetchScalarGridSpec(
+            num_scalar_prefetch=1,
+            grid=(base_steps + 1 + tok_count // TOKEN_TILE,),
+            in_specs=[
+                pl.BlockSpec((n_own // 2, n_slot // CHUNKS, width), lambda i, pos: (part(i) % 2, part(i) // 2, 0)),
+                pl.BlockSpec(over.shape, origin),
+            ],
+            out_specs=[pl.BlockSpec((TOKEN_TILE, d_model), token_tile)] * 2,
+            scratch_shapes=[pltpu.VMEM((n_rows * 8, 128), F32)] * 2 + [pltpu.VMEM((TOKEN_TILE * 8, 128), F32)] * 2,
+        ),
         out_shape=[shape, shape],
-        cost_estimate=pl.CostEstimate(flops=14_000_000_000, bytes_accessed=16_000_000, transcendentals=0),
+        compiler_params=pltpu.CompilerParams(dimension_semantics=('arbitrary',)),
+        cost_estimate=pl.CostEstimate(flops=10_000_000_000, bytes_accessed=16_000_000, transcendentals=0),
         name='unpermute',
-    )(pos.reshape(1, tok_count), *[base] * CHUNKS, over)
+    )(pos, base, over)
 
 
 def gate(x, wg, expert):
@@ -139,7 +201,7 @@
 
 def activations(x, dy, w_up, w_down, cols):
     a = dot(x, w_up[:, cols])
-    dh = dot(dy, w_down[cols, :], ((1,), (1,)))
+    dh = dot(dy, w_down[cols, :], BY_COLS)
     cubic = (SQRT_2_PI * CUBIC) * (a * a)
     half = 0.5 + 0.5 * jnp.tanh(a * (SQRT_2_PI + cubic))
     h = a * half
@@ -159,18 +221,18 @@
         h_ref[:, cols] = h
         da_ref[:, cols] = da
     y = dot(h_ref[...], w_down[...]).astype(BF16).astype(F32)
-    dxe = dot(da_ref[...], w_up[...], ((1,), (1,))).astype(BF16).astype(F32)
+    dxe = dot(da_ref[...], w_up[...], BY_COLS).astype(BF16).astype(F32)
     d_gate = jnp.sum(gy_full * y, axis=1, keepdims=True)
     d_logit = ((d_gate * gate_val) * (onehot.astype(F32) - prob)).astype(BF16)
-    dwg_ref[...] += dot(d_logit, x, ((0,), (0,)))
+    dwg_ref[...] += dot(d_logit, x, BY_ROWS)
     out = (gate_val * y).astype(BF16)
-    dx = (dxe + dot(d_logit, wg_ref[...], ((1,), (1,)))).astype(BF16)
+    dx = (dxe + dot(d_logit, wg_ref[...], BY_COLS)).astype(BF16)
     return out, dx
 
 
 def own_base_kernel(first_ref, rows_ref, wg_ref, up_ref, down_ref, dwg_in, *refs):
     od_ref, x_ref, dy_ref, h_ref, da_ref, dwg_ref, zero_ref = refs[-7:]
-    step = pl.program_id(0)
+    step = step_id()
     d_model = wg_ref.shape[0]
 
     @pl.when(step == 0)
@@ -195,7 +257,6 @@
     lead = chunk * count
     row_spec = lambda at: pl.BlockSpec((n_src, 1, seg, width), lambda e, first: (0, at + e, 0, 0))
     store_spec = lambda cols: pl.BlockSpec((tile, cols), lambda e, first: (lead + e, 0))
-    const = lambda e, first: (0, 0)
     rows_of = lambda cols: jax.ShapeDtypeStruct((local * tile, cols), BF16)
     zero_block = (over_shape[0] // local,) + over_shape[1:]
     kept = [] if stores is None else list(stores)
@@ -206,13 +267,13 @@
             grid=(count,),
             in_specs=[
                 row_spec(0),
-                pl.BlockSpec(wg.shape, const),
+                pl.BlockSpec(wg.shape, origin),
                 pl.BlockSpec((1, d_model, d_ff), lambda e, first: (lead + e, 0, 0)),
                 pl.BlockSpec((1, d_ff, d_model), lambda e, first: (lead + e, 0, 0)),
-                pl.BlockSpec(dwg.shape, const),
+                pl.BlockSpec(dwg.shape, origin),
             ] + [pl.BlockSpec(memory_space=pl.ANY)] * len(kept),
             out_specs=[row_spec(lead), store_spec(d_model), store_spec(d_model), store_spec(d_ff), store_spec(d_ff),
-                       pl.BlockSpec(dwg.shape, const), pl.BlockSpec(zero_block, lambda e, first: (lead + e, 0, 0))],
+                       pl.BlockSpec(dwg.shape, origin), pl.BlockSpec(zero_block, lambda e, first: (lead + e, 0, 0))],
         ),
         out_shape=[jax.ShapeDtypeStruct((n_src, local, seg, width), BF16), rows_of(d_model), rows_of(d_model), rows_of(d_ff), rows_of(d_ff),
                    jax.ShapeDtypeStruct(dwg.shape, F32), jax.ShapeDtypeStruct(over_shape, BF16)],
@@ -227,7 +288,7 @@
 def run_copies(runs_ref, tile, n_runs, hbm, buf, sem, to_hbm):
     def body(r, carry):
         at = (tile * RUNS + r) * 3
-        first, left, slot = runs_ref[at], runs_ref[at + 1], runs_ref[at + 2]
+        first, left, slot = (runs_ref[at + k] for k in range(3))
         for size in RUN_SIZES:
             take = left >= size
 
@@ -260,39 +321,39 @@
 def own_over_kernel(tab_ref, runs_ref, first_ref, rows_hbm, wg_ref, up_ref, down_ref, dwg_in, zero_od,
                     od_hbm, x_ref, dy_ref, h_ref, da_ref, dwg_ref, in_buf, out_buf, in_sem, out_sem):
     del zero_od
-    step = pl.program_id(0)
+    step = step_id()
     d_model = wg_ref.shape[0]
     slot = step % 2
-    count = tab_ref[1, step]
+    count = tab_ref[COUNT, step]
 
     @pl.when(step == 0)
     def _():
         dwg_ref[...] = dwg_in[...]
-        run_copies(runs_ref, 0, tab_ref[4, 0], rows_hbm, in_buf.at[0], in_sem.at[0], False)
+        run_copies(runs_ref, 0, tab_ref[N_RUNS, 0], rows_hbm, in_buf.at[0], in_sem.at[0], False)
 
     @pl.when(count > 0)
     def _():
         run_waits(count, rows_hbm, in_buf.at[slot], in_sem.at[slot], False)
 
-        @pl.when(step + 1 < pl.num_programs(0))
+        @pl.when(step + 1 < step_count())
         def _():
-            run_copies(runs_ref, step + 1, tab_ref[4, step + 1], rows_hbm, in_buf.at[1 - slot], in_sem.at[1 - slot], False)
+            run_copies(runs_ref, step + 1, tab_ref[N_RUNS, step + 1], rows_hbm, in_buf.at[1 - slot], in_sem.at[1 - slot], False)
 
         rows = tile_rows(in_buf.at[slot], count)
         x = rows[:, :d_model]
         x_ref[...] = x
-        out, dx = own_rows_step(x, rows[:, d_model:], first_ref[0] + tab_ref[0, step], wg_ref,
+        out, dx = own_rows_step(x, rows[:, d_model:], first_ref[0] + tab_ref[EXPERT, step], wg_ref,
                                 up_ref.at[0], down_ref.at[0], (dy_ref, h_ref, da_ref), dwg_ref)
 
         @pl.when(step > 0)
         def _():
-            run_waits(tab_ref[1, step - 1], od_hbm, out_buf, out_sem, True)
+            run_waits(tab_ref[COUNT, step - 1], od_hbm, out_buf, out_sem, True)
 
         out_buf[:, :, :d_model] = out.reshape(TILE_GROUPS, GROUP, d_model)
         out_buf[:, :, d_model:] = dx.reshape(TILE_GROUPS, GROUP, d_model)
-        run_copies(runs_ref, step, tab_ref[4, step], od_hbm, out_buf, out_sem, True)
-
-        @pl.when(tab_ref[3, step] == 1)
+        run_copies(runs_ref, step, tab_ref[N_RUNS, step], od_hbm, out_buf, out_sem, True)
+
+        @pl.when(tab_ref[LAST, step] == 1)
         def _():
             run_waits(count, od_hbm, out_buf, out_sem, True)
 
@@ -302,8 +363,7 @@
     width = rows.shape[-1]
     n_tiles = table.shape[1]
     hbm = pl.BlockSpec(memory_space=pl.ANY)
-    const = lambda i, tab, runs, first: (0, 0)
-    store_spec = lambda cols: pl.BlockSpec((TILE, cols), lambda i, tab, runs, first: (tab[2, i], 0))
+    store_spec = lambda cols: pl.BlockSpec((TILE, cols), lambda i, tab, runs, first: (tab[STORE, i], 0))
     rows_of = lambda cols: jax.ShapeDtypeStruct((n_tiles * TILE, cols), BF16)
     return pl.pallas_call(
         own_over_kernel,
@@ -312,14 +372,14 @@
             grid=(n_tiles,),
             in_specs=[
                 hbm,
-                pl.BlockSpec(wg.shape, const),
-                pl.BlockSpec((1, d_model, d_ff), lambda i, tab, runs, first: (tab[0, i], 0, 0)),
-                pl.BlockSpec((1, d_ff, d_model), lambda i, tab, runs, first: (tab[0, i], 0, 0)),
-                pl.BlockSpec(dwg.shape, const),
+                pl.BlockSpec(wg.shape, origin),
+                pl.BlockSpec((1, d_model, d_ff), lambda i, tab, runs, first: (tab[EXPERT, i], 0, 0)),
+                pl.BlockSpec((1, d_ff, d_model), lambda i, tab, runs, first: (tab[EXPERT, i], 0, 0)),
+                pl.BlockSpec(dwg.shape, origin),
                 hbm,
             ],
             out_specs=[hbm, store_spec(d_model), store_spec(d_model), store_spec(d_ff), store_spec(d_ff),
-                       pl.BlockSpec(dwg.shape, const)],
+                       pl.BlockSpec(dwg.shape, origin)],
             scratch_shapes=[
                 pltpu.VMEM((2, TILE_GROUPS, GROUP, width), BF16),
                 pltpu.VMEM((TILE_GROUPS, GROUP, width), BF16),
@@ -342,9 +402,9 @@
 def grad_kernel(tab_ref, runs_ref, first_ref, xb_ref, dyb_ref, hb_ref, dab_ref, xo_ref, dyo_ref, ho_ref, dao_ref, *refs):
     *base_hbm, over_hbm, wg_ref, up_hbm, down_hbm, dup_hbm, ddown_hbm = refs[:-12]
     dup, ddown, up_buf, down_buf, h_buf, da_buf, base_buf, in_buf, w_sems, base_sem, in_sem, out_sems = refs[-12:]
-    step = pl.program_id(0)
+    step = step_id()
     d_model, d_ff = dup.shape
-    expert, kind, last, count = tab_ref[0, step], tab_ref[1, step], tab_ref[2, step], tab_ref[4, step]
+    expert, kind, last, _, count = (tab_ref[row, step] for row in range(5))
     n_local = dup_hbm.shape[0]
     base_rows = h_buf.shape[0]
 
@@ -361,13 +421,13 @@
     def add_down(dy, h_src, add):
         for lo in range(0, d_ff, CHUNK):
             cols = pl.ds(lo, CHUNK)
-            term = dot(h_src[:, cols], dy, ((0,), (0,)))
+            term = dot(h_src[:, cols], dy, BY_ROWS)
             ddown[cols, :] = ddown[cols, :] + term if add else term
 
     def add_up(x, da_src, add):
         for lo in range(0, d_ff, CHUNK):
             cols = pl.ds(lo, CHUNK)
-            term = dot(x, da_src[:, cols], ((0,), (0,)))
+            term = dot(x, da_src[:, cols], BY_ROWS)
             dup[:, cols] = dup[:, cols] + term if add else term
 
     def accumulate(x, dy, h_src, da_src):
@@ -398,9 +458,9 @@
         return pltpu.make_async_copy(chunk.at[:, e % chunk.shape[1]], base_buf, base_sem)
 
     ahead = step + 1
-    ahead_at = jnp.minimum(ahead, pl.num_programs(0) - 1)
-
-    @pl.when((ahead < pl.num_programs(0)) & (tab_ref[1, ahead_at] == OTHER_OVER))
+    ahead_at = jnp.minimum(ahead, step_count() - 1)
+
+    @pl.when((ahead < step_count()) & (tab_ref[1, ahead_at] == OTHER_OVER))
     def _():
         run_copies(runs_ref, tab_ref[5, ahead_at], tab_ref[7, ahead_at], over_hbm, in_buf.at[ahead % 2], in_sem.at[ahead % 2],
                    False)
@@ -482,7 +542,7 @@
                 over_spec(d_ff),
                 *[hbm for _ in base],
                 hbm,
-                pl.BlockSpec(wg.shape, lambda i, tab, ids, first: (0, 0)),
+                pl.BlockSpec(wg.shape, origin),
                 hbm,
                 hbm,
             ],
@@ -532,9 +592,8 @@
         @pl.when((groups > 0) & (tile < MAX_OVER_TILES))
         def _():
             at = (tile * RUNS + n_runs[tile]) * 3
-            runs[at] = begin
-            runs[at + 1] = groups
-            runs[at + 2] = slot
+            for k, value in enumerate((begin, groups, slot)):
+                runs[at + k] = value
             n_runs[tile] = n_runs[tile] + 1
             count[tile] = count[tile] + groups
 
@@ -572,14 +631,12 @@
     spans, n_tiles = fill_tiles(count_ref.shape[0], local, lead_ref[0], size_s, first_s, runs_ref, n_runs.at[0], count.at[0])
     last = jnp.maximum(n_tiles - 1, 0)
     for t in range(MAX_OVER_TILES):
-        tab_ref[0, t] = local - 1
-        tab_ref[1, t] = count[0, t]
-        tab_ref[2, t] = jnp.minimum(t, last)
-        tab_ref[3, t] = (last == t).astype(I32)
-        tab_ref[4, t] = n_runs[0, t]
+        row = (local - 1, count[0, t], jnp.minimum(t, last), (last == t).astype(I32), n_runs[0, t])
+        for k, value in enumerate(row):
+            tab_ref[k, t] = value
     for e, (tile, tiles) in enumerate(spans):
         def body(k, c, e=e, tile=tile):
-            tab_ref[0, tile + k] = e
+            tab_ref[EXPERT, tile + k] = e
             return c
 
         lax.fori_loop(0, tiles, body, 0)
@@ -598,15 +655,11 @@
     max_steps = tab_ref.shape[1]
 
     def emit(step, expert, kind, own_tile, other_tile, next_base):
-        over = (kind == OTHER_OVER).astype(I32) if not isinstance(kind, int) else int(kind == OTHER_OVER)
-        tab_ref[0, step] = expert
-        tab_ref[1, step] = kind
-        tab_ref[2, step] = 0
-        tab_ref[3, step] = jnp.clip(own_tile, 0, MAX_OVER_TILES - 1)
-        tab_ref[4, step] = count[1, other_tile] * over
-        tab_ref[5, step] = other_tile
-        tab_ref[6, step] = next_base
-        tab_ref[7, step] = n_runs[1, other_tile] * over
+        over = int(kind == OTHER_OVER)
+        row = (expert, kind, 0, jnp.clip(own_tile, 0, MAX_OVER_TILES - 1), count[1, other_tile] * over, other_tile, next_base,
+               n_runs[1, other_tile] * over)
+        for k, value in enumerate(row):
+            tab_ref[k, step] = value
 
     step = jnp.int32(0)
     for e in range(local):
@@ -695,10 +748,10 @@
         hid_full, gelu_back = jax.vjp(jax.nn.gelu, pre_act)
         hidden = hid_full.astype(BF16)
         out_rows = dot(hidden, down).astype(BF16)
-        d_pre = gelu_back(dot(grad, down, ((1,), (1,))))[0].astype(BF16)
-        grad_down = dot(hidden, grad, ((0,), (0,)))
-        grad_up = dot(rows, d_pre, ((0,), (0,)))
-        d_rows = dot(d_pre, up, ((1,), (1,))).astype(BF16)
+        d_pre = gelu_back(dot(grad, down, BY_COLS))[0].astype(BF16)
+        grad_down = dot(hidden, grad, BY_ROWS)
+        grad_up = dot(rows, d_pre, BY_ROWS)
+        d_rows = dot(d_pre, up, BY_COLS).astype(BF16)
         shape = (ep_size, cap_rows, d_model)
         return carry, (out_rows.reshape(shape), d_rows.reshape(shape), grad_up, grad_down)
 
@@ -710,9 +763,9 @@
     dx_expert = combine(d_rows)
     d_gate = jnp.sum(gy_full * y_tok.astype(F32), axis=1)
     d_logit = ((d_gate * gate_val)[:, None] * (onehot.astype(F32) - router_prob)).astype(BF16)
-    dx_router = dot(d_logit, w_gate, ((1,), (1,)))
+    dx_router = dot(d_logit, w_gate, BY_COLS)
     grad_x = (dx_expert.astype(F32) + dx_router).astype(BF16)
-    grad_gate = dot(x_loc, d_logit, ((0,), (0,)))
+    grad_gate = dot(x_loc, d_logit, BY_ROWS)
 
     def sum_dp(term):
         total = term
@@ -777,7 +830,15 @@
         over_back = lax.psum_scatter(od_over.reshape(ep_size, SENT_GROUPS, GROUP, width), 'ep', scatter_dimension=0)
         d_up, d_down = grad_pass(gtable, runs_z, first_expert, base_store, (x_o, dy_o, h_o, da_o), base_z, over_z,
                                  w_gate, w_up, w_down)
-        d_gate = jnp.sum(lax.all_gather(dwg, ('dp', 'ep')), axis=0).T
+
+        def from_peer(axis, bits, value):
+            return lax.ppermute(value, axis, [(i, i ^ bits) for i in range(mesh.shape[axis])])
+
+        pair = dwg + from_peer('ep', 1, dwg)
+        near = pair + from_peer('ep', 2, pair)
+        far = from_peer('ep', 4, pair) + from_peer('ep', 6, pair)
+        plane = near + far
+        d_gate = (plane + from_peer('dp', 1, plane)).T
         moe_out, grad_x = unpermute_rows(pos, base_back, over_back.reshape(-1, width))
         sparse = (moe_out, grad_x, d_up, d_down, d_gate)
 

time: 514 us -> 517 us (level)
  starting transfers between devices: 35.5 us -> 45.8 us
  Pallas kernels: 275 us -> 266 us
    ppermute x0 -> x5, waiting for transfers between devices: none -> 100 us  [from_peer(): lax.ppermute(value, axis, [(i, i ^ bits) for i in range(mesh.shape[axis])])]
    ppermute x2, waiting for transfers between devices: 98.3 us -> 0.01 us  [local_step(): base_z.append(lax.ppermute(base[c], 'dp', swap).reshape(slots))]
    pallas_call x1, Pallas kernels: 23.2 us -> 15.1 us  [unpermute_rows(): pl.pallas_call(unpermute_kernel, grid_spec=pltpu.PrefetchScalarGridSpec(n...]
    all_to_all x1, starting transfers between devices: 4.65 us -> 10.7 us  [local_step(): lax.all_to_all(od.reshape(ep_size, -1, width), 'ep', 0, 0, tiled=True)]
  transfers between devices with their start and end apart: 10 -> 14, of which waited for: 5 -> 7; matrix products, arithmetic and copies ran while one was open for 1% -> 1% of each run, Pallas kernels for 48% -> 48%
where the time goes in v4:
time: 517 us; the launch traced here: 509 us
  Pallas kernels  266 us (51%)
  waiting for transfers between devices  173 us (33%)
  starting transfers between devices  45.8 us (9%)
  between operations  14.8 us (3%)
    pallas_call x1, Pallas kernels, grad_pass(): pl.pallas_call(grad_kernel, grid_spec=pltpu.PrefetchScalarGridSpec(num_sc...  133 us
    ppermute x5, waiting for transfers between devices, from_peer(): lax.ppermute(value, axis, [(i, i ^ bits) for i in range(mesh.shape[axis])])  100 us
    pallas_call x2, Pallas kernels, own_base_pass(): pl.pallas_call(own_base_kernel, grid_spec=pltpu.PrefetchScalarGridSpec(nu...  57.3 us
    all_to_all x2, waiting for transfers between devices, local_step(): lax.all_to_all(sent.reshape(ep_size, -1, width), 'ep', 0, 0, tiled=True)  44.6 us
    ppermute x1, waiting for transfers between devices, local_step(): over_sent_z = lax.ppermute(over_sent, 'dp', swap)  28.7 us
    pallas_call x1, Pallas kernels, own_over_pass(): pl.pallas_call(own_over_kernel, grid_spec=pltpu.PrefetchScalarGridSpec(nu...  27.4 us
    pallas_call x3, Pallas kernels, permute_rows(): pl.pallas_call(permute_kernel, grid=(n_rows // tile,), in_specs=[pl.Block...  25.4 us
    ppermute x2, starting transfers between devices, local_step(): base_z.append(lax.ppermute(base[c], 'dp', swap).reshape(slots))  17.3 us
  transfers between devices with their start and end apart: 14, of which 7 were waited for; matrix products, arithmetic and copies ran while one was open for 1% of the time, Pallas kernels for 48%

profile of v4, /device:TPU:9, one launch (start us, length us, event | category | flops | bytes accessed | tf_op | source)
XLA Modules:
  0.0 508.9 jit_solution(8238842232598739730)
XLA Ops:
  11.5 6.6 %permute.3 = bf16[408,1536]{1,0:T(8,128)(2,1)} custom-call(s32[1,2048]{1,0:T(1,128)} %get-tuple-element.401.pos_ref, bf16[2048,768]{1,0:T(8,128)(2,1)} %x_ref.5, bf16[2048,768]{1,0:T(8,128)(2,1)} %gy_ref.5, bf16[8,1536]{1,0:T(8,128)(2,1)} %pad.4.refs_0_), custom_call_target="tpu_custom_call" | custom-call | flops 2516582400 | bytes 16000000 | tf_op jit(solution)/shard_map/permute/pallas_call | solution.py:100
  18.3 28.7 %collective-permute-done.2 = bf16[51,8,1536]{2,1,0:T(8,128)(2,1)} collective-permute-done((bf16[51,8,1536]{2,1,0:T(8,128)(2,1)}, bf16[51,8,1536]{2,1,0:T(8,128)(2,1)}, u32[]{:S(2)}, u32[]{:S(2)}) %collective-permute-start.2) | collective-permute-done | bytes 1253408 | tf_op jit(solution)/shard_map/ppermute | solution.py:810
  47.0 9.5 %permute.5 = bf16[896,1536]{1,0:T(8,128)(2,1)} custom-call(s32[1,2048]{1,0:T(1,128)} %bitcast.213, bf16[2048,768]{1,0:T(8,128)(2,1)S(1)} %copy-done.2, bf16[2048,768]{1,0:T(8,128)(2,1)} %gy_ref.5), custom_call_target="tpu_custom_call" | custom-call | flops 5637144576 | bytes 16000000 | tf_op jit(solution)/shard_map/permute/pallas_call | solution.py:100
  56.6 5.5 %all-to-all-start.5 = ((bf16[8,112,1536]{2,1,0:T(8,128)(2,1)}), bf16[8,112,1536]{2,1,0:T(8,128)(2,1)}, u32[]{:S(2)}, u32[]{:S(2)}) async-start(bf16[8,112,1536]{2,1,0:T(8,128)(2,1)} %bitcast.207), calls=%async_computation.5 | async-start | bytes 5505024 | tf_op jit(solution)/shard_map/all_to_all | solution.py:805
  62.1 9.3 %permute.4 = bf16[896,1536]{1,0:T(8,128)(2,1)} custom-call(s32[1,2048]{1,0:T(1,128)} %get-tuple-element.400.pos_ref, bf16[2048,768]{1,0:T(8,128)(2,1)S(1)} %copy-done.2, bf16[2048,768]{1,0:T(8,128)(2,1)} %gy_ref.5), custom_call_target="tpu_custom_call" | custom-call | flops 5637144576 | bytes 16000000 | tf_op jit(solution)/shard_map/permute/pallas_call | solution.py:100
  71.4 31.2 %all-to-all-done.5 = bf16[8,112,1536]{2,1,0:T(8,128)(2,1)} async-done(((bf16[8,112,1536]{2,1,0:T(8,128)(2,1)}), bf16[8,112,1536]{2,1,0:T(8,128)(2,1)}, u32[]{:S(2)}, u32[]{:S(2)}) %all-to-all-start.5) | async-done | bytes 2752544 | tf_op jit(solution)/shard_map/all_to_all | solution.py:805
  102.6 7.5 %all-to-all-start.4 = ((bf16[8,112,1536]{2,1,0:T(8,128)(2,1)}), bf16[8,112,1536]{2,1,0:T(8,128)(2,1)}, u32[]{:S(2)}, u32[]{:S(2)}) async-start(bf16[8,112,1536]{2,1,0:T(8,128)(2,1)} %bitcast.206), calls=%async_computation.4 | async-start | bytes 5505024 | tf_op jit(solution)/shard_map/all_to_all | solution.py:805
  111.9 28.4 %own_base.2 = (bf16[8,4,56,1536]{3,2,1,0:T(8,128)(2,1)}, bf16[1792,768]{1,0:T(8,128)(2,1)}, bf16[1792,768]{1,0:T(8,128)(2,1)}, bf16[1792,3072]{1,0:T(8,128)(2,1)...) custom-call(s32[1]{0:T(128)} %bitcast.54.lead_ref.first_ref, ...), custom_call_target="tpu_custom_call" | custom-call | flops 16999999488 | bytes 40000000 | tf_op jit(solution)/shard_map/own_base/pallas_call | solution.py:263
  140.3 13.3 %all-to-all-done.4 = bf16[8,112,1536]{2,1,0:T(8,128)(2,1)} async-done(((bf16[8,112,1536]{2,1,0:T(8,128)(2,1)}), bf16[8,112,1536]{2,1,0:T(8,128)(2,1)}, u32[]{:S(2)}, u32[]{:S(2)}) %all-to-all-start.4) | async-done | bytes 2752544 | tf_op jit(solution)/shard_map/all_to_all | solution.py:805
  153.7 28.9 %own_base.3 = (bf16[8,4,56,1536]{3,2,1,0:T(8,128)(2,1)}, bf16[1792,768]{1,0:T(8,128)(2,1)}, bf16[1792,768]{1,0:T(8,128)(2,1)}, bf16[1792,3072]{1,0:T(8,128)(2,1)...) custom-call(s32[1]{0:T(128)S(6)} %add.224.first_ref, ...), custom_call_target="tpu_custom_call", output_to_operand_aliasing={{0}: (6, {}), {1}: (7, {}), {2}: (8, {}), {3}: (9, {}), {4}... | custom-call | flops 16999999488 | bytes 40000000 | tf_op jit(solution)/shard_map/own_base/pallas_call | solution.py:263
  182.6 3.1 shard_map.102
  185.8 27.4 %own_over.1 = (bf16[408,8,1536]{2,1,0:T(8,128)(2,1)}, bf16[1664,768]{1,0:T(8,128)(2,1)}, bf16[1664,768]{1,0:T(8,128)(2,1)}, bf16[1664,3072]{1,0:T(8,128)(2,1)}, ...) custom-call(s32[5,8]{1,0:T(8,128)} %get-tuple-element.221.tab_ref, ...), custom_call_target="tpu_custom_call", output_to_operand_aliasing={{0}: (8, {})} | custom-call | flops 10000000000 | bytes 40000000 | tf_op jit(solution)/shard_map/own_over/pallas_call | solution.py:368
  213.2 17.3 %collective-permute-start.3 = (bf16[8,112,1536]{2,1,0:T(8,128)(2,1)}, bf16[8,112,1536]{2,1,0:T(8,128)(2,1)}, u32[]{:S(2)}, u32[]{:S(2)}) collective-permute-start(bf16[8,112,1536]{2,1,0:T(8,128)(2,1)} %all-to-all-done.5), channel_id=1, source_target_pairs={{0,8},{8,0},{1,9},{9,1},{2,10},{10,2},{3,11},{11,3},{4,12},{12,4},... | collective-permute-start | bytes 8257544 | tf_op jit(solution)/shard_map/ppermute | solution.py:806
  230.5 1.5 collective-permute-done.5
  233.0 2.6 collective-permute-start.6
  235.6 2.5 collective-permute-done.8
  238.1 1.3 collective-permute-done.7
  239.5 1.6 collective-permute-start.9
  241.1 94.6 %collective-permute-done.9 = f32[32,768]{1,0:T(8,128)S(1)} collective-permute-done((f32[32,768]{1,0:T(8,128)S(1)}, f32[32,768]{1,0:T(8,128)S(1)}, u32[]{:S(2)}, u32[]{:S(2)}) %collective-permute-start.9) | collective-permute-done | bytes 98336 | tf_op jit(solution)/shard_map/ppermute | solution.py:835
  336.4 4.5 shard_map.101
  341.6 10.7 %all-to-all-start.6 = ((bf16[8,224,1536]{2,1,0:T(8,128)(2,1)}), bf16[8,224,1536]{2,1,0:T(8,128)(2,1)}, u32[]{:S(2)}, u32[]{:S(2)}) async-start(bf16[8,224,1536]{2,1,0:T(8,128)(2,1)} %bitcast.199), calls=%async_computation.6 | async-start | bytes 11010048 | tf_op jit(solution)/shard_map/all_to_all | solution.py:827
  352.3 133.4 %grad_pass.1 = (f32[4,768,3072]{2,1,0:T(8,128)}, f32[4,3072,768]{2,1,0:T(8,128)}) custom-call(s32[8,24]{1,0:T(8,128)} %get-tuple-element.228.tab_ref, s32[192]{0:T(256)} %get-tuple-element.229.runs_ref, s32[1]{0:T(128)} %bitcast.54.lead_ref.first_ref, bf16[1792,768]{1,0:T(8,128)(2,1)} %get-tuple-element.230.xb_ref, ...), custom_call_target="tpu_custom_call" | custom-call | flops 70000001024 | bytes 150000000 | tf_op jit(solution)/shard_map/grad_pass/pallas_call | solution.py:529
  485.8 15.1 %unpermute.1 = (bf16[2048,768]{1,0:T(8,128)(2,1)}, bf16[2048,768]{1,0:T(8,128)(2,1)}) custom-call(s32[2048]{0:T(1024)} %get-tuple-element.402.pos_ref, bf16[8,224,1536]{2,1,0:T(8,128)(2,1)} %all-to-all-done.6.base_ref, bf16[408,1536]{1,0:T(8,128)(2,1)} %bitcast.214), custom_call_target="tpu_custom_call" | custom-call | flops 10000000000 | bytes 16000000 | tf_op jit(solution)/shard_map/unpermute/pallas_call | solution.py:174
  500.9 1.3 while.34
  (48 shorter events, 8.0 us)
Async XLA Ops:
  7.2 39.9 %copy-start.2 = (bf16[2048,768]{1,0:T(8,128)(2,1)S(1)}, bf16[2048,768]{1,0:T(8,128)(2,1)}, u32[]{:S(2)}) copy-start(bf16[2048,768]{1,0:T(8,128)(2,1)} %x_ref.5) | copy-start | bytes 9437188
  7.2 175.4 %all-gather.8.cloned.1.call-start = ((), (), s32[]{:S(2)}) async-start(), calls=%async_computation.9 | async-start | bytes 11280384 | tf_op jit(solution)/shard_map/all_gather | solution.py:809
  10.3 36.7 %copy-start.23 = (s32[16,128]{1,0:T(8,128)}, s32[16,128]{1,0:T(8,128)S(1)}, u32[]{:S(2)}) copy-start(s32[16,128]{1,0:T(8,128)S(1)} %get-tuple-element.403) | copy-start | bytes 24580
  18.2 318.2 %all-gather.10.cloned.1.call-start = ((), (), s32[]{:S(2)}) async-start(), calls=%async_computation.11 | async-start | bytes 11280384 | tf_op jit(solution)/shard_map/all_gather | solution.py:811
  18.2 28.8 %collective-permute-start.2 = (bf16[51,8,1536]{2,1,0:T(8,128)(2,1)}, bf16[51,8,1536]{2,1,0:T(8,128)(2,1)}, u32[]{:S(2)}, u32[]{:S(2)}) collective-permute-start(bf16[51,8,1536]{2,1,0:T(8,128)(2,1)} %bitcast.209), channel_id=1, source_target_pairs={{0,8},{8,0},{1,9},{9,1},{2,10},{10,2},{3,11},{11,3},{4,12},{12,4},... | collective-permute-start | bytes 3760136 | tf_op jit(solution)/shard_map/ppermute | solution.py:810
  56.6 46.0 %all-to-all-start.5 = ((bf16[8,112,1536]{2,1,0:T(8,128)(2,1)}), bf16[8,112,1536]{2,1,0:T(8,128)(2,1)}, u32[]{:S(2)}, u32[]{:S(2)}) async-start(bf16[8,112,1536]{2,1,0:T(8,128)(2,1)} %bitcast.207), calls=%async_computation.5 | async-start | bytes 5505024 | tf_op jit(solution)/shard_map/all_to_all | solution.py:805
  62.1 48.3 %copy-start.12 = (bf16[768,32]{0,1:T(8,128)(2,1)S(1)}, bf16[768,32]{0,1:T(8,128)(2,1)}, u32[]{:S(2)}) copy-start(bf16[768,32]{0,1:T(8,128)(2,1)} %param.13) | copy-start | bytes 147460
  102.6 51.0 %all-to-all-start.4 = ((bf16[8,112,1536]{2,1,0:T(8,128)(2,1)}), bf16[8,112,1536]{2,1,0:T(8,128)(2,1)}, u32[]{:S(2)}, u32[]{:S(2)}) async-start(bf16[8,112,1536]{2,1,0:T(8,128)(2,1)} %bitcast.206), calls=%async_computation.4 | async-start | bytes 5505024 | tf_op jit(solution)/shard_map/all_to_all | solution.py:805
  110.1 375.6 %reduce-scatter.2.cloned.1.call-start = ((), (), s32[]{:S(2)}) async-start(), calls=%async_computation.10 | async-start | bytes 11280384 | tf_op jit(solution)/shard_map/reduce_scatter | solution.py:830
  213.2 139.1 %collective-permute-start.3 = (bf16[8,112,1536]{2,1,0:T(8,128)(2,1)}, bf16[8,112,1536]{2,1,0:T(8,128)(2,1)}, u32[]{:S(2)}, u32[]{:S(2)}) collective-permute-start(bf16[8,112,1536]{2,1,0:T(8,128)(2,1)} %all-to-all-done.5), channel_id=1, source_target_pairs={{0,8},{8,0},{1,9},{9,1},{2,10},{10,2},{3,11},{11,3},{4,12},{12,4},... | collective-permute-start | bytes 8257544 | tf_op jit(solution)/shard_map/ppermute | solution.py:806
  230.5 121.8 %collective-permute-start.4 = (bf16[8,112,1536]{2,1,0:T(8,128)(2,1)}, bf16[8,112,1536]{2,1,0:T(8,128)(2,1)}, u32[]{:S(2)}, u32[]{:S(2)}) collective-permute-start(bf16[8,112,1536]{2,1,0:T(8,128)(2,1)} %all-to-all-done.4), channel_id=1, source_target_pairs={{0,8},{8,0},{1,9},{9,1},{2,10},{10,2},{3,11},{11,3},{4,12},{12,4},... | collective-permute-start | bytes 8257544 | tf_op jit(solution)/shard_map/ppermute | solution.py:806
  230.5 1.5 collective-permute-start.5
  232.9 5.2 %collective-permute-start.8 = (f32[32,768]{1,0:T(8,128)S(1)}, f32[32,768]{1,0:T(8,128)S(1)}, u32[]{:S(2)}, u32[]{:S(2)}) collective-permute-start(f32[32,768]{1,0:T(8,128)S(1)} %add.225), channel_id=1, source_target_pairs={{0,6},{1,7},{2,4},{3,5},{4,2},{5,3},{6,0},{7,1},{8,14},{9,15},{10,... | collective-permute-start | bytes 294920 | tf_op jit(solution)/shard_map/ppermute | solution.py:835
  233.0 6.4 %collective-permute-start.7 = (f32[32,768]{1,0:T(8,128)S(1)}, f32[32,768]{1,0:T(8,128)S(1)}, u32[]{:S(2)}, u32[]{:S(2)}) collective-permute-start(f32[32,768]{1,0:T(8,128)S(1)} %add.225), channel_id=1, source_target_pairs={{0,4},{1,5},{2,6},{3,7},{4,0},{5,1},{6,2},{7,3},{8,12},{9,13},{10,... | collective-permute-start | bytes 294920 | tf_op jit(solution)/shard_map/ppermute | solution.py:835
  233.0 6.4 %collective-permute-start.6 = (f32[32,768]{1,0:T(8,128)S(1)}, f32[32,768]{1,0:T(8,128)S(1)}, u32[]{:S(2)}, u32[]{:S(2)}) collective-permute-start(f32[32,768]{1,0:T(8,128)S(1)} %add.225), channel_id=1, source_target_pairs={{0,2},{1,3},{2,0},{3,1},{4,6},{5,7},{6,4},{7,5},{8,10},{9,11},{10,... | collective-permute-start | bytes 294920 | tf_op jit(solution)/shard_map/ppermute | solution.py:835
  239.5 96.3 %collective-permute-start.9 = (f32[32,768]{1,0:T(8,128)S(1)}, f32[32,768]{1,0:T(8,128)S(1)}, u32[]{:S(2)}, u32[]{:S(2)}) collective-permute-start(f32[32,768]{1,0:T(8,128)S(1)} %add_add_fusion), channel_id=1, source_target_pairs={{0,8},{8,0},{1,9},{9,1},{2,10},{10,2},{3,11},{11,3},{4,12},{12,4},... | collective-permute-start | bytes 294920 | tf_op jit(solution)/shard_map/ppermute | solution.py:835
  341.6 144.2 %all-to-all-start.6 = ((bf16[8,224,1536]{2,1,0:T(8,128)(2,1)}), bf16[8,224,1536]{2,1,0:T(8,128)(2,1)}, u32[]{:S(2)}, u32[]{:S(2)}) async-start(bf16[8,224,1536]{2,1,0:T(8,128)(2,1)} %bitcast.199), calls=%async_computation.6 | async-start | bytes 11010048 | tf_op jit(solution)/shard_map/all_to_all | solution.py:827
  485.8 15.1 %copy-start.3 = (bf16[2048,768]{1,0:T(8,128)(2,1)S(1)}, bf16[2048,768]{1,0:T(8,128)(2,1)}, u32[]{:S(2)}) copy-start(bf16[2048,768]{1,0:T(8,128)(2,1)} %x_ref.5) | copy-start | bytes 9437188
  485.8 15.1 %copy-start.9 = (s32[2048]{0:T(1024)S(1)}, s32[2048]{0:T(1024)}, u32[]{:S(2)}) copy-start(s32[2048]{0:T(1024)} %param.12) | copy-start | bytes 24580
  485.8 15.1 %copy-start.13 = (bf16[768,32]{0,1:T(8,128)(2,1)S(1)}, bf16[768,32]{0,1:T(8,128)(2,1)}, u32[]{:S(2)}) copy-start(bf16[768,32]{0,1:T(8,128)(2,1)} %param.13) | copy-start | bytes 147460
Sparse Core Ops, SparseCore 0:
  18.3 76.2 all-gather.7
  96.4 93.0 all-gather.9
  213.3 88.2 reduce-scatter.1

commit v5 on v4

--- a/solution.py
+++ b/solution.py
@@ -625,10 +625,16 @@
         copy.wait()
 
 
-def own_plan_kernel(local, lead_ref, count_ref, tab_ref, runs_ref, size_v, first_v, size_s, first_s, n_runs, count, sems):
-    size_v[...], first_v[...], _ = overflow_spans(count_ref, local)
+def own_plan_kernel(local, lead_ref, count_ref, tab_ref, runs_ref, span_ref, size_v, first_v, size_s, first_s, n_runs, count,
+                    sems):
+    size_v[0], first_v[0], excess = overflow_spans(count_ref, local)
     to_scalars([(size_v, size_s), (first_v, first_s)], sems)
-    spans, n_tiles = fill_tiles(count_ref.shape[0], local, lead_ref[0], size_s, first_s, runs_ref, n_runs.at[0], count.at[0])
+    spans, n_tiles = fill_tiles(count_ref.shape[0], local, lead_ref[0], size_s.at[0], first_s.at[0], runs_ref, n_runs.at[0],
+                                count.at[0])
+    for e, (tile, tiles) in enumerate(spans):
+        span_ref[e] = tile
+        span_ref[local + e] = tiles
+    span_ref[2 * local] = (excess <= 0.0).astype(I32)
     last = jnp.maximum(n_tiles - 1, 0)
     for t in range(MAX_OVER_TILES):
         row = (local - 1, count[0, t], jnp.minimum(t, last), (last == t).astype(I32), n_runs[0, t])
@@ -642,22 +648,22 @@
         lax.fori_loop(0, tiles, body, 0)
 
 
-def grad_plan_kernel(local, lead_ref, own_ref, other_ref, tab_ref, runs_ref, fits_ref, size_v, first_v, size_s, first_s,
+def grad_plan_kernel(local, lead_ref, span_ref, other_ref, tab_ref, runs_ref, fits_ref, size_v, first_v, size_s, first_s,
                      n_runs, count, sems):
-    n_src = own_ref.shape[0]
-    size_v[0], first_v[0], own_excess = overflow_spans(own_ref, local)
-    size_v[1], first_v[1], other_excess = overflow_spans(other_ref, local)
+    n_src = other_ref.shape[0]
+    size_v[0], first_v[0], excess = overflow_spans(other_ref, local)
     to_scalars([(size_v, size_s), (first_v, first_s)], sems)
-    fits_ref[0] = (jnp.maximum(own_excess, other_excess) <= 0.0).astype(I32)
+    fits_ref[0] = span_ref[2 * local] * (excess <= 0.0).astype(I32)
     lead = lead_ref[0]
-    own, n_tiles = fill_tiles(n_src, local, lead, size_s.at[0], first_s.at[0], runs_ref, n_runs.at[0], count.at[0])
-    other, _ = fill_tiles(n_src, local, lead, size_s.at[1], first_s.at[1], runs_ref, n_runs.at[1], count.at[1])
+    own = [(span_ref[e], span_ref[local + e]) for e in range(local)]
+    n_tiles = own[-1][0] + own[-1][1]
+    other, _ = fill_tiles(n_src, local, lead, size_s.at[0], first_s.at[0], runs_ref, n_runs.at[0], count.at[0])
     max_steps = tab_ref.shape[1]
 
     def emit(step, expert, kind, own_tile, other_tile, next_base):
         over = int(kind == OTHER_OVER)
-        row = (expert, kind, 0, jnp.clip(own_tile, 0, MAX_OVER_TILES - 1), count[1, other_tile] * over, other_tile, next_base,
-               n_runs[1, other_tile] * over)
+        row = (expert, kind, 0, jnp.clip(own_tile, 0, MAX_OVER_TILES - 1), count[0, other_tile] * over, other_tile, next_base,
+               n_runs[0, other_tile] * over)
         for k, value in enumerate(row):
             tab_ref[k, step] = value
 
@@ -692,21 +698,19 @@
     lax.fori_loop(step, max_steps, dead, 0)
 
 
-def plan_call(kernel, local, lead, counts, out_shapes, planes):
-    n_src = counts[0].shape[0]
+def plan_call(kernel, local, scalars, counts, out_shapes):
+    n_src = counts.shape[0]
     smem = pl.BlockSpec(memory_space=pltpu.SMEM)
-    spec = pl.BlockSpec((n_src, 1, GROUP, 128), lambda i: (0, OVER_GROUPS, 0, 0))
-    shape = (n_src, 128) if planes == 1 else (planes, n_src, 128)
+    shape = (1, n_src, 128)
     return pl.pallas_call(
         functools.partial(kernel, local),
         grid=(1,),
-        in_specs=[smem] + [spec] * len(counts),
+        in_specs=[smem] * len(scalars) + [pl.BlockSpec((n_src, 1, GROUP, 128), lambda i: (0, OVER_GROUPS, 0, 0))],
         out_specs=[smem] * len(out_shapes),
         out_shape=[jax.ShapeDtypeStruct(o, I32) for o in out_shapes],
-        scratch_shapes=[pltpu.VMEM(shape, I32), pltpu.VMEM(shape, I32), pltpu.SMEM(shape, I32), pltpu.SMEM(shape, I32),
-                        pltpu.SMEM((planes, MAX_OVER_TILES), I32), pltpu.SMEM((planes, MAX_OVER_TILES), I32),
-                        pltpu.SemaphoreType.DMA((2,))],
-    )(lead, *counts)
+        scratch_shapes=[pltpu.VMEM(shape, I32)] * 2 + [pltpu.SMEM(shape, I32)] * 2
+        + [pltpu.SMEM((1, MAX_OVER_TILES), I32)] * 2 + [pltpu.SemaphoreType.DMA((2,))],
+    )(*scalars, counts)
 
 
 def padded_step(x_loc, gy_loc, idx_loc, w_gate, w_up, w_down, ep_size, dp_size):
@@ -811,9 +815,10 @@
         over_z = lax.all_gather(over_sent_z, 'ep')
 
         n_runs = MAX_OVER_TILES * RUNS * 3
-        table, runs = plan_call(own_plan_kernel, local, first_expert, [over], [(5, MAX_OVER_TILES), (n_runs,)], 1)
-        gtable, runs_z, fits = plan_call(grad_plan_kernel, local, first_expert, [over, over_z],
-                                         [(8, 2 * (local + MAX_OVER_TILES)), (n_runs,), (1,)], 2)
+        table, runs, spans = plan_call(own_plan_kernel, local, [first_expert], over,
+                                       [(5, MAX_OVER_TILES), (n_runs,), (2 * local + 1,)])
+        gtable, runs_z, fits = plan_call(grad_plan_kernel, local, [first_expert, spans], over_z,
+                                         [(8, 2 * (local + MAX_OVER_TILES)), (n_runs,), (1,)])
         over_shape = (ep_size * SENT_GROUPS, GROUP, width)
         over = over.reshape(over_shape)
         over_z = over_z.reshape(over_shape)
@@ -830,15 +835,7 @@
         over_back = lax.psum_scatter(od_over.reshape(ep_size, SENT_GROUPS, GROUP, width), 'ep', scatter_dimension=0)
         d_up, d_down = grad_pass(gtable, runs_z, first_expert, base_store, (x_o, dy_o, h_o, da_o), base_z, over_z,
                                  w_gate, w_up, w_down)
-
-        def from_peer(axis, bits, value):
-            return lax.ppermute(value, axis, [(i, i ^ bits) for i in range(mesh.shape[axis])])
-
-        pair = dwg + from_peer('ep', 1, dwg)
-        near = pair + from_peer('ep', 2, pair)
-        far = from_peer('ep', 4, pair) + from_peer('ep', 6, pair)
-        plane = near + far
-        d_gate = (plane + from_peer('dp', 1, plane)).T
+        d_gate = jnp.sum(lax.all_gather(dwg, ('dp', 'ep')), axis=0).T
         moe_out, grad_x = unpermute_rows(pos, base_back, over_back.reshape(-1, width))
         sparse = (moe_out, grad_x, d_up, d_down, d_gate)
 

time: 517 us -> 506 us (0.979)
  starting transfers between devices: 45.8 us -> 35.5 us
    ppermute x5 -> x0, waiting for transfers between devices: 100 us -> none  [from_peer(): lax.ppermute(value, axis, [(i, i ^ bits) for i in range(mesh.shape[axis])])]
    ppermute x2, waiting for transfers between devices: 0.01 us -> 99.4 us  [local_step(): base_z.append(lax.ppermute(base[c], 'dp', swap).reshape(slots))]
    all_to_all x1, starting transfers between devices: 10.7 us -> 4.65 us  [local_step(): lax.all_to_all(od.reshape(ep_size, -1, width), 'ep', 0, 0, tiled=True)]
  transfers between devices with their start and end apart: 14 -> 10, of which waited for: 7 -> 5; matrix products, arithmetic and copies ran while one was open for 1% -> 1% of each run, Pallas kernels for 48% -> 49%
where the time goes in v5:
time: 506 us; the launch traced here: 498 us
  Pallas kernels  265 us (52%)
  waiting for transfers between devices  173 us (34%)
  starting transfers between devices  35.5 us (7%)
  between operations  14.8 us (3%)
    pallas_call x1, Pallas kernels, grad_pass(): pl.pallas_call(grad_kernel, grid_spec=pltpu.PrefetchScalarGridSpec(num_sc...  133 us
    ppermute x2, waiting for transfers between devices, local_step(): base_z.append(lax.ppermute(base[c], 'dp', swap).reshape(slots))  99.4 us
    pallas_call x2, Pallas kernels, own_base_pass(): pl.pallas_call(own_base_kernel, grid_spec=pltpu.PrefetchScalarGridSpec(nu...  57.1 us
    all_to_all x2, waiting for transfers between devices, local_step(): lax.all_to_all(sent.reshape(ep_size, -1, width), 'ep', 0, 0, tiled=True)  44.6 us
    ppermute x1, waiting for transfers between devices, local_step(): over_sent_z = lax.ppermute(over_sent, 'dp', swap)  28.7 us
    pallas_call x1, Pallas kernels, own_over_pass(): pl.pallas_call(own_over_kernel, grid_spec=pltpu.PrefetchScalarGridSpec(nu...  27.8 us
    pallas_call x3, Pallas kernels, permute_rows(): pl.pallas_call(permute_kernel, grid=(n_rows // tile,), in_specs=[pl.Block...  25.4 us
    ppermute x2, starting transfers between devices, local_step(): base_z.append(lax.ppermute(base[c], 'dp', swap).reshape(slots))  17.3 us
  transfers between devices with their start and end apart: 10, of which 5 were waited for; matrix products, arithmetic and copies ran while one was open for 1% of the time, Pallas kernels for 49%

profile of v5, /device:TPU:9, one launch (start us, length us, event | category | flops | bytes accessed | tf_op | source)
XLA Modules:
  0.0 498.2 jit_solution(457562547188915387)
XLA Ops:
  7.2 1.1 convert_reduce_fusion.2
  8.7 1.0 fusion.41
  11.6 6.6 %permute.3 = bf16[408,1536]{1,0:T(8,128)(2,1)} custom-call(s32[1,2048]{1,0:T(1,128)} %get-tuple-element.379.pos_ref, bf16[2048,768]{1,0:T(8,128)(2,1)} %x_ref.5, bf16[2048,768]{1,0:T(8,128)(2,1)} %gy_ref.5, bf16[8,1536]{1,0:T(8,128)(2,1)} %pad.4.refs_0_), custom_call_target="tpu_custom_call" | custom-call | flops 2516582400 | bytes 16000000 | tf_op jit(solution)/shard_map/permute/pallas_call | solution.py:100
  18.3 28.7 %collective-permute-done.2 = bf16[51,8,1536]{2,1,0:T(8,128)(2,1)} collective-permute-done((bf16[51,8,1536]{2,1,0:T(8,128)(2,1)}, bf16[51,8,1536]{2,1,0:T(8,128)(2,1)}, u32[]{:S(2)}, u32[]{:S(2)}) %collective-permute-start.2) | collective-permute-done | bytes 1253408 | tf_op jit(solution)/shard_map/ppermute | solution.py:814
  47.1 9.5 %permute.5 = bf16[896,1536]{1,0:T(8,128)(2,1)} custom-call(s32[1,2048]{1,0:T(1,128)} %bitcast.215, bf16[2048,768]{1,0:T(8,128)(2,1)S(1)} %copy-done.2, bf16[2048,768]{1,0:T(8,128)(2,1)} %gy_ref.5), custom_call_target="tpu_custom_call" | custom-call | flops 5637144576 | bytes 16000000 | tf_op jit(solution)/shard_map/permute/pallas_call | solution.py:100
  56.6 5.5 %all-to-all-start.5 = ((bf16[8,112,1536]{2,1,0:T(8,128)(2,1)}), bf16[8,112,1536]{2,1,0:T(8,128)(2,1)}, u32[]{:S(2)}, u32[]{:S(2)}) async-start(bf16[8,112,1536]{2,1,0:T(8,128)(2,1)} %bitcast.207), calls=%async_computation.5 | async-start | bytes 5505024 | tf_op jit(solution)/shard_map/all_to_all | solution.py:809
  62.1 9.3 %permute.4 = bf16[896,1536]{1,0:T(8,128)(2,1)} custom-call(s32[1,2048]{1,0:T(1,128)} %get-tuple-element.378.pos_ref, bf16[2048,768]{1,0:T(8,128)(2,1)S(1)} %copy-done.2, bf16[2048,768]{1,0:T(8,128)(2,1)} %gy_ref.5), custom_call_target="tpu_custom_call" | custom-call | flops 5637144576 | bytes 16000000 | tf_op jit(solution)/shard_map/permute/pallas_call | solution.py:100
  71.4 31.2 %all-to-all-done.5 = bf16[8,112,1536]{2,1,0:T(8,128)(2,1)} async-done(((bf16[8,112,1536]{2,1,0:T(8,128)(2,1)}), bf16[8,112,1536]{2,1,0:T(8,128)(2,1)}, u32[]{:S(2)}, u32[]{:S(2)}) %all-to-all-start.5) | async-done | bytes 2752544 | tf_op jit(solution)/shard_map/all_to_all | solution.py:809
  102.6 7.5 %all-to-all-start.4 = ((bf16[8,112,1536]{2,1,0:T(8,128)(2,1)}), bf16[8,112,1536]{2,1,0:T(8,128)(2,1)}, u32[]{:S(2)}, u32[]{:S(2)}) async-start(bf16[8,112,1536]{2,1,0:T(8,128)(2,1)} %bitcast.206), calls=%async_computation.4 | async-start | bytes 5505024 | tf_op jit(solution)/shard_map/all_to_all | solution.py:809
  110.5 0.8 copy.49.wg_ref.refs_3_
  111.9 28.4 %own_base.2 = (bf16[8,4,56,1536]{3,2,1,0:T(8,128)(2,1)}, bf16[1792,768]{1,0:T(8,128)(2,1)}, bf16[1792,768]{1,0:T(8,128)(2,1)}, bf16[1792,3072]{1,0:T(8,128)(2,1)...) custom-call(s32[1]{0:T(128)} %bitcast.54.lead_ref.first_ref, ...), custom_call_target="tpu_custom_call" | custom-call | flops 16999999488 | bytes 40000000 | tf_op jit(solution)/shard_map/own_base/pallas_call | solution.py:263
  140.3 13.3 %all-to-all-done.4 = bf16[8,112,1536]{2,1,0:T(8,128)(2,1)} async-done(((bf16[8,112,1536]{2,1,0:T(8,128)(2,1)}), bf16[8,112,1536]{2,1,0:T(8,128)(2,1)}, u32[]{:S(2)}, u32[]{:S(2)}) %all-to-all-start.4) | async-done | bytes 2752544 | tf_op jit(solution)/shard_map/all_to_all | solution.py:809
  153.7 28.8 %own_base.3 = (bf16[8,4,56,1536]{3,2,1,0:T(8,128)(2,1)}, bf16[1792,768]{1,0:T(8,128)(2,1)}, bf16[1792,768]{1,0:T(8,128)(2,1)}, bf16[1792,3072]{1,0:T(8,128)(2,1)...) custom-call(s32[1]{0:T(128)S(6)} %add.209.first_ref, ...), custom_call_target="tpu_custom_call", output_to_operand_aliasing={{0}: (6, {}), {1}: (7, {}), {2}: (8, {}), {3}: (9, {}), {4}... | custom-call | flops 16999999488 | bytes 40000000 | tf_op jit(solution)/shard_map/own_base/pallas_call | solution.py:263
  182.4 3.1 shard_map.101
  185.6 27.8 %own_over.1 = (bf16[408,8,1536]{2,1,0:T(8,128)(2,1)}, bf16[1664,768]{1,0:T(8,128)(2,1)}, bf16[1664,768]{1,0:T(8,128)(2,1)}, bf16[1664,3072]{1,0:T(8,128)(2,1)}, ...) custom-call(s32[5,8]{1,0:T(8,128)} %get-tuple-element.223.tab_ref, ...), custom_call_target="tpu_custom_call", output_to_operand_aliasing={{0}: (8, {})} | custom-call | flops 10000000000 | bytes 40000000 | tf_op jit(solution)/shard_map/own_over/pallas_call | solution.py:368
  214.1 17.3 %collective-permute-start.3 = (bf16[8,112,1536]{2,1,0:T(8,128)(2,1)}, bf16[8,112,1536]{2,1,0:T(8,128)(2,1)}, u32[]{:S(2)}, u32[]{:S(2)}) collective-permute-start(bf16[8,112,1536]{2,1,0:T(8,128)(2,1)} %all-to-all-done.5), channel_id=1, source_target_pairs={{0,8},{8,0},{1,9},{9,1},{2,10},{10,2},{3,11},{11,3},{4,12},{12,4},... | collective-permute-start | bytes 8257544 | tf_op jit(solution)/shard_map/ppermute | solution.py:810
  231.4 3.4 shard_map.102
  235.5 4.6 all-to-all-start.6
  240.1 56.7 %collective-permute-done.3 = bf16[8,112,1536]{2,1,0:T(8,128)(2,1)} collective-permute-done((bf16[8,112,1536]{2,1,0:T(8,128)(2,1)}, bf16[8,112,1536]{2,1,0:T(8,128)(2,1)}, u32[]{:S(2)}, u32[]{:S(2)}) %collective-permute-start.3) | collective-permute-done | bytes 2752544 | tf_op jit(solution)/shard_map/ppermute | solution.py:810
  296.8 42.7 %collective-permute-done.4 = bf16[8,112,1536]{2,1,0:T(8,128)(2,1)} collective-permute-done((bf16[8,112,1536]{2,1,0:T(8,128)(2,1)}, bf16[8,112,1536]{2,1,0:T(8,128)(2,1)}, u32[]{:S(2)}, u32[]{:S(2)}) %collective-permute-start.4) | collective-permute-done | bytes 2752544 | tf_op jit(solution)/shard_map/ppermute | solution.py:810
  339.5 133.4 %grad_pass.1 = (f32[4,768,3072]{2,1,0:T(8,128)}, f32[4,3072,768]{2,1,0:T(8,128)}) custom-call(s32[8,24]{1,0:T(8,128)} %get-tuple-element.230.tab_ref, s32[192]{0:T(256)} %get-tuple-element.231.runs_ref, s32[1]{0:T(128)} %bitcast.54.lead_ref.first_ref, bf16[1792,768]{1,0:T(8,128)(2,1)} %get-tuple-element.232.xb_ref, ...), custom_call_target="tpu_custom_call" | custom-call | flops 70000001024 | bytes 150000000 | tf_op jit(solution)/shard_map/grad_pass/pallas_call | solution.py:529
  472.9 2.1 reduce_sum.84
  475.1 15.1 %unpermute.1 = (bf16[2048,768]{1,0:T(8,128)(2,1)}, bf16[2048,768]{1,0:T(8,128)(2,1)}) custom-call(s32[2048]{0:T(1024)} %get-tuple-element.380.pos_ref, bf16[8,224,1536]{2,1,0:T(8,128)(2,1)} %all-to-all-done.6.base_ref, bf16[408,1536]{1,0:T(8,128)(2,1)} %bitcast.216), custom_call_target="tpu_custom_call" | custom-call | flops 10000000000 | bytes 16000000 | tf_op jit(solution)/shard_map/unpermute/pallas_call | solution.py:174
  490.2 1.2 while.34
  (39 shorter events, 4.0 us)
Async XLA Ops:
  7.2 39.9 %copy-start.2 = (bf16[2048,768]{1,0:T(8,128)(2,1)S(1)}, bf16[2048,768]{1,0:T(8,128)(2,1)}, u32[]{:S(2)}) copy-start(bf16[2048,768]{1,0:T(8,128)(2,1)} %x_ref.5) | copy-start | bytes 9437188
  7.2 175.3 %all-gather.10.cloned.1.call-start = ((), (), s32[]{:S(2)}) async-start(), calls=%async_computation.9 | async-start | bytes 11280384 | tf_op jit(solution)/shard_map/all_gather | solution.py:813
  10.3 36.7 %copy-start.23 = (s32[16,128]{1,0:T(8,128)}, s32[16,128]{1,0:T(8,128)S(1)}, u32[]{:S(2)}) copy-start(s32[16,128]{1,0:T(8,128)S(1)} %get-tuple-element.381) | copy-start | bytes 24580
  18.2 213.2 %all-gather.12.cloned.1.call-start = ((), (), s32[]{:S(2)}) async-start(), calls=%async_computation.11 | async-start | bytes 11280384 | tf_op jit(solution)/shard_map/all_gather | solution.py:815
  18.2 28.8 %collective-permute-start.2 = (bf16[51,8,1536]{2,1,0:T(8,128)(2,1)}, bf16[51,8,1536]{2,1,0:T(8,128)(2,1)}, u32[]{:S(2)}, u32[]{:S(2)}) collective-permute-start(bf16[51,8,1536]{2,1,0:T(8,128)(2,1)} %bitcast.210), channel_id=1, source_target_pairs={{0,8},{8,0},{1,9},{9,1},{2,10},{10,2},{3,11},{11,3},{4,12},{12,4},... | collective-permute-start | bytes 3760136 | tf_op jit(solution)/shard_map/ppermute | solution.py:814
  56.6 46.0 %all-to-all-start.5 = ((bf16[8,112,1536]{2,1,0:T(8,128)(2,1)}), bf16[8,112,1536]{2,1,0:T(8,128)(2,1)}, u32[]{:S(2)}, u32[]{:S(2)}) async-start(bf16[8,112,1536]{2,1,0:T(8,128)(2,1)} %bitcast.207), calls=%async_computation.5 | async-start | bytes 5505024 | tf_op jit(solution)/shard_map/all_to_all | solution.py:809
  62.1 48.3 %copy-start.12 = (bf16[768,32]{0,1:T(8,128)(2,1)S(1)}, bf16[768,32]{0,1:T(8,128)(2,1)}, u32[]{:S(2)}) copy-start(bf16[768,32]{0,1:T(8,128)(2,1)} %param.13) | copy-start | bytes 147460
  102.6 51.0 %all-to-all-start.4 = ((bf16[8,112,1536]{2,1,0:T(8,128)(2,1)}), bf16[8,112,1536]{2,1,0:T(8,128)(2,1)}, u32[]{:S(2)}, u32[]{:S(2)}) async-start(bf16[8,112,1536]{2,1,0:T(8,128)(2,1)} %bitcast.206), calls=%async_computation.4 | async-start | bytes 5505024 | tf_op jit(solution)/shard_map/all_to_all | solution.py:809
  110.1 362.8 %all-gather.14.cloned.1.call-start = ((), (), s32[]{:S(2)}) async-start(), calls=%async_computation.12 | async-start | bytes 1671168 | tf_op jit(solution)/shard_map/all_gather | solution.py:838
  213.5 261.6 %reduce-scatter.2.cloned.1.call-start = ((), (), s32[]{:S(2)}) async-start(), calls=%async_computation.10 | async-start | bytes 11280384 | tf_op jit(solution)/shard_map/reduce_scatter | solution.py:835
  214.1 82.8 %collective-permute-start.3 = (bf16[8,112,1536]{2,1,0:T(8,128)(2,1)}, bf16[8,112,1536]{2,1,0:T(8,128)(2,1)}, u32[]{:S(2)}, u32[]{:S(2)}) collective-permute-start(bf16[8,112,1536]{2,1,0:T(8,128)(2,1)} %all-to-all-done.5), channel_id=1, source_target_pairs={{0,8},{8,0},{1,9},{9,1},{2,10},{10,2},{3,11},{11,3},{4,12},{12,4},... | collective-permute-start | bytes 8257544 | tf_op jit(solution)/shard_map/ppermute | solution.py:810
  231.3 108.2 %collective-permute-start.4 = (bf16[8,112,1536]{2,1,0:T(8,128)(2,1)}, bf16[8,112,1536]{2,1,0:T(8,128)(2,1)}, u32[]{:S(2)}, u32[]{:S(2)}) collective-permute-start(bf16[8,112,1536]{2,1,0:T(8,128)(2,1)} %all-to-all-done.4), channel_id=1, source_target_pairs={{0,8},{8,0},{1,9},{9,1},{2,10},{10,2},{3,11},{11,3},{4,12},{12,4},... | collective-permute-start | bytes 8257544 | tf_op jit(solution)/shard_map/ppermute | solution.py:810
  235.5 239.6 %all-to-all-start.6 = ((bf16[8,224,1536]{2,1,0:T(8,128)(2,1)}), bf16[8,224,1536]{2,1,0:T(8,128)(2,1)}, u32[]{:S(2)}, u32[]{:S(2)}) async-start(bf16[8,224,1536]{2,1,0:T(8,128)(2,1)} %bitcast.199), calls=%async_computation.6 | async-start | bytes 11010048 | tf_op jit(solution)/shard_map/all_to_all | solution.py:832
  475.1 15.1 %copy-start.3 = (bf16[2048,768]{1,0:T(8,128)(2,1)S(1)}, bf16[2048,768]{1,0:T(8,128)(2,1)}, u32[]{:S(2)}) copy-start(bf16[2048,768]{1,0:T(8,128)(2,1)} %x_ref.5) | copy-start | bytes 9437188
  475.1 15.1 %copy-start.9 = (s32[2048]{0:T(1024)S(1)}, s32[2048]{0:T(1024)}, u32[]{:S(2)}) copy-start(s32[2048]{0:T(1024)} %param.12) | copy-start | bytes 24580
  475.1 15.1 %copy-start.13 = (bf16[768,32]{0,1:T(8,128)(2,1)S(1)}, bf16[768,32]{0,1:T(8,128)(2,1)}, u32[]{:S(2)}) copy-start(bf16[768,32]{0,1:T(8,128)(2,1)} %param.13) | copy-start | bytes 147460
Sparse Core Ops, SparseCore 0:
  18.3 76.2 all-gather.9
  96.4 93.0 all-gather.11
  213.6 65.5 all-gather.13
  282.6 72.7 reduce-scatter.1
